TPU v7x, 256 devices: a whole 4x4x8 slice. The times are simulated.
256 devices in a mesh: gx: 8 (over y, core), gy: 4 (over z_hi), gz: 8 (over z_lo, x).
Axes of the slice: x: 4, y: 4, z: 8 (z_hi: 4, z_lo: 2; z = z_hi * 2 + z_lo), core: 2. Of those that a mesh axis runs over, the one named last changes fastest.
Arguments:
- features: bfloat16 [32, 24, 32, 1024], P(None, 'gx', 'gy', 'gz'), may hold values from -6 to 6
- edge_state: bfloat16 [3, 32, 24, 32, 1024], P(None, None, 'gx', 'gy', 'gz'), may hold values from -6 to 6
- multiplicity: int32 [24, 32, 1024], P('gx', 'gy', 'gz'), may hold values from 0 to 8
- edge_in: bfloat16 [3, 32, 96], replicated, may hold values from -0.625 to 0.625
- edge_out: bfloat16 [3, 32, 32], replicated, may hold values from -1 to 1
- edge_bias: float32 [3, 32], replicated, may hold values from -3 to 3
- node_in: bfloat16 [3, 32, 64], replicated, may hold values from -0.75 to 0.75
- node_out: bfloat16 [3, 32, 32], replicated, may hold values from -1 to 1
- node_bias: float32 [3, 32], replicated, may hold values from -3 to 3
Outputs:
- updated_features: bfloat16 [32, 24, 32, 1024], P(None, 'gx', 'gy', 'gz')
All inputs are finite; a program needn't handle non-finite values.
Results may differ from a plain program's by a relative error of at most 0.009.
Values sent between devices are 32-bit elements; how exact they have to be, the bound alone decides.
No kernel may reach another device: no remote copies, remote signals or barrier semaphores. Data moves between devices by JAX's collectives and lax.ppermute only.
A program may use at most 64 MiB of HBM per device.

v0:
```python
import jax
import jax.numpy as jnp
from jax import lax
from jax.sharding import PartitionSpec as P


def with_halo(block, sides, width):
    for axis, dim in sides:
        count = lax.axis_size(axis)
        forward = [(i, i + 1) for i in range(count - 1)]
        backward = [(target, source) for source, target in forward]
        low = lax.ppermute(
            lax.slice_in_dim(block, block.shape[dim] - width, None, axis=dim), axis, forward
        )
        high = lax.ppermute(lax.slice_in_dim(block, 0, width, axis=dim), axis, backward)
        block = jnp.concatenate([low, block, high], axis=dim)
    return block


def ahead(values, axis_pos):
    length = values.shape[axis_pos]
    remainder = lax.slice_in_dim(values, 1, length, axis=axis_pos)
    filler = jnp.zeros_like(lax.slice_in_dim(values, 0, 1, axis=axis_pos))
    return jnp.concatenate([remainder, filler], axis=axis_pos)


def behind(values, axis_pos):
    length = values.shape[axis_pos]
    remainder = lax.slice_in_dim(values, 0, length - 1, axis=axis_pos)
    filler = jnp.zeros_like(lax.slice_in_dim(values, 0, 1, axis=axis_pos))
    return jnp.concatenate([filler, remainder], axis=axis_pos)


def edge_layer(
    hidden_nodes, edges, counts, fluid, weight_in, weight_out, bias_in, spatial, count_dims
):
    channels = hidden_nodes.shape[0]
    shape = hidden_nodes.shape
    flat = hidden_nodes.reshape(channels, -1)
    stacked = jnp.concatenate(
        [weight_in[:, :channels], weight_in[:, channels : 2 * channels]], axis=0
    )
    projected = jnp.dot(stacked, flat, preferred_element_type=jnp.float32)
    own_part = projected[:channels].reshape(shape)
    other_part = projected[channels:].reshape(shape)
    bias = bias_in.reshape((channels,) + (1,) * (hidden_nodes.ndim - 1))
    incoming = jnp.zeros(shape, jnp.float32)
    updated = []
    for direction in range(3):
        edge_now = edges[direction]
        edge_term = jnp.dot(
            weight_in[:, 2 * channels :],
            edge_now.reshape(channels, -1),
            preferred_element_type=jnp.float32,
        ).reshape(shape)
        preact = own_part + ahead(other_part, spatial[direction]) + edge_term + bias
        edge_hidden = jax.nn.silu(preact).astype(jnp.bfloat16)
        message = jnp.dot(
            weight_out, edge_hidden.reshape(channels, -1), preferred_element_type=jnp.float32
        ).reshape(shape)
        updated.append((edge_now + message).astype(jnp.bfloat16))
        shared_count = jnp.minimum(counts, ahead(counts, count_dims[direction]))
        weight_edge = jnp.where(
            fluid & (shared_count > 0), 1.0 / jnp.maximum(shared_count, 1).astype(jnp.float32), 0.0
        )
        weighted = weight_edge[None] * message
        incoming = incoming + weighted + behind(weighted, spatial[direction])
    return (incoming, jnp.stack(updated))


def node_layer(hidden_nodes, incoming_rounded, weight_in, weight_out, bias_in):
    channels = hidden_nodes.shape[0]
    shape = hidden_nodes.shape
    node_pre = jnp.dot(
        weight_in[:, :channels],
        hidden_nodes.reshape(channels, -1),
        preferred_element_type=jnp.float32,
    )
    node_pre = node_pre + jnp.dot(
        weight_in[:, channels:],
        incoming_rounded.reshape(channels, -1),
        preferred_element_type=jnp.float32,
    )
    node_pre = node_pre + bias_in[:, None]
    node_hidden = jax.nn.silu(node_pre).astype(jnp.bfloat16)
    result = jnp.dot(weight_out, node_hidden, preferred_element_type=jnp.float32).reshape(shape)
    return (hidden_nodes + result).astype(jnp.bfloat16)


def fold_copies(padded, axis_pos):
    width = padded.shape[axis_pos] - 2
    inner = lax.slice_in_dim(padded, 1, width + 1, axis=axis_pos)
    lower = lax.index_in_dim(padded, 0, axis_pos, keepdims=False)
    upper = lax.index_in_dim(padded, width + 1, axis_pos, keepdims=False)
    front = (slice(None),) * axis_pos
    return inner.at[front + (0,)].add(lower).at[front + (width - 1,)].add(upper)


def sum_copies(incoming):
    padded = with_halo(incoming, (("gx", 1), ("gy", 2), ("gz", 3)), 1)
    return fold_copies(fold_copies(fold_copies(padded, 3), 2), 1)


def on_device(
    features, edge_state, multiplicity, edge_in, edge_out, edge_bias, node_in, node_out, node_bias
):
    fluid = multiplicity[1, 1, 1] > 0
    hidden_nodes = features
    edges = edge_state
    for layer_index in range(edge_in.shape[0]):
        incoming, edges = edge_layer(
            hidden_nodes,
            edges,
            multiplicity,
            fluid,
            edge_in[layer_index],
            edge_out[layer_index],
            edge_bias[layer_index],
            (1, 2, 3),
            (0, 1, 2),
        )
        incoming = sum_copies(incoming)
        hidden_nodes = node_layer(
            hidden_nodes,
            incoming.astype(jnp.bfloat16),
            node_in[layer_index],
            node_out[layer_index],
            node_bias[layer_index],
        )
    return hidden_nodes


def solution(mesh):
    placed = (
        P(None, "gx", "gy", "gz"),
        P(None, None, "gx", "gy", "gz"),
        P("gx", "gy", "gz"),
        P(),
        P(),
        P(),
        P(),
        P(),
        P(),
    )
    return jax.shard_map(
        on_device, mesh=mesh, in_specs=placed, out_specs=P(None, "gx", "gy", "gz"), check_vma=False
    )
```

profile of v0, /device:TPU:232, one launch (start us, length us, event | category | flops | bytes accessed | tf_op | source)
XLA Modules:
  0.0 166.7 jit_solution(9116237188329100645)
XLA Ops:
  0.8 1.2 fusion.67
  9.2 1.9 %collective-permute-start.1 = (f32[32,1,8,128]{3,2,1,0:T(8,128)S(1)}, f32[32,1,8,128]{3,2,1,0:T(8,128)S(1)}, u32[]{:S(2)}, u32[]{:S(2)}) collective-permute-start(f32[32,1,8,128]{3,2,1,0:T(8,128)S(1)} %get-tuple-element.253), channel_id=1, source_target_pairs={{32,0},{64,32},{96,64},{128,96},{160,128},{192,160},{224,192},{33,... | collective-permute-start | bytes 393224 | tf_op jit(solution)/shard_map/ppermute | solution.py:15
  11.1 2.4 %collective-permute-start = (f32[32,1,8,128]{3,2,1,0:T(8,128)S(1)}, f32[32,1,8,128]{3,2,1,0:T(8,128)S(1)}, u32[]{:S(2)}, u32[]{:S(2)}) collective-permute-start(f32[32,1,8,128]{3,2,1,0:T(8,128)S(1)} %get-tuple-element.252), channel_id=1, source_target_pairs={{0,32},{32,64},{64,96},{96,128},{128,160},{160,192},{192,224},{1,3... | collective-permute-start | bytes 393224 | tf_op jit(solution)/shard_map/ppermute | solution.py:12
  15.4 2.0 %collective-permute-done = f32[32,1,8,128]{3,2,1,0:T(8,128)S(1)} collective-permute-done((f32[32,1,8,128]{3,2,1,0:T(8,128)S(1)}, f32[32,1,8,128]{3,2,1,0:T(8,128)S(1)}, u32[]{:S(2)}, u32[]{:S(2)}) %collective-permute-start) | collective-permute-done | bytes 131104 | tf_op jit(solution)/shard_map/ppermute | solution.py:12
  17.4 0.9 pad_maximum_fusion.3
  18.3 2.2 %copy.163 = f32[32,5,8,128]{0,3,2,1:T(8,128)S(1)} copy(f32[32,5,8,128]{3,2,1,0:T(8,128)} %pad_maximum_fusion.3) | data formatting | bytes 1310720 | tf_op jit(solution)/shard_map/concatenate | solution.py:16
  20.5 3.4 %collective-permute-start.3 = (f32[32,5,1,128]{0,3,2,1:T(8,128)S(1)}, f32[32,5,1,128]{0,3,2,1:T(8,128)S(1)}, u32[]{:S(2)}, u32[]{:S(2)}) collective-permute-start(f32[32,5,1,128]{0,3,2,1:T(8,128)S(1)} %get-tuple-element.232), channel_id=1, source_target_pairs={{8,0},{16,8},{24,16},{9,1},{17,9},{25,17},{10,2},{18,10},{26,18},{... | collective-permute-start | bytes 245768 | tf_op jit(solution)/shard_map/ppermute | solution.py:15
  23.9 1.3 collective-permute-start.2
  25.5 4.8 %collective-permute-done.3 = f32[32,5,1,128]{0,3,2,1:T(8,128)S(1)} collective-permute-done((f32[32,5,1,128]{0,3,2,1:T(8,128)S(1)}, f32[32,5,1,128]{0,3,2,1:T(8,128)S(1)}, u32[]{:S(2)}, u32[]{:S(2)}) %collective-permute-start.3) | collective-permute-done | bytes 81952 | tf_op jit(solution)/shard_map/ppermute | solution.py:15
  30.3 10.9 %collective-permute-done.2 = f32[32,5,1,128]{0,3,2,1:T(8,128)S(1)} collective-permute-done((f32[32,5,1,128]{0,3,2,1:T(8,128)S(1)}, f32[32,5,1,128]{0,3,2,1:T(8,128)S(1)}, u32[]{:S(2)}, u32[]{:S(2)}) %collective-permute-start.2) | collective-permute-done | bytes 81952 | tf_op jit(solution)/shard_map/ppermute | solution.py:12
  41.1 2.0 %pad_maximum_fusion = f32[32,5,10,128]{0,3,2,1:T(8,128)S(1)} fusion(f32[32,5,1,128]{0,3,2,1:T(8,128)S(1)} %collective-permute-done.3, f32[32,5,8,128]{0,3,2,1:T(8,128)} %copy-done.1, f32[32,5,1,128]{0,3,2,1:T(8,128)S(1)} %collective-permute-done.2), kind=kLoop, calls=%fused_computation.9 | loop fusion | flops 409600 | bytes 1638400 | tf_op jit(solution)/shard_map/concatenate | solution.py:16
  43.2 3.4 %collective-permute-start.4 = (f32[32,5,10,1]{0,3,2,1:T(1,128)S(1)}, f32[32,5,10,1]{0,3,2,1:T(1,128)S(1)}, u32[]{:S(2)}, u32[]{:S(2)}) collective-permute-start(f32[32,5,10,1]{0,3,2,1:T(1,128)S(1)} %slice.930), channel_id=1, source_target_pairs={{0,1},{1,2},{2,3},{3,4},{4,5},{5,6},{6,7},{8,9},{9,10},{10,11},{11... | collective-permute-start | bytes 19208 | tf_op jit(solution)/shard_map/ppermute | solution.py:12
  46.9 4.4 %collective-permute-done.4 = f32[32,5,10,1]{0,3,2,1:T(1,128)S(1)} collective-permute-done((f32[32,5,10,1]{0,3,2,1:T(1,128)S(1)}, f32[32,5,10,1]{0,3,2,1:T(1,128)S(1)}, u32[]{:S(2)}, u32[]{:S(2)}) %collective-permute-start.4) | collective-permute-done | bytes 6432 | tf_op jit(solution)/shard_map/ppermute | solution.py:12
  51.9 3.9 %collective-permute-start.5 = (f32[32,5,10,1]{0,3,2,1:T(1,128)}, f32[32,5,10,1]{0,3,2,1:T(1,128)}, u32[]{:S(2)}, u32[]{:S(2)}) collective-permute-start(f32[32,5,10,1]{0,3,2,1:T(1,128)} %get-tuple-element.225), channel_id=1, source_target_pairs={{1,0},{2,1},{3,2},{4,3},{5,4},{6,5},{7,6},{9,8},{10,9},{11,10},{12... | collective-permute-start | bytes 19208 | tf_op jit(solution)/shard_map/ppermute | solution.py:15
  56.1 0.8 copy.222
  56.9 0.8 copy.225
  57.7 0.8 copy.228
  58.6 0.8 scatter-add.60
  67.5 1.9 %collective-permute-start.7 = (f32[32,1,8,128]{3,2,1,0:T(8,128)S(1)}, f32[32,1,8,128]{3,2,1,0:T(8,128)S(1)}, u32[]{:S(2)}, u32[]{:S(2)}) collective-permute-start(f32[32,1,8,128]{3,2,1,0:T(8,128)S(1)} %get-tuple-element.251), channel_id=1, source_target_pairs={{32,0},{64,32},{96,64},{128,96},{160,128},{192,160},{224,192},{33,... | collective-permute-start | bytes 393224 | tf_op jit(solution)/shard_map/ppermute | solution.py:15
  69.5 2.4 %collective-permute-start.6 = (f32[32,1,8,128]{3,2,1,0:T(8,128)S(1)}, f32[32,1,8,128]{3,2,1,0:T(8,128)S(1)}, u32[]{:S(2)}, u32[]{:S(2)}) collective-permute-start(f32[32,1,8,128]{3,2,1,0:T(8,128)S(1)} %get-tuple-element.250), channel_id=1, source_target_pairs={{0,32},{32,64},{64,96},{96,128},{128,160},{160,192},{192,224},{1,3... | collective-permute-start | bytes 393224 | tf_op jit(solution)/shard_map/ppermute | solution.py:12
  72.0 3.8 %collective-permute-done.6 = f32[32,1,8,128]{3,2,1,0:T(8,128)S(1)} collective-permute-done((f32[32,1,8,128]{3,2,1,0:T(8,128)S(1)}, f32[32,1,8,128]{3,2,1,0:T(8,128)S(1)}, u32[]{:S(2)}, u32[]{:S(2)}) %collective-permute-start.6) | collective-permute-done | bytes 131104 | tf_op jit(solution)/shard_map/ppermute | solution.py:12
  75.7 0.9 pad_maximum_fusion.4
  76.6 2.2 %copy.178 = f32[32,5,8,128]{0,3,2,1:T(8,128)S(1)} copy(f32[32,5,8,128]{3,2,1,0:T(8,128)} %pad_maximum_fusion.4) | data formatting | bytes 1310720 | tf_op jit(solution)/shard_map/concatenate | solution.py:16
  78.9 3.4 %collective-permute-start.9 = (f32[32,5,1,128]{0,3,2,1:T(8,128)S(1)}, f32[32,5,1,128]{0,3,2,1:T(8,128)S(1)}, u32[]{:S(2)}, u32[]{:S(2)}) collective-permute-start(f32[32,5,1,128]{0,3,2,1:T(8,128)S(1)} %get-tuple-element.230), channel_id=1, source_target_pairs={{8,0},{16,8},{24,16},{9,1},{17,9},{25,17},{10,2},{18,10},{26,18},{... | collective-permute-start | bytes 245768 | tf_op jit(solution)/shard_map/ppermute | solution.py:15
  82.3 1.3 collective-permute-start.8
  83.6 1.2 convolution_bitcast_fusion.7
  84.8 3.7 %collective-permute-done.9 = f32[32,5,1,128]{0,3,2,1:T(8,128)S(1)} collective-permute-done((f32[32,5,1,128]{0,3,2,1:T(8,128)S(1)}, f32[32,5,1,128]{0,3,2,1:T(8,128)S(1)}, u32[]{:S(2)}, u32[]{:S(2)}) %collective-permute-start.9) | collective-permute-done | bytes 81952 | tf_op jit(solution)/shard_map/ppermute | solution.py:15
  88.6 8.2 %collective-permute-done.8 = f32[32,5,1,128]{0,3,2,1:T(8,128)S(1)} collective-permute-done((f32[32,5,1,128]{0,3,2,1:T(8,128)S(1)}, f32[32,5,1,128]{0,3,2,1:T(8,128)S(1)}, u32[]{:S(2)}, u32[]{:S(2)}) %collective-permute-start.8) | collective-permute-done | bytes 81952 | tf_op jit(solution)/shard_map/ppermute | solution.py:12
  96.8 2.0 %pad_maximum_fusion.1 = f32[32,5,10,128]{0,3,2,1:T(8,128)S(1)} fusion(f32[32,5,1,128]{0,3,2,1:T(8,128)S(1)} %collective-permute-done.9, f32[32,5,8,128]{0,3,2,1:T(8,128)} %copy-done, f32[32,5,1,128]{0,3,2,1:T(8,128)S(1)} %collective-permute-done.8), kind=kLoop, calls=%fused_computation.10 | loop fusion | flops 409600 | bytes 1638400 | tf_op jit(solution)/shard_map/concatenate | solution.py:16
  98.8 3.9 %collective-permute-start.10 = (f32[32,5,10,1]{0,3,2,1:T(1,128)S(1)}, f32[32,5,10,1]{0,3,2,1:T(1,128)S(1)}, u32[]{:S(2)}, u32[]{:S(2)}) collective-permute-start(f32[32,5,10,1]{0,3,2,1:T(1,128)S(1)} %slice.960), channel_id=1, source_target_pairs={{0,1},{1,2},{2,3},{3,4},{4,5},{5,6},{6,7},{8,9},{9,10},{10,11},{11... | collective-permute-start | bytes 19208 | tf_op jit(solution)/shard_map/ppermute | solution.py:12
  103.0 4.0 %collective-permute-done.10 = f32[32,5,10,1]{0,3,2,1:T(1,128)S(1)} collective-permute-done((f32[32,5,10,1]{0,3,2,1:T(1,128)S(1)}, f32[32,5,10,1]{0,3,2,1:T(1,128)S(1)}, u32[]{:S(2)}, u32[]{:S(2)}) %collective-permute-start.10) | collective-permute-done | bytes 6432 | tf_op jit(solution)/shard_map/ppermute | solution.py:12
  107.0 3.9 %collective-permute-start.11 = (f32[32,5,10,1]{0,3,2,1:T(1,128)S(1)}, f32[32,5,10,1]{0,3,2,1:T(1,128)S(1)}, u32[]{:S(2)}, u32[]{:S(2)}) collective-permute-start(f32[32,5,10,1]{0,3,2,1:T(1,128)S(1)} %get-tuple-element.223), channel_id=1, source_target_pairs={{1,0},{2,1},{3,2},{4,3},{5,4},{6,5},{7,6},{9,8},{10,9},{11,10},{12... | collective-permute-start | bytes 19208 | tf_op jit(solution)/shard_map/ppermute | solution.py:15
  112.1 0.8 copy.238
  112.9 0.8 copy.241
  119.9 1.9 %collective-permute-start.13 = (f32[32,1,8,128]{3,2,1,0:T(8,128)S(1)}, f32[32,1,8,128]{3,2,1,0:T(8,128)S(1)}, u32[]{:S(2)}, u32[]{:S(2)}) collective-permute-start(f32[32,1,8,128]{3,2,1,0:T(8,128)S(1)} %get-tuple-element.249), channel_id=1, source_target_pairs={{32,0},{64,32},{96,64},{128,96},{160,128},{192,160},{224,192},{33,... | collective-permute-start | bytes 393224 | tf_op jit(solution)/shard_map/ppermute | solution.py:15
  121.8 2.4 %collective-permute-start.12 = (f32[32,1,8,128]{3,2,1,0:T(8,128)S(1)}, f32[32,1,8,128]{3,2,1,0:T(8,128)S(1)}, u32[]{:S(2)}, u32[]{:S(2)}) collective-permute-start(f32[32,1,8,128]{3,2,1,0:T(8,128)S(1)} %get-tuple-element.248), channel_id=1, source_target_pairs={{0,32},{32,64},{64,96},{96,128},{128,160},{160,192},{192,224},{1,3... | collective-permute-start | bytes 393224 | tf_op jit(solution)/shard_map/ppermute | solution.py:12
  124.3 3.8 %collective-permute-done.12 = f32[32,1,8,128]{3,2,1,0:T(8,128)S(1)} collective-permute-done((f32[32,1,8,128]{3,2,1,0:T(8,128)S(1)}, f32[32,1,8,128]{3,2,1,0:T(8,128)S(1)}, u32[]{:S(2)}, u32[]{:S(2)}) %collective-permute-start.12) | collective-permute-done | bytes 131104 | tf_op jit(solution)/shard_map/ppermute | solution.py:12
  128.1 1.3 copy.193
  129.5 3.1 %collective-permute-start.15 = (f32[32,5,1,128]{0,3,2,1:T(8,128)S(1)}, f32[32,5,1,128]{0,3,2,1:T(8,128)S(1)}, u32[]{:S(2)}, u32[]{:S(2)}) collective-permute-start(f32[32,5,1,128]{0,3,2,1:T(8,128)S(1)} %get-tuple-element.228), channel_id=1, source_target_pairs={{8,0},{16,8},{24,16},{9,1},{17,9},{25,17},{10,2},{18,10},{26,18},{... | collective-permute-start | bytes 245768 | tf_op jit(solution)/shard_map/ppermute | solution.py:15
  132.6 1.3 collective-permute-start.14
  133.9 3.9 %collective-permute-done.15 = f32[32,5,1,128]{0,3,2,1:T(8,128)S(1)} collective-permute-done((f32[32,5,1,128]{0,3,2,1:T(8,128)S(1)}, f32[32,5,1,128]{0,3,2,1:T(8,128)S(1)}, u32[]{:S(2)}, u32[]{:S(2)}) %collective-permute-start.15) | collective-permute-done | bytes 81952 | tf_op jit(solution)/shard_map/ppermute | solution.py:15
  137.8 8.7 %collective-permute-done.14 = f32[32,5,1,128]{0,3,2,1:T(8,128)S(1)} collective-permute-done((f32[32,5,1,128]{0,3,2,1:T(8,128)S(1)}, f32[32,5,1,128]{0,3,2,1:T(8,128)S(1)}, u32[]{:S(2)}, u32[]{:S(2)}) %collective-permute-start.14) | collective-permute-done | bytes 81952 | tf_op jit(solution)/shard_map/ppermute | solution.py:12
  146.5 2.0 %pad_maximum_fusion.2 = f32[32,5,10,128]{0,3,2,1:T(8,128)S(1)} fusion(f32[32,5,1,128]{0,3,2,1:T(8,128)S(1)} %collective-permute-done.15, f32[32,5,8,128]{0,3,2,1:T(8,128)} %copy-done.2, f32[32,5,1,128]{0,3,2,1:T(8,128)S(1)} %collective-permute-done.14), kind=kLoop, calls=%fused_computation.11 | loop fusion | flops 409600 | bytes 1638400 | tf_op jit(solution)/shard_map/concatenate | solution.py:16
  148.6 3.9 %collective-permute-start.16 = (f32[32,5,10,1]{0,3,2,1:T(1,128)S(1)}, f32[32,5,10,1]{0,3,2,1:T(1,128)S(1)}, u32[]{:S(2)}, u32[]{:S(2)}) collective-permute-start(f32[32,5,10,1]{0,3,2,1:T(1,128)S(1)} %slice.990), channel_id=1, source_target_pairs={{0,1},{1,2},{2,3},{3,4},{4,5},{5,6},{6,7},{8,9},{9,10},{10,11},{11... | collective-permute-start | bytes 19208 | tf_op jit(solution)/shard_map/ppermute | solution.py:12
  152.5 3.9 %collective-permute-done.16 = f32[32,5,10,1]{0,3,2,1:T(1,128)S(1)} collective-permute-done((f32[32,5,10,1]{0,3,2,1:T(1,128)S(1)}, f32[32,5,10,1]{0,3,2,1:T(1,128)S(1)}, u32[]{:S(2)}, u32[]{:S(2)}) %collective-permute-start.16) | collective-permute-done | bytes 6432 | tf_op jit(solution)/shard_map/ppermute | solution.py:12
  156.5 2.2 %collective-permute-start.17 = (f32[32,5,10,1]{0,3,2,1:T(1,128)S(1)}, f32[32,5,10,1]{0,3,2,1:T(1,128)}, u32[]{:S(2)}, u32[]{:S(2)}) collective-permute-start(f32[32,5,10,1]{0,3,2,1:T(1,128)S(1)} %get-tuple-element.221), channel_id=1, source_target_pairs={{1,0},{2,1},{3,2},{4,3},{5,4},{6,5},{7,6},{9,8},{10,9},{11,10},{12... | collective-permute-start | bytes 19208 | tf_op jit(solution)/shard_map/ppermute | solution.py:15
  158.8 3.5 %collective-permute-done.17 = f32[32,5,10,1]{0,3,2,1:T(1,128)} collective-permute-done((f32[32,5,10,1]{0,3,2,1:T(1,128)S(1)}, f32[32,5,10,1]{0,3,2,1:T(1,128)}, u32[]{:S(2)}, u32[]{:S(2)}) %collective-permute-start.17) | collective-permute-done | bytes 6432 | tf_op jit(solution)/shard_map/ppermute | solution.py:15
  164.7 1.1 convolution_bitcast_fusion.1
  (256 shorter events, 29.0 us)
Async XLA Ops:
  0.0 2.4 %copy-start.32 = (s32[3,8,128]{2,1,0:T(8,128)S(1)}, s32[3,8,128]{2,1,0:T(8,128)}, u32[]{:S(2)}) copy-start(s32[3,8,128]{2,1,0:T(8,128)} %param.47) | copy-start | bytes 36868
  2.0 1.3 copy-start.30
  2.1 1.3 copy-start.43
  3.4 21.7 %copy-start.17 = (bf16[32,3072]{1,0:T(8,128)(2,1)}, bf16[32,3072]{1,0:T(8,128)(2,1)S(1)}, u32[]{:S(2)}) copy-start(bf16[32,3072]{1,0:T(8,128)(2,1)S(1)} %reshape_squeeze.12) | copy-start | bytes 589828
  4.7 51.1 %copy-start.15 = (bf16[32,3072]{1,0:T(8,128)(2,1)}, bf16[32,3072]{1,0:T(8,128)(2,1)S(1)}, u32[]{:S(2)}) copy-start(bf16[32,3072]{1,0:T(8,128)(2,1)S(1)} %reshape_squeeze.14) | copy-start | bytes 589828
  5.4 19.8 %copy-start.9 = (f32[3072,32]{0,1:T(8,128)}, f32[3072,32]{0,1:T(8,128)S(1)}, u32[]{:S(2)}) copy-start(f32[3072,32]{0,1:T(8,128)S(1)} %fusion.64) | copy-start | bytes 1179652
  6.5 1.6 copy-start.18
  6.6 2.2 %copy-start.33 = (s32[3,8,128]{2,1,0:T(8,128)S(1)}, s32[3,8,128]{2,1,0:T(8,128)}, u32[]{:S(2)}) copy-start(s32[3,8,128]{2,1,0:T(8,128)} %param.47) | copy-start | bytes 36868
  6.6 2.2 %slice-start = ((s32[3,8,128]{2,1,0:T(8,128)}), s32[2,8,128]{2,1,0:T(8,128)S(1)}, s32[]{:S(2)}) async-start(s32[3,8,128]{2,1,0:T(8,128)} %param.47), calls=%async_computation | async-start | bytes 16384 | tf_op jit(solution)/shard_map/slice | solution.py:22
  8.8 4.7 %copy-start.41 = (bf16[3,32,64]{2,1,0:T(8,128)(2,1)S(1)}, bf16[3,32,64]{2,1,0:T(8,128)(2,1)}, u32[]{:S(2)}) copy-start(bf16[3,32,64]{2,1,0:T(8,128)(2,1)} %param.51) | copy-start | bytes 36868
  8.9 5.9 %copy-start.44 = (f32[3,32]{1,0:T(4,128)S(1)}, f32[3,32]{1,0:T(4,128)}, u32[]{:S(2)}) copy-start(f32[3,32]{1,0:T(4,128)} %param.53) | copy-start | bytes 1156
  9.2 6.2 %collective-permute-start.1 = (f32[32,1,8,128]{3,2,1,0:T(8,128)S(1)}, f32[32,1,8,128]{3,2,1,0:T(8,128)S(1)}, u32[]{:S(2)}, u32[]{:S(2)}) collective-permute-start(f32[32,1,8,128]{3,2,1,0:T(8,128)S(1)} %get-tuple-element.253), channel_id=1, source_target_pairs={{32,0},{64,32},{96,64},{128,96},{160,128},{192,160},{224,192},{33,... | collective-permute-start | bytes 393224 | tf_op jit(solution)/shard_map/ppermute | solution.py:15
  11.1 6.3 %collective-permute-start = (f32[32,1,8,128]{3,2,1,0:T(8,128)S(1)}, f32[32,1,8,128]{3,2,1,0:T(8,128)S(1)}, u32[]{:S(2)}, u32[]{:S(2)}) collective-permute-start(f32[32,1,8,128]{3,2,1,0:T(8,128)S(1)} %get-tuple-element.252), channel_id=1, source_target_pairs={{0,32},{32,64},{64,96},{96,128},{128,160},{160,192},{192,224},{1,3... | collective-permute-start | bytes 393224 | tf_op jit(solution)/shard_map/ppermute | solution.py:12
  20.4 9.8 %copy-start.1 = (f32[32,5,8,128]{0,3,2,1:T(8,128)}, f32[32,5,8,128]{0,3,2,1:T(8,128)S(1)}, u32[]{:S(2)}) copy-start(f32[32,5,8,128]{0,3,2,1:T(8,128)S(1)} %copy.163) | copy-start | bytes 1966084
  20.5 9.8 %collective-permute-start.3 = (f32[32,5,1,128]{0,3,2,1:T(8,128)S(1)}, f32[32,5,1,128]{0,3,2,1:T(8,128)S(1)}, u32[]{:S(2)}, u32[]{:S(2)}) collective-permute-start(f32[32,5,1,128]{0,3,2,1:T(8,128)S(1)} %get-tuple-element.232), channel_id=1, source_target_pairs={{8,0},{16,8},{24,16},{9,1},{17,9},{25,17},{10,2},{18,10},{26,18},{... | collective-permute-start | bytes 245768 | tf_op jit(solution)/shard_map/ppermute | solution.py:15
  23.9 17.3 %collective-permute-start.2 = (f32[32,5,1,128]{0,3,2,1:T(8,128)S(1)}, f32[32,5,1,128]{0,3,2,1:T(8,128)S(1)}, u32[]{:S(2)}, u32[]{:S(2)}) collective-permute-start(f32[32,5,1,128]{0,3,2,1:T(8,128)S(1)} %get-tuple-element.231), channel_id=1, source_target_pairs={{0,8},{8,16},{16,24},{1,9},{9,17},{17,25},{2,10},{10,18},{18,26},{... | collective-permute-start | bytes 245768 | tf_op jit(solution)/shard_map/ppermute | solution.py:12
  25.4 21.2 %copy-start.7 = (f32[3072,32]{0,1:T(8,128)S(1)}, f32[3072,32]{0,1:T(8,128)}, u32[]{:S(2)}) copy-start(f32[3072,32]{0,1:T(8,128)} %copy-done.6) | copy-start | bytes 1179652
  25.5 21.2 %copy-start.19 = (bf16[32,3072]{1,0:T(8,128)(2,1)S(1)}, bf16[32,3072]{1,0:T(8,128)(2,1)}, u32[]{:S(2)}) copy-start(bf16[32,3072]{1,0:T(8,128)(2,1)} %copy-done.18) | copy-start | bytes 589828
  25.5 30.3 %copy-start.4 = (f32[3072,32]{0,1:T(8,128)S(1)}, f32[3072,32]{0,1:T(8,128)}, u32[]{:S(2)}) copy-start(f32[3072,32]{0,1:T(8,128)} %copy-done.3) | copy-start | bytes 1179652
  43.2 8.1 %collective-permute-start.4 = (f32[32,5,10,1]{0,3,2,1:T(1,128)S(1)}, f32[32,5,10,1]{0,3,2,1:T(1,128)S(1)}, u32[]{:S(2)}, u32[]{:S(2)}) collective-permute-start(f32[32,5,10,1]{0,3,2,1:T(1,128)S(1)} %slice.930), channel_id=1, source_target_pairs={{0,1},{1,2},{2,3},{3,4},{4,5},{5,6},{6,7},{8,9},{9,10},{10,11},{11... | collective-permute-start | bytes 19208 | tf_op jit(solution)/shard_map/ppermute | solution.py:12
  51.9 7.5 %collective-permute-start.5 = (f32[32,5,10,1]{0,3,2,1:T(1,128)}, f32[32,5,10,1]{0,3,2,1:T(1,128)}, u32[]{:S(2)}, u32[]{:S(2)}) collective-permute-start(f32[32,5,10,1]{0,3,2,1:T(1,128)} %get-tuple-element.225), channel_id=1, source_target_pairs={{1,0},{2,1},{3,2},{4,3},{5,4},{6,5},{7,6},{9,8},{10,9},{11,10},{12... | collective-permute-start | bytes 19208 | tf_op jit(solution)/shard_map/ppermute | solution.py:15
  61.2 1.3 copy-start.39
  61.2 1.3 copy-start.40
  62.9 1.2 copy-start.28
  67.5 4.4 %collective-permute-start.7 = (f32[32,1,8,128]{3,2,1,0:T(8,128)S(1)}, f32[32,1,8,128]{3,2,1,0:T(8,128)S(1)}, u32[]{:S(2)}, u32[]{:S(2)}) collective-permute-start(f32[32,1,8,128]{3,2,1,0:T(8,128)S(1)} %get-tuple-element.251), channel_id=1, source_target_pairs={{32,0},{64,32},{96,64},{128,96},{160,128},{192,160},{224,192},{33,... | collective-permute-start | bytes 393224 | tf_op jit(solution)/shard_map/ppermute | solution.py:15
  69.5 6.3 %collective-permute-start.6 = (f32[32,1,8,128]{3,2,1,0:T(8,128)S(1)}, f32[32,1,8,128]{3,2,1,0:T(8,128)S(1)}, u32[]{:S(2)}, u32[]{:S(2)}) collective-permute-start(f32[32,1,8,128]{3,2,1,0:T(8,128)S(1)} %get-tuple-element.250), channel_id=1, source_target_pairs={{0,32},{32,64},{64,96},{96,128},{128,160},{160,192},{192,224},{1,3... | collective-permute-start | bytes 393224 | tf_op jit(solution)/shard_map/ppermute | solution.py:12
  76.6 7.0 %copy-start.10 = (f32[3072,32]{0,1:T(8,128)S(1)}, f32[3072,32]{0,1:T(8,128)}, u32[]{:S(2)}) copy-start(f32[3072,32]{0,1:T(8,128)} %copy-done.9) | copy-start | bytes 1179652
  78.9 9.7 %copy-start = (f32[32,5,8,128]{0,3,2,1:T(8,128)}, f32[32,5,8,128]{0,3,2,1:T(8,128)S(1)}, u32[]{:S(2)}) copy-start(f32[32,5,8,128]{0,3,2,1:T(8,128)S(1)} %copy.178) | copy-start | bytes 1966084
  78.9 9.6 %collective-permute-start.9 = (f32[32,5,1,128]{0,3,2,1:T(8,128)S(1)}, f32[32,5,1,128]{0,3,2,1:T(8,128)S(1)}, u32[]{:S(2)}, u32[]{:S(2)}) collective-permute-start(f32[32,5,1,128]{0,3,2,1:T(8,128)S(1)} %get-tuple-element.230), channel_id=1, source_target_pairs={{8,0},{16,8},{24,16},{9,1},{17,9},{25,17},{10,2},{18,10},{26,18},{... | collective-permute-start | bytes 245768 | tf_op jit(solution)/shard_map/ppermute | solution.py:15
  82.3 14.5 %collective-permute-start.8 = (f32[32,5,1,128]{0,3,2,1:T(8,128)S(1)}, f32[32,5,1,128]{0,3,2,1:T(8,128)S(1)}, u32[]{:S(2)}, u32[]{:S(2)}) collective-permute-start(f32[32,5,1,128]{0,3,2,1:T(8,128)S(1)} %get-tuple-element.229), channel_id=1, source_target_pairs={{0,8},{8,16},{16,24},{1,9},{9,17},{17,25},{2,10},{10,18},{18,26},{... | collective-permute-start | bytes 245768 | tf_op jit(solution)/shard_map/ppermute | solution.py:12
  84.8 17.9 %copy-start.8 = (f32[3072,32]{0,1:T(8,128)S(1)}, f32[3072,32]{0,1:T(8,128)}, u32[]{:S(2)}) copy-start(f32[3072,32]{0,1:T(8,128)} %copy-done.6) | copy-start | bytes 1179652
  84.8 17.9 %copy-start.14 = (f32[3072,32]{0,1:T(8,128)S(1)}, f32[3072,32]{0,1:T(8,128)}, u32[]{:S(2)}) copy-start(f32[3072,32]{0,1:T(8,128)} %copy-done.13) | copy-start | bytes 1179652
  84.8 17.9 %copy-start.20 = (bf16[32,3072]{1,0:T(8,128)(2,1)S(1)}, bf16[32,3072]{1,0:T(8,128)(2,1)}, u32[]{:S(2)}) copy-start(bf16[32,3072]{1,0:T(8,128)(2,1)} %copy-done.18) | copy-start | bytes 589828
  84.8 26.1 %copy-start.5 = (f32[3072,32]{0,1:T(8,128)S(1)}, f32[3072,32]{0,1:T(8,128)}, u32[]{:S(2)}) copy-start(f32[3072,32]{0,1:T(8,128)} %copy-done.3) | copy-start | bytes 1179652
  84.8 26.1 %copy-start.12 = (f32[3072,32]{0,1:T(8,128)S(1)}, f32[3072,32]{0,1:T(8,128)}, u32[]{:S(2)}) copy-start(f32[3072,32]{0,1:T(8,128)} %copy-done.11) | copy-start | bytes 1179652
  84.8 26.1 %copy-start.16 = (bf16[32,3072]{1,0:T(8,128)(2,1)S(1)}, bf16[32,3072]{1,0:T(8,128)(2,1)}, u32[]{:S(2)}) copy-start(bf16[32,3072]{1,0:T(8,128)(2,1)} %copy-done.15) | copy-start | bytes 589828
  98.8 8.2 %collective-permute-start.10 = (f32[32,5,10,1]{0,3,2,1:T(1,128)S(1)}, f32[32,5,10,1]{0,3,2,1:T(1,128)S(1)}, u32[]{:S(2)}, u32[]{:S(2)}) collective-permute-start(f32[32,5,10,1]{0,3,2,1:T(1,128)S(1)} %slice.960), channel_id=1, source_target_pairs={{0,1},{1,2},{2,3},{3,4},{4,5},{5,6},{6,7},{8,9},{9,10},{10,11},{11... | collective-permute-start | bytes 19208 | tf_op jit(solution)/shard_map/ppermute | solution.py:12
  107.0 6.8 %collective-permute-start.11 = (f32[32,5,10,1]{0,3,2,1:T(1,128)S(1)}, f32[32,5,10,1]{0,3,2,1:T(1,128)S(1)}, u32[]{:S(2)}, u32[]{:S(2)}) collective-permute-start(f32[32,5,10,1]{0,3,2,1:T(1,128)S(1)} %get-tuple-element.223), channel_id=1, source_target_pairs={{1,0},{2,1},{3,2},{4,3},{5,4},{6,5},{7,6},{9,8},{10,9},{11,10},{12... | collective-permute-start | bytes 19208 | tf_op jit(solution)/shard_map/ppermute | solution.py:15
  115.0 1.3 copy-start.37
  115.0 1.3 copy-start.38
  116.7 1.2 copy-start.25
  119.9 4.4 %collective-permute-start.13 = (f32[32,1,8,128]{3,2,1,0:T(8,128)S(1)}, f32[32,1,8,128]{3,2,1,0:T(8,128)S(1)}, u32[]{:S(2)}, u32[]{:S(2)}) collective-permute-start(f32[32,1,8,128]{3,2,1,0:T(8,128)S(1)} %get-tuple-element.249), channel_id=1, source_target_pairs={{32,0},{64,32},{96,64},{128,96},{160,128},{192,160},{224,192},{33,... | collective-permute-start | bytes 393224 | tf_op jit(solution)/shard_map/ppermute | solution.py:15
  121.8 6.3 %collective-permute-start.12 = (f32[32,1,8,128]{3,2,1,0:T(8,128)S(1)}, f32[32,1,8,128]{3,2,1,0:T(8,128)S(1)}, u32[]{:S(2)}, u32[]{:S(2)}) collective-permute-start(f32[32,1,8,128]{3,2,1,0:T(8,128)S(1)} %get-tuple-element.248), channel_id=1, source_target_pairs={{0,32},{32,64},{64,96},{96,128},{128,160},{160,192},{192,224},{1,3... | collective-permute-start | bytes 393224 | tf_op jit(solution)/shard_map/ppermute | solution.py:12
  129.4 8.4 %copy-start.2 = (f32[32,5,8,128]{0,3,2,1:T(8,128)}, f32[32,5,8,128]{0,3,2,1:T(8,128)S(1)}, u32[]{:S(2)}) copy-start(f32[32,5,8,128]{0,3,2,1:T(8,128)S(1)} %copy.193) | copy-start | bytes 1966084
  129.5 8.4 %collective-permute-start.15 = (f32[32,5,1,128]{0,3,2,1:T(8,128)S(1)}, f32[32,5,1,128]{0,3,2,1:T(8,128)S(1)}, u32[]{:S(2)}, u32[]{:S(2)}) collective-permute-start(f32[32,5,1,128]{0,3,2,1:T(8,128)S(1)} %get-tuple-element.228), channel_id=1, source_target_pairs={{8,0},{16,8},{24,16},{9,1},{17,9},{25,17},{10,2},{18,10},{26,18},{... | collective-permute-start | bytes 245768 | tf_op jit(solution)/shard_map/ppermute | solution.py:15
  132.6 13.9 %collective-permute-start.14 = (f32[32,5,1,128]{0,3,2,1:T(8,128)S(1)}, f32[32,5,1,128]{0,3,2,1:T(8,128)S(1)}, u32[]{:S(2)}, u32[]{:S(2)}) collective-permute-start(f32[32,5,1,128]{0,3,2,1:T(8,128)S(1)} %get-tuple-element.227), channel_id=1, source_target_pairs={{0,8},{8,16},{16,24},{1,9},{9,17},{17,25},{2,10},{10,18},{18,26},{... | collective-permute-start | bytes 245768 | tf_op jit(solution)/shard_map/ppermute | solution.py:12
  148.6 7.8 %collective-permute-start.16 = (f32[32,5,10,1]{0,3,2,1:T(1,128)S(1)}, f32[32,5,10,1]{0,3,2,1:T(1,128)S(1)}, u32[]{:S(2)}, u32[]{:S(2)}) collective-permute-start(f32[32,5,10,1]{0,3,2,1:T(1,128)S(1)} %slice.990), channel_id=1, source_target_pairs={{0,1},{1,2},{2,3},{3,4},{4,5},{5,6},{6,7},{8,9},{9,10},{10,11},{11... | collective-permute-start | bytes 19208 | tf_op jit(solution)/shard_map/ppermute | solution.py:12
  156.5 5.8 %collective-permute-start.17 = (f32[32,5,10,1]{0,3,2,1:T(1,128)S(1)}, f32[32,5,10,1]{0,3,2,1:T(1,128)}, u32[]{:S(2)}, u32[]{:S(2)}) collective-permute-start(f32[32,5,10,1]{0,3,2,1:T(1,128)S(1)} %get-tuple-element.221), channel_id=1, source_target_pairs={{1,0},{2,1},{3,2},{4,3},{5,4},{6,5},{7,6},{9,8},{10,9},{11,10},{12... | collective-permute-start | bytes 19208 | tf_op jit(solution)/shard_map/ppermute | solution.py:15
  (20 other events, 18.1 us)
where the time goes:
time: 168 us; the launch traced here: 167 us
  waiting for transfers between devices  65.6 us (39%)
  starting transfers between devices  48.1 us (29%)
  local copies, waits for them, and re-layouts  26.8 us (16%)
  other arithmetic  14.1 us (8%)
  matrix products  9.69 us (6%)
  between operations  2.35 us (1%)
    ppermute x9, waiting for transfers between devices, with_halo(): lax.ppermute(lax.slice_in_dim(block, block.shape[dim] - width, None, axis...  49.6 us
    ppermute x9, starting transfers between devices, with_halo(): lax.ppermute(lax.slice_in_dim(block, 0, width, axis=dim), axis, backward)  25.7 us
    ppermute x9, starting transfers between devices, with_halo(): lax.ppermute(lax.slice_in_dim(block, block.shape[dim] - width, None, axis...  22.4 us
    ppermute x9, waiting for transfers between devices, with_halo(): lax.ppermute(lax.slice_in_dim(block, 0, width, axis=dim), axis, backward)  16 us
    unnamed x137, local copies, waits for them, and re-layouts  12.6 us
    concatenate x6, other arithmetic, with_halo(): block = jnp.concatenate([low, block, high], axis=dim)  7.77 us
    concatenate x3, local copies, waits for them, and re-layouts, with_halo(): block = jnp.concatenate([low, block, high], axis=dim)  5.65 us
    dot_general x9, matrix products, edge_layer(): jnp.dot(weight_in[:, 2 * channels:], edge_now.reshape(channels, -1), pref...  3.4 us
  transfers between devices with their start and end apart: 18, of which 15 were waited for; matrix products, arithmetic and copies ran while one was open for 6% of the time, Pallas kernels for 0%

commit v1 on v0

v1 whole, which is shorter than its diff:
```python
import functools

import jax
import jax.numpy as jnp
from jax import lax
from jax.experimental import pallas as pl
from jax.experimental.pallas import tpu as pltpu
from jax.sharding import PartitionSpec as P

F32 = jnp.float32
BF16 = jnp.bfloat16
LANES = 128


def swap_pairs(count, offset):
    pairs = []
    for i in range(offset, count, 2):
        j = (i + 1) % count
        pairs += [(i, j), (j, i)]
    return pairs


def exchange(values, axis):
    count = lax.axis_size(axis)
    even, odd = values
    got_odd = lax.ppermute(odd, axis, swap_pairs(count, 1))
    got_even = lax.ppermute(even, axis, swap_pairs(count, 0))
    return got_even, got_odd


def silu(v):
    return v / (1.0 + jnp.exp(-v))


def column(row):
    width = row.shape[1]
    eye = lax.broadcasted_iota(jnp.int32, (width, width), 0) == lax.broadcasted_iota(
        jnp.int32, (width, width), 1
    )
    return jnp.sum(jnp.where(eye, row, 0.0), axis=1, keepdims=True)


def tile(values, k):
    return values[:, k * LANES : (k + 1) * LANES]


def place(position, count, got_even, got_odd):
    is_even = position % 2 == 0
    low = jnp.where(is_even, got_odd, got_even)
    high = jnp.where(is_even, got_even, got_odd)
    low = jnp.where(position > 0, low, 0.0)
    high = jnp.where(position < count - 1, high, 0.0)
    return low, high


def edge_stage(sizes, layer, last, h_ref, e_in, e_out, w_ref, win, wout, bias, p_ref, sxe, sxo, pos):
    nx, ny = sizes
    lane = lax.broadcasted_iota(jnp.int32, (32, LANES), 1)
    span = ny * LANES
    w_in, w_out = win[layer], wout[layer]
    b = column(bias[layer : layer + 1, :])
    zero_tile = jnp.zeros((32, LANES), BF16)
    prev_x = None
    for x in range(nx):
        cur = h_ref[:, x * span : (x + 1) * span]
        ahead_x = h_ref[:, (x + 1) * span : (x + 2) * span] if x + 1 < nx else jnp.zeros_like(cur)
        ahead_y = jnp.concatenate([cur[:, LANES:], zero_tile], axis=1)
        ahead_z = jnp.concatenate(
            [
                jnp.where(
                    lane < LANES - 1, pltpu.roll(tile(cur, y).astype(F32), LANES - 1, 1), 0.0
                ).astype(BF16)
                for y in range(ny)
            ],
            axis=1,
        )
        weighted = []
        for d, shifted in enumerate((ahead_x, ahead_y, ahead_z)):
            edge = e_in[d, :, x * span : (x + 1) * span]
            pre = jnp.dot(
                w_in, jnp.concatenate([cur, shifted, edge], axis=0), preferred_element_type=F32
            )
            hid = silu(pre + b).astype(BF16)
            msg = jnp.dot(w_out, hid, preferred_element_type=F32)
            if not last:
                e_out[d, :, x * span : (x + 1) * span] = (edge.astype(F32) + msg).astype(BF16)
            weighted.append(
                [tile(msg, y) * w_ref[d, x * ny + y : x * ny + y + 1, :] for y in range(ny)]
            )
        wx, wy, wz = weighted
        for y in range(ny):
            acc = wx[y] + wy[y] + wz[y] + pltpu.roll(wz[y], 1, 1)
            if y > 0:
                acc = acc + wy[y - 1]
            if x > 0:
                acc = acc + prev_x[y]
            p_ref[:, (x * ny + y) * LANES : (x * ny + y + 1) * LANES] = acc
        prev_x = wx
    low = slice(0, span)
    high = slice((nx - 1) * span, nx * span)

    @pl.when(pos % 2 == 0)
    def _():
        sxe[...] = p_ref[:, high]
        sxo[...] = p_ref[:, low]

    @pl.when(pos % 2 == 1)
    def _():
        sxe[...] = p_ref[:, low]
        sxo[...] = p_ref[:, high]


def first_kernel(
    sizes, f_ref, es_ref, m_ref, win, wout, bias, h_ref, e_ref, w_ref, p_ref, sxe, sxo, e0, buf
):
    nx, ny = sizes
    rows = nx * ny

    def unpack(source, dest):
        buf[...] = source.astype(F32).reshape(buf.shape)
        for r in range(rows):
            dest[..., r * LANES : (r + 1) * LANES] = buf[pl.ds(r, 32, stride=rows), :].astype(BF16)

    unpack(f_ref[...], h_ref)
    for d in range(3):
        unpack(es_ref[d], e0.at[d])
    counts = m_ref[...]
    fluid = counts[1, 1:2, 1:2] > 0
    lane = lax.broadcasted_iota(jnp.int32, (ny, LANES), 1)
    sub = lax.broadcasted_iota(jnp.int32, (ny, LANES), 0)
    for x in range(nx):
        here = counts[x]
        for d in range(3):
            if d == 0:
                there = counts[x + 1] if x + 1 < nx else jnp.zeros_like(here)
            elif d == 1:
                there = jnp.where(sub < ny - 1, pltpu.roll(here, ny - 1, 0), 0)
            else:
                there = jnp.where(lane < LANES - 1, pltpu.roll(here, LANES - 1, 1), 0)
            shared = jnp.minimum(here, there)
            share = 1.0 / jnp.maximum(shared, 1).astype(F32)
            w_ref[d, x * ny : (x + 1) * ny, :] = jnp.where(fluid & (shared > 0), share, 0.0)
    edge_stage(
        sizes, 0, False, h_ref, e0, e_ref, w_ref, win, wout, bias, p_ref, sxe, sxo, lax.axis_index("gx")
    )


def y_faces(sizes, xcount, ycount, p_ref, rxe, rxo, sye, syo):
    nx, ny = sizes
    low_x, high_x = place(lax.axis_index("gx"), xcount, rxe[...], rxo[...])
    faces = []
    for y in (0, ny - 1):
        pieces = []
        for x in range(nx):
            t = p_ref[:, (x * ny + y) * LANES : (x * ny + y + 1) * LANES]
            if x == 0:
                t = t + tile(low_x, y)
            if x == nx - 1:
                t = t + tile(high_x, y)
            pieces.append(t)
        faces.append(jnp.concatenate(pieces, axis=1))
    low, high = faces
    is_even = lax.axis_index("gy") % 2 == 0
    sye[...] = jnp.where(is_even, high, low)
    syo[...] = jnp.where(is_even, low, high)


def folded_tile(sizes, p_ref, low_x, high_x, low_y, high_y, x, y):
    nx, ny = sizes
    t = p_ref[:, (x * ny + y) * LANES : (x * ny + y + 1) * LANES]
    if x == 0:
        t = t + tile(low_x, y)
    if x == nx - 1:
        t = t + tile(high_x, y)
    if y == 0:
        t = t + tile(low_y, x)
    if y == ny - 1:
        t = t + tile(high_y, x)
    return t


def z_faces(sizes, xcount, ycount, p_ref, rxe, rxo, rye, ryo, sz):
    nx, ny = sizes
    low_x, high_x = place(lax.axis_index("gx"), xcount, rxe[...], rxo[...])
    low_y, high_y = place(lax.axis_index("gy"), ycount, rye[...], ryo[...])
    lane = lax.broadcasted_iota(jnp.int32, (32, LANES), 1)
    acc = jnp.zeros((32, LANES), F32)
    for x in range(nx):
        for y in range(ny):
            k = x * ny + y
            t = folded_tile(sizes, p_ref, low_x, high_x, low_y, high_y, x, y)
            mine = (lane == 2 * k) | (lane == (2 * k - 1) % LANES)
            acc = jnp.where(mine, pltpu.roll(t, 2 * k, 1) if k else t, acc)
    sz[...] = acc


def node_stage(
    sizes, counts, layer, h_in, p_ref, rxe, rxo, rye, ryo, rze, rzo, nin, nout, nbias, write
):
    nx, ny = sizes
    xcount, ycount, zcount = counts
    low_x, high_x = place(lax.axis_index("gx"), xcount, rxe[...], rxo[...])
    low_y, high_y = place(lax.axis_index("gy"), ycount, rye[...], ryo[...])
    low_z, high_z = place(lax.axis_index("gz"), zcount, rze[...], rzo[...])
    lane = lax.broadcasted_iota(jnp.int32, (32, LANES), 1)
    joined = jnp.where(lane % 2 == 0, pltpu.roll(low_z, 1, 1), pltpu.roll(high_z, LANES - 1, 1))
    w_in, w_out = nin[layer], nout[layer]
    b = column(nbias[layer : layer + 1, :])
    ends = (lane == 0) | (lane == LANES - 1)
    for x in range(nx):
        pieces = []
        for y in range(ny):
            k = x * ny + y
            t = folded_tile(sizes, p_ref, low_x, high_x, low_y, high_y, x, y)
            back = pltpu.roll(joined, LANES - 2 * k, 1) if k else joined
            pieces.append((t + jnp.where(ends, back, 0.0)).astype(BF16))
        span = slice(x * ny * LANES, (x + 1) * ny * LANES)
        cur = h_in[:, span]
        stacked = jnp.concatenate([cur, jnp.concatenate(pieces, axis=1)], axis=0)
        hid = silu(jnp.dot(w_in, stacked, preferred_element_type=F32) + b).astype(BF16)
        res = jnp.dot(w_out, hid, preferred_element_type=F32)
        write(x, cur.astype(F32) + res)


def middle_kernel(
    sizes, counts, layer, last, h_in, e_in, w_ref, p_in, rxe, rxo, rye, ryo, rze, rzo,
    nin, nout, nbias, win, wout, bias, *outs,
):
    nx, ny = sizes
    if last:
        h_out, p_ref, sxe, sxo = outs
        e_out = None
    else:
        h_out, e_out, p_ref, sxe, sxo = outs

    def write(x, value):
        h_out[:, x * ny * LANES : (x + 1) * ny * LANES] = value.astype(BF16)

    node_stage(
        sizes, counts, layer, h_in, p_in, rxe, rxo, rye, ryo, rze, rzo, nin, nout, nbias, write
    )
    edge_stage(
        sizes, layer + 1, last, h_out, e_in, e_out, w_ref, win, wout, bias, p_ref, sxe, sxo,
        lax.axis_index("gx"),
    )


def last_kernel(
    sizes, counts, layer, h_in, p_in, rxe, rxo, rye, ryo, rze, rzo, nin, nout, nbias, out, buf
):
    nx, ny = sizes
    rows = nx * ny

    def write(x, value):
        for y in range(ny):
            buf[pl.ds(x * ny + y, 32, stride=rows), :] = tile(value, y)

    node_stage(
        sizes, counts, layer, h_in, p_in, rxe, rxo, rye, ryo, rze, rzo, nin, nout, nbias, write
    )
    out[...] = buf[...].reshape(out.shape).astype(BF16)


def call(body, args, outs, scratch=()):
    vmem = pl.BlockSpec(memory_space=pltpu.VMEM)
    return pl.pallas_call(
        body,
        out_shape=[jax.ShapeDtypeStruct(s, d) for s, d in outs],
        in_specs=[vmem] * len(args),
        out_specs=[vmem] * len(outs),
        scratch_shapes=list(scratch),
    )(*args)


def on_device(
    features, edge_state, multiplicity, edge_in, edge_out, edge_bias, node_in, node_out, node_bias
):
    ch, nx, ny, nz = features.shape
    layers = edge_in.shape[0]
    sizes = (nx, ny)
    counts = tuple(lax.axis_size(a) for a in ("gx", "gy", "gz"))
    rows = nx * ny
    nodes = rows * nz
    h_t = ((ch, nodes), BF16)
    e_t = ((3, ch, nodes), BF16)
    p_t = ((ch, nodes), F32)
    sx_t = ((ch, ny * nz), F32)
    sy_t = ((ch, nx * nz), F32)
    sz_t = ((ch, LANES), F32)
    h, e, w, p, sxe, sxo = call(
        functools.partial(first_kernel, sizes),
        (features, edge_state, multiplicity, edge_in, edge_out, edge_bias),
        (h_t, e_t, ((3, rows, nz), F32), p_t, sx_t, sx_t),
        (pltpu.VMEM((3, ch, nodes), BF16), pltpu.VMEM((ch * rows, nz), F32)),
    )
    for layer in range(layers):
        rxe, rxo = exchange((sxe, sxo), "gx")
        sye, syo = call(
            functools.partial(y_faces, sizes, counts[0], counts[1]), (p, rxe, rxo), (sy_t, sy_t)
        )
        rye, ryo = exchange((sye, syo), "gy")
        (sz,) = call(
            functools.partial(z_faces, sizes, counts[0], counts[1]),
            (p, rxe, rxo, rye, ryo),
            (sz_t,),
        )
        rze, rzo = exchange((sz, sz), "gz")
        got = (rxe, rxo, rye, ryo, rze, rzo)
        if layer + 1 < layers:
            last = layer + 2 == layers
            res = call(
                functools.partial(middle_kernel, sizes, counts, layer, last),
                (h, e, w, p, *got, node_in, node_out, node_bias, edge_in, edge_out, edge_bias),
                (h_t, p_t, sx_t, sx_t) if last else (h_t, e_t, p_t, sx_t, sx_t),
            )
            if last:
                h, p, sxe, sxo = res
            else:
                h, e, p, sxe, sxo = res
        else:
            (out,) = call(
                functools.partial(last_kernel, sizes, counts, layer),
                (h, p, *got, node_in, node_out, node_bias),
                ((features.shape, BF16),),
                (pltpu.VMEM((ch * rows, nz), F32),),
            )
    return out


def solution(mesh):
    placed = (
        P(None, "gx", "gy", "gz"),
        P(None, None, "gx", "gy", "gz"),
        P("gx", "gy", "gz"),
        P(),
        P(),
        P(),
        P(),
        P(),
        P(),
    )
    return jax.shard_map(
        on_device, mesh=mesh, in_specs=placed, out_specs=P(None, "gx", "gy", "gz"), check_vma=False
    )
```

time: 168 us -> 97.2 us (0.58)
  the two profiles are of different devices: /device:TPU:232 before, /device:TPU:32 now
where the time goes in v1:
time: 97.2 us; the launch traced here: 96.9 us
  waiting for transfers between devices  32.1 us (33%)
  starting transfers between devices  31.1 us (32%)
  Pallas kernels  28.1 us (29%)
  local copies, waits for them, and re-layouts  5.59 us (6%)
    ppermute x9, waiting for transfers between devices, exchange(): got_odd = lax.ppermute(odd, axis, swap_pairs(count, 1))  29.4 us
    pallas_call x10, Pallas kernels, call(): pl.pallas_call(body, out_shape=[jax.ShapeDtypeStruct(s, d) for s, d in ou...  28.1 us
    ppermute x9, starting transfers between devices, exchange(): got_odd = lax.ppermute(odd, axis, swap_pairs(count, 1))  23.9 us
    ppermute x9, starting transfers between devices, exchange(): got_even = lax.ppermute(even, axis, swap_pairs(count, 0))  7.18 us
    unnamed x36, local copies, waits for them, and re-layouts  5.59 us
    ppermute x9, waiting for transfers between devices, exchange(): got_even = lax.ppermute(even, axis, swap_pairs(count, 0))  2.63 us
  transfers between devices with their start and end apart: 18, of which 13 were waited for; matrix products, arithmetic and copies ran while one was open for 0% of the time, Pallas kernels for 0%

profile of v1, /device:TPU:32, one launch (start us, length us, event | category | flops | bytes accessed | tf_op | source)
XLA Modules:
  0.0 96.9 jit_solution(11273397276766078458)
XLA Ops:
  0.0 4.3 %shard_map.91 = (bf16[32,3072]{1,0:T(8,128)(2,1)}, bf16[3,32,3072]{2,1,0:T(8,128)(2,1)}, f32[3,24,128]{2,1,0:T(8,128)}, f32[32,3072]{1,0:T(8,128)}, f32[32,1024]{1,0:T(8,128)}, /*index=5*/f32[32,1024]{1,0:T(8,128)}) custom-call(bf16[32,3,8,128]{3,2,1,0:T(8,128)(2,1)} %f_ref.1, bf16[3,32,3,8,128]{4,3,2,1,0:T(8,128)(2,1)} %es_ref.1, s32[3,8,128]{2,1,0:T(8,128)} %m_ref.1, ...), custom_call_target="tpu_custom_call" | custom-call | tf_op jit(solution)/shard_map/pallas_call | solution.py:266
  4.3 3.1 %collective-permute-start.1 = (f32[32,1024]{1,0:T(8,128)}, f32[32,1024]{1,0:T(8,128)S(1)}, u32[]{:S(2)}, u32[]{:S(2)}) collective-permute-start(f32[32,1024]{1,0:T(8,128)} %get-tuple-element.31), channel_id=1, source_target_pairs={{32,64},{64,32},{96,128},{128,96},{160,192},{192,160},{224,0},{0,2... | collective-permute-start | bytes 393224 | tf_op jit(solution)/shard_map/ppermute | solution.py:26
  7.4 2.9 %collective-permute-done.1.rxo = f32[32,1024]{1,0:T(8,128)S(1)} collective-permute-done((f32[32,1024]{1,0:T(8,128)}, f32[32,1024]{1,0:T(8,128)S(1)}, u32[]{:S(2)}, u32[]{:S(2)}) %collective-permute-start.1) | collective-permute-done | bytes 131104 | tf_op jit(solution)/shard_map/ppermute | solution.py:26
  10.3 0.7 copy-done.4
  10.9 1.7 %shard_map.92 = (f32[32,384]{1,0:T(8,128)}, f32[32,384]{1,0:T(8,128)}) custom-call(f32[32,3072]{1,0:T(8,128)} %get-tuple-element.29.p_ref.p_in, f32[32,1024]{1,0:T(8,128)} %copy-done.2, f32[32,1024]{1,0:T(8,128)} %copy-done.4), custom_call_target="tpu_custom_call" | custom-call | tf_op jit(solution)/shard_map/pallas_call | solution.py:266
  12.7 3.3 %collective-permute-start.2 = (f32[32,384]{1,0:T(8,128)}, f32[32,384]{1,0:T(8,128)S(1)}, u32[]{:S(2)}, u32[]{:S(2)}) collective-permute-start(f32[32,384]{1,0:T(8,128)} %get-tuple-element.32), channel_id=1, source_target_pairs={{0,8},{8,0},{16,24},{24,16},{1,9},{9,1},{17,25},{25,17},{2,10},{10... | collective-permute-start | bytes 147464 | tf_op jit(solution)/shard_map/ppermute | solution.py:27
  16.0 3.6 %collective-permute-start.3 = (f32[32,384]{1,0:T(8,128)}, f32[32,384]{1,0:T(8,128)S(1)}, u32[]{:S(2)}, u32[]{:S(2)}) collective-permute-start(f32[32,384]{1,0:T(8,128)} %get-tuple-element.33), channel_id=1, source_target_pairs={{8,16},{16,8},{24,0},{0,24},{9,17},{17,9},{25,1},{1,25},{10,18},{1... | collective-permute-start | bytes 147464 | tf_op jit(solution)/shard_map/ppermute | solution.py:26
  19.5 3.2 %collective-permute-done.3.ryo = f32[32,384]{1,0:T(8,128)S(1)} collective-permute-done((f32[32,384]{1,0:T(8,128)}, f32[32,384]{1,0:T(8,128)S(1)}, u32[]{:S(2)}, u32[]{:S(2)}) %collective-permute-start.3) | collective-permute-done | bytes 49184 | tf_op jit(solution)/shard_map/ppermute | solution.py:26
  22.8 0.6 copy-done.10
  23.4 1.9 %shard_map.93 = f32[32,128]{1,0:T(8,128)} custom-call(f32[32,3072]{1,0:T(8,128)} %get-tuple-element.29.p_ref.p_in, f32[32,1024]{1,0:T(8,128)} %copy-done.2, f32[32,1024]{1,0:T(8,128)} %copy-done.4, f32[32,384]{1,0:T(8,128)} %copy-done.8, f32[32,384]{1,0:T(8,128)} %copy-done.10), custom_call_target="tpu_custom_call" | custom-call | tf_op jit(solution)/shard_map/pallas_call | solution.py:266
  25.3 2.2 %collective-permute-start.5 = (f32[32,128]{1,0:T(8,128)}, f32[32,128]{1,0:T(8,128)S(1)}, u32[]{:S(2)}, u32[]{:S(2)}) collective-permute-start(f32[32,128]{1,0:T(8,128)} %shard_map.93), channel_id=1, source_target_pairs={{1,2},{2,1},{3,4},{4,3},{5,6},{6,5},{7,0},{0,7},{9,10},{10,9},{11,... | collective-permute-start | bytes 49160 | tf_op jit(solution)/shard_map/ppermute | solution.py:26
  27.5 0.7 collective-permute-start.4
  28.3 3.1 %collective-permute-done.5.rzo = f32[32,128]{1,0:T(8,128)S(1)} collective-permute-done((f32[32,128]{1,0:T(8,128)}, f32[32,128]{1,0:T(8,128)S(1)}, u32[]{:S(2)}, u32[]{:S(2)}) %collective-permute-start.5) | collective-permute-done | bytes 16416 | tf_op jit(solution)/shard_map/ppermute | solution.py:26
  31.4 0.1 collective-permute-done.4.rze
  31.5 0.5 copy-done.14
  32.0 0.1 copy-done.16
  32.1 5.2 %shard_map.94 = (bf16[32,3072]{1,0:T(8,128)(2,1)}, bf16[3,32,3072]{2,1,0:T(8,128)(2,1)}, f32[32,3072]{1,0:T(8,128)}, f32[32,1024]{1,0:T(8,128)}, f32[32,1024]{1,0:T(8,128)}) custom-call(bf16[32,3072]{1,0:T(8,128)(2,1)} %get-tuple-element.26.h_in, bf16[3,32,3072]{2,1,0:T(8,128)(2,1)} %get-tuple-element.27.e_in, f32[3,24,128]{2,1,0:T(8,128)} %get-tuple-element.28.w_ref, ...), custom_call_target="tpu_custom_call" | custom-call | tf_op jit(solution)/shard_map/pallas_call | solution.py:266
  37.3 2.7 %collective-permute-start.7 = (f32[32,1024]{1,0:T(8,128)}, f32[32,1024]{1,0:T(8,128)S(1)}, u32[]{:S(2)}, u32[]{:S(2)}) collective-permute-start(f32[32,1024]{1,0:T(8,128)} %get-tuple-element.38), channel_id=1, source_target_pairs={{32,64},{64,32},{96,128},{128,96},{160,192},{192,160},{224,0},{0,2... | collective-permute-start | bytes 393224 | tf_op jit(solution)/shard_map/ppermute | solution.py:26
  39.9 3.2 %collective-permute-done.7.rxo = f32[32,1024]{1,0:T(8,128)S(1)} collective-permute-done((f32[32,1024]{1,0:T(8,128)}, f32[32,1024]{1,0:T(8,128)S(1)}, u32[]{:S(2)}, u32[]{:S(2)}) %collective-permute-start.7) | collective-permute-done | bytes 131104 | tf_op jit(solution)/shard_map/ppermute | solution.py:26
  43.2 0.6 copy-done.5
  43.8 1.8 %shard_map.95 = (f32[32,384]{1,0:T(8,128)}, f32[32,384]{1,0:T(8,128)}) custom-call(f32[32,3072]{1,0:T(8,128)} %get-tuple-element.36.p_ref.p_in, f32[32,1024]{1,0:T(8,128)} %copy-done.3, f32[32,1024]{1,0:T(8,128)} %copy-done.5), custom_call_target="tpu_custom_call" | custom-call | tf_op jit(solution)/shard_map/pallas_call | solution.py:266
  45.6 2.0 %collective-permute-start.8 = (f32[32,384]{1,0:T(8,128)}, f32[32,384]{1,0:T(8,128)S(1)}, u32[]{:S(2)}, u32[]{:S(2)}) collective-permute-start(f32[32,384]{1,0:T(8,128)} %get-tuple-element.39), channel_id=1, source_target_pairs={{0,8},{8,0},{16,24},{24,16},{1,9},{9,1},{17,25},{25,17},{2,10},{10... | collective-permute-start | bytes 147464 | tf_op jit(solution)/shard_map/ppermute | solution.py:27
  47.5 3.7 %collective-permute-start.9 = (f32[32,384]{1,0:T(8,128)}, f32[32,384]{1,0:T(8,128)S(1)}, u32[]{:S(2)}, u32[]{:S(2)}) collective-permute-start(f32[32,384]{1,0:T(8,128)} %get-tuple-element.40), channel_id=1, source_target_pairs={{8,16},{16,8},{24,0},{0,24},{9,17},{17,9},{25,1},{1,25},{10,18},{1... | collective-permute-start | bytes 147464 | tf_op jit(solution)/shard_map/ppermute | solution.py:26
  51.2 3.2 %collective-permute-done.9.ryo = f32[32,384]{1,0:T(8,128)S(1)} collective-permute-done((f32[32,384]{1,0:T(8,128)}, f32[32,384]{1,0:T(8,128)S(1)}, u32[]{:S(2)}, u32[]{:S(2)}) %collective-permute-start.9) | collective-permute-done | bytes 49184 | tf_op jit(solution)/shard_map/ppermute | solution.py:26
  54.4 0.6 copy-done.11
  55.0 1.9 %shard_map.96 = f32[32,128]{1,0:T(8,128)} custom-call(f32[32,3072]{1,0:T(8,128)} %get-tuple-element.36.p_ref.p_in, f32[32,1024]{1,0:T(8,128)} %copy-done.3, f32[32,1024]{1,0:T(8,128)} %copy-done.5, f32[32,384]{1,0:T(8,128)} %copy-done.9, f32[32,384]{1,0:T(8,128)} %copy-done.11), custom_call_target="tpu_custom_call" | custom-call | tf_op jit(solution)/shard_map/pallas_call | solution.py:266
  56.9 2.1 %collective-permute-start.11 = (f32[32,128]{1,0:T(8,128)}, f32[32,128]{1,0:T(8,128)S(1)}, u32[]{:S(2)}, u32[]{:S(2)}) collective-permute-start(f32[32,128]{1,0:T(8,128)} %shard_map.96), channel_id=1, source_target_pairs={{1,2},{2,1},{3,4},{4,3},{5,6},{6,5},{7,0},{0,7},{9,10},{10,9},{11,... | collective-permute-start | bytes 49160 | tf_op jit(solution)/shard_map/ppermute | solution.py:26
  59.1 3.9 %collective-permute-done.11.rzo = f32[32,128]{1,0:T(8,128)S(1)} collective-permute-done((f32[32,128]{1,0:T(8,128)}, f32[32,128]{1,0:T(8,128)S(1)}, u32[]{:S(2)}, u32[]{:S(2)}) %collective-permute-start.11) | collective-permute-done | bytes 16416 | tf_op jit(solution)/shard_map/ppermute | solution.py:26
  63.0 0.6 copy-done.15
  63.6 5.0 %shard_map.97 = (bf16[32,3072]{1,0:T(8,128)(2,1)}, f32[32,3072]{1,0:T(8,128)}, f32[32,1024]{1,0:T(8,128)}, f32[32,1024]{1,0:T(8,128)}) custom-call(bf16[32,3072]{1,0:T(8,128)(2,1)} %get-tuple-element.34.h_in, bf16[3,32,3072]{2,1,0:T(8,128)(2,1)} %get-tuple-element.35.e_in, f32[3,24,128]{2,1,0:T(8,128)} %get-tuple-element.28.w_ref, ...), custom_call_target="tpu_custom_call" | custom-call | tf_op jit(solution)/shard_map/pallas_call | solution.py:266
  68.6 0.2 collective-permute-start.12
  68.8 0.1 collective-permute-start.13
  68.9 1.4 %collective-permute-done.12.rxe = f32[32,1024]{1,0:T(8,128)S(1)} collective-permute-done((f32[32,1024]{1,0:T(8,128)}, f32[32,1024]{1,0:T(8,128)S(1)}, u32[]{:S(2)}, u32[]{:S(2)}) %collective-permute-start.12) | collective-permute-done | bytes 131104 | tf_op jit(solution)/shard_map/ppermute | solution.py:27
  70.3 4.4 %collective-permute-done.13.rxo = f32[32,1024]{1,0:T(8,128)S(1)} collective-permute-done((f32[32,1024]{1,0:T(8,128)}, f32[32,1024]{1,0:T(8,128)S(1)}, u32[]{:S(2)}, u32[]{:S(2)}) %collective-permute-start.13) | collective-permute-done | bytes 131104 | tf_op jit(solution)/shard_map/ppermute | solution.py:26
  74.7 0.6 copy-done.1
  75.3 1.7 %shard_map.98 = (f32[32,384]{1,0:T(8,128)}, f32[32,384]{1,0:T(8,128)}) custom-call(f32[32,3072]{1,0:T(8,128)} %get-tuple-element.42.p_ref.p_in, f32[32,1024]{1,0:T(8,128)} %copy-done, f32[32,1024]{1,0:T(8,128)} %copy-done.1), custom_call_target="tpu_custom_call" | custom-call | tf_op jit(solution)/shard_map/pallas_call | solution.py:266
  77.1 1.0 collective-permute-start.14
  78.0 3.7 %collective-permute-start.15 = (f32[32,384]{1,0:T(8,128)}, f32[32,384]{1,0:T(8,128)S(1)}, u32[]{:S(2)}, u32[]{:S(2)}) collective-permute-start(f32[32,384]{1,0:T(8,128)} %get-tuple-element.46), channel_id=1, source_target_pairs={{8,16},{16,8},{24,0},{0,24},{9,17},{17,9},{25,1},{1,25},{10,18},{1... | collective-permute-start | bytes 147464 | tf_op jit(solution)/shard_map/ppermute | solution.py:26
  81.8 0.5 collective-permute-done.14.rye
  82.3 2.2 %collective-permute-done.15.ryo = f32[32,384]{1,0:T(8,128)S(1)} collective-permute-done((f32[32,384]{1,0:T(8,128)}, f32[32,384]{1,0:T(8,128)S(1)}, u32[]{:S(2)}, u32[]{:S(2)}) %collective-permute-start.15) | collective-permute-done | bytes 49184 | tf_op jit(solution)/shard_map/ppermute | solution.py:26
  84.5 0.6 copy-done.7
  85.1 1.9 %shard_map.99 = f32[32,128]{1,0:T(8,128)} custom-call(f32[32,3072]{1,0:T(8,128)} %get-tuple-element.42.p_ref.p_in, f32[32,1024]{1,0:T(8,128)} %copy-done, f32[32,1024]{1,0:T(8,128)} %copy-done.1, f32[32,384]{1,0:T(8,128)} %copy-done.6, f32[32,384]{1,0:T(8,128)} %copy-done.7), custom_call_target="tpu_custom_call" | custom-call | tf_op jit(solution)/shard_map/pallas_call | solution.py:266
  87.0 2.6 %collective-permute-start.17 = (f32[32,128]{1,0:T(8,128)}, f32[32,128]{1,0:T(8,128)S(1)}, u32[]{:S(2)}, u32[]{:S(2)}) collective-permute-start(f32[32,128]{1,0:T(8,128)} %shard_map.99), channel_id=1, source_target_pairs={{1,2},{2,1},{3,4},{4,3},{5,6},{6,5},{7,0},{0,7},{9,10},{10,9},{11,... | collective-permute-start | bytes 49160 | tf_op jit(solution)/shard_map/ppermute | solution.py:26
  89.6 3.4 %collective-permute-done.17.rzo = f32[32,128]{1,0:T(8,128)S(1)} collective-permute-done((f32[32,128]{1,0:T(8,128)}, f32[32,128]{1,0:T(8,128)S(1)}, u32[]{:S(2)}, u32[]{:S(2)}) %collective-permute-start.17) | collective-permute-done | bytes 16416 | tf_op jit(solution)/shard_map/ppermute | solution.py:26
  93.0 0.5 collective-permute-done.16.rze
  93.6 0.1 copy-done.12
  93.6 0.5 copy-done.13
  94.2 2.7 %shard_map.100 = bf16[32,3,8,128]{3,2,1,0:T(8,128)(2,1)} custom-call(bf16[32,3072]{1,0:T(8,128)(2,1)} %get-tuple-element.41.h_in, f32[32,3072]{1,0:T(8,128)} %get-tuple-element.42.p_ref.p_in, f32[32,1024]{1,0:T(8,128)} %copy-done, f32[32,1024]{1,0:T(8,128)} %copy-done.1, f32[32,384]{1,0:T(8,128)} %copy-done.6, f32[32,384]{1,0:T(8,128)} %copy-done.7, ...), custom_call_target="tpu_custom_call" | custom-call | tf_op jit(solution)/shard_map/pallas_call | solution.py:266
  (34 shorter events, 0.1 us)
Async XLA Ops:
  4.3 3.1 %collective-permute-start = (f32[32,1024]{1,0:T(8,128)}, f32[32,1024]{1,0:T(8,128)S(1)}, u32[]{:S(2)}, u32[]{:S(2)}) collective-permute-start(f32[32,1024]{1,0:T(8,128)} %get-tuple-element.30), channel_id=1, source_target_pairs={{0,32},{32,0},{64,96},{96,64},{128,160},{160,128},{192,224},{224,1... | collective-permute-start | bytes 393224 | tf_op jit(solution)/shard_map/ppermute | solution.py:27
  4.3 6.0 %collective-permute-start.1 = (f32[32,1024]{1,0:T(8,128)}, f32[32,1024]{1,0:T(8,128)S(1)}, u32[]{:S(2)}, u32[]{:S(2)}) collective-permute-start(f32[32,1024]{1,0:T(8,128)} %get-tuple-element.31), channel_id=1, source_target_pairs={{32,64},{64,32},{96,128},{128,96},{160,192},{192,160},{224,0},{0,2... | collective-permute-start | bytes 393224 | tf_op jit(solution)/shard_map/ppermute | solution.py:26
  7.4 2.9 %copy-start.2 = (f32[32,1024]{1,0:T(8,128)}, f32[32,1024]{1,0:T(8,128)S(1)}, u32[]{:S(2)}) copy-start(f32[32,1024]{1,0:T(8,128)S(1)} %collective-permute-done.rxe) | copy-start | bytes 393220
  10.3 0.7 copy-start.4
  12.7 6.9 %collective-permute-start.2 = (f32[32,384]{1,0:T(8,128)}, f32[32,384]{1,0:T(8,128)S(1)}, u32[]{:S(2)}, u32[]{:S(2)}) collective-permute-start(f32[32,384]{1,0:T(8,128)} %get-tuple-element.32), channel_id=1, source_target_pairs={{0,8},{8,0},{16,24},{24,16},{1,9},{9,1},{17,25},{25,17},{2,10},{10... | collective-permute-start | bytes 147464 | tf_op jit(solution)/shard_map/ppermute | solution.py:27
  16.0 6.8 %collective-permute-start.3 = (f32[32,384]{1,0:T(8,128)}, f32[32,384]{1,0:T(8,128)S(1)}, u32[]{:S(2)}, u32[]{:S(2)}) collective-permute-start(f32[32,384]{1,0:T(8,128)} %get-tuple-element.33), channel_id=1, source_target_pairs={{8,16},{16,8},{24,0},{0,24},{9,17},{17,9},{25,1},{1,25},{10,18},{1... | collective-permute-start | bytes 147464 | tf_op jit(solution)/shard_map/ppermute | solution.py:26
  19.5 3.2 %copy-start.8 = (f32[32,384]{1,0:T(8,128)}, f32[32,384]{1,0:T(8,128)S(1)}, u32[]{:S(2)}) copy-start(f32[32,384]{1,0:T(8,128)S(1)} %collective-permute-done.2.rye) | copy-start | bytes 147460
  22.8 0.6 copy-start.10
  25.3 6.1 %collective-permute-start.5 = (f32[32,128]{1,0:T(8,128)}, f32[32,128]{1,0:T(8,128)S(1)}, u32[]{:S(2)}, u32[]{:S(2)}) collective-permute-start(f32[32,128]{1,0:T(8,128)} %shard_map.93), channel_id=1, source_target_pairs={{1,2},{2,1},{3,4},{4,3},{5,6},{6,5},{7,0},{0,7},{9,10},{10,9},{11,... | collective-permute-start | bytes 49160 | tf_op jit(solution)/shard_map/ppermute | solution.py:26
  27.5 3.9 %collective-permute-start.4 = (f32[32,128]{1,0:T(8,128)}, f32[32,128]{1,0:T(8,128)S(1)}, u32[]{:S(2)}, u32[]{:S(2)}) collective-permute-start(f32[32,128]{1,0:T(8,128)} %shard_map.93), channel_id=1, source_target_pairs={{0,1},{1,0},{2,3},{3,2},{4,5},{5,4},{6,7},{7,6},{8,9},{9,8},{10,11... | collective-permute-start | bytes 49160 | tf_op jit(solution)/shard_map/ppermute | solution.py:27
  31.4 0.6 copy-start.14
  31.5 0.6 copy-start.16
  37.2 2.7 %collective-permute-start.6 = (f32[32,1024]{1,0:T(8,128)}, f32[32,1024]{1,0:T(8,128)S(1)}, u32[]{:S(2)}, u32[]{:S(2)}) collective-permute-start(f32[32,1024]{1,0:T(8,128)} %get-tuple-element.37), channel_id=1, source_target_pairs={{0,32},{32,0},{64,96},{96,64},{128,160},{160,128},{192,224},{224,1... | collective-permute-start | bytes 393224 | tf_op jit(solution)/shard_map/ppermute | solution.py:27
  37.3 5.9 %collective-permute-start.7 = (f32[32,1024]{1,0:T(8,128)}, f32[32,1024]{1,0:T(8,128)S(1)}, u32[]{:S(2)}, u32[]{:S(2)}) collective-permute-start(f32[32,1024]{1,0:T(8,128)} %get-tuple-element.38), channel_id=1, source_target_pairs={{32,64},{64,32},{96,128},{128,96},{160,192},{192,160},{224,0},{0,2... | collective-permute-start | bytes 393224 | tf_op jit(solution)/shard_map/ppermute | solution.py:26
  39.9 3.2 %copy-start.3 = (f32[32,1024]{1,0:T(8,128)}, f32[32,1024]{1,0:T(8,128)S(1)}, u32[]{:S(2)}) copy-start(f32[32,1024]{1,0:T(8,128)S(1)} %collective-permute-done.6.rxe) | copy-start | bytes 393220
  43.2 0.7 copy-start.5
  45.6 5.7 %collective-permute-start.8 = (f32[32,384]{1,0:T(8,128)}, f32[32,384]{1,0:T(8,128)S(1)}, u32[]{:S(2)}, u32[]{:S(2)}) collective-permute-start(f32[32,384]{1,0:T(8,128)} %get-tuple-element.39), channel_id=1, source_target_pairs={{0,8},{8,0},{16,24},{24,16},{1,9},{9,1},{17,25},{25,17},{2,10},{10... | collective-permute-start | bytes 147464 | tf_op jit(solution)/shard_map/ppermute | solution.py:27
  47.5 6.9 %collective-permute-start.9 = (f32[32,384]{1,0:T(8,128)}, f32[32,384]{1,0:T(8,128)S(1)}, u32[]{:S(2)}, u32[]{:S(2)}) collective-permute-start(f32[32,384]{1,0:T(8,128)} %get-tuple-element.40), channel_id=1, source_target_pairs={{8,16},{16,8},{24,0},{0,24},{9,17},{17,9},{25,1},{1,25},{10,18},{1... | collective-permute-start | bytes 147464 | tf_op jit(solution)/shard_map/ppermute | solution.py:26
  51.2 3.2 %copy-start.9 = (f32[32,384]{1,0:T(8,128)}, f32[32,384]{1,0:T(8,128)S(1)}, u32[]{:S(2)}) copy-start(f32[32,384]{1,0:T(8,128)S(1)} %collective-permute-done.8.rye) | copy-start | bytes 147460
  54.4 0.6 copy-start.11
  56.9 6.1 %collective-permute-start.11 = (f32[32,128]{1,0:T(8,128)}, f32[32,128]{1,0:T(8,128)S(1)}, u32[]{:S(2)}, u32[]{:S(2)}) collective-permute-start(f32[32,128]{1,0:T(8,128)} %shard_map.96), channel_id=1, source_target_pairs={{1,2},{2,1},{3,4},{4,3},{5,6},{6,5},{7,0},{0,7},{9,10},{10,9},{11,... | collective-permute-start | bytes 49160 | tf_op jit(solution)/shard_map/ppermute | solution.py:26
  59.1 3.9 %collective-permute-start.10 = (f32[32,128]{1,0:T(8,128)}, f32[32,128]{1,0:T(8,128)S(1)}, u32[]{:S(2)}, u32[]{:S(2)}) collective-permute-start(f32[32,128]{1,0:T(8,128)} %shard_map.96), channel_id=1, source_target_pairs={{0,1},{1,0},{2,3},{3,2},{4,5},{5,4},{6,7},{7,6},{8,9},{9,8},{10,11... | collective-permute-start | bytes 49160 | tf_op jit(solution)/shard_map/ppermute | solution.py:27
  63.0 0.6 copy-start.15
  63.0 0.6 copy-start.17
  68.6 1.8 %collective-permute-start.12 = (f32[32,1024]{1,0:T(8,128)}, f32[32,1024]{1,0:T(8,128)S(1)}, u32[]{:S(2)}, u32[]{:S(2)}) collective-permute-start(f32[32,1024]{1,0:T(8,128)} %get-tuple-element.43), channel_id=1, source_target_pairs={{0,32},{32,0},{64,96},{96,64},{128,160},{160,128},{192,224},{224,1... | collective-permute-start | bytes 393224 | tf_op jit(solution)/shard_map/ppermute | solution.py:27
  68.8 5.9 %collective-permute-start.13 = (f32[32,1024]{1,0:T(8,128)}, f32[32,1024]{1,0:T(8,128)S(1)}, u32[]{:S(2)}, u32[]{:S(2)}) collective-permute-start(f32[32,1024]{1,0:T(8,128)} %get-tuple-element.44), channel_id=1, source_target_pairs={{32,64},{64,32},{96,128},{128,96},{160,192},{192,160},{224,0},{0,2... | collective-permute-start | bytes 393224 | tf_op jit(solution)/shard_map/ppermute | solution.py:26
  70.3 4.4 %copy-start = (f32[32,1024]{1,0:T(8,128)}, f32[32,1024]{1,0:T(8,128)S(1)}, u32[]{:S(2)}) copy-start(f32[32,1024]{1,0:T(8,128)S(1)} %collective-permute-done.12.rxe) | copy-start | bytes 393220
  74.7 0.6 copy-start.1
  77.1 5.2 %collective-permute-start.14 = (f32[32,384]{1,0:T(8,128)}, f32[32,384]{1,0:T(8,128)S(1)}, u32[]{:S(2)}, u32[]{:S(2)}) collective-permute-start(f32[32,384]{1,0:T(8,128)} %get-tuple-element.45), channel_id=1, source_target_pairs={{0,8},{8,0},{16,24},{24,16},{1,9},{9,1},{17,25},{25,17},{2,10},{10... | collective-permute-start | bytes 147464 | tf_op jit(solution)/shard_map/ppermute | solution.py:27
  78.0 6.4 %collective-permute-start.15 = (f32[32,384]{1,0:T(8,128)}, f32[32,384]{1,0:T(8,128)S(1)}, u32[]{:S(2)}, u32[]{:S(2)}) collective-permute-start(f32[32,384]{1,0:T(8,128)} %get-tuple-element.46), channel_id=1, source_target_pairs={{8,16},{16,8},{24,0},{0,24},{9,17},{17,9},{25,1},{1,25},{10,18},{1... | collective-permute-start | bytes 147464 | tf_op jit(solution)/shard_map/ppermute | solution.py:26
  82.3 2.2 %copy-start.6 = (f32[32,384]{1,0:T(8,128)}, f32[32,384]{1,0:T(8,128)S(1)}, u32[]{:S(2)}) copy-start(f32[32,384]{1,0:T(8,128)S(1)} %collective-permute-done.14.rye) | copy-start | bytes 147460
  84.5 0.6 copy-start.7
  87.0 6.1 %collective-permute-start.17 = (f32[32,128]{1,0:T(8,128)}, f32[32,128]{1,0:T(8,128)S(1)}, u32[]{:S(2)}, u32[]{:S(2)}) collective-permute-start(f32[32,128]{1,0:T(8,128)} %shard_map.99), channel_id=1, source_target_pairs={{1,2},{2,1},{3,4},{4,3},{5,6},{6,5},{7,0},{0,7},{9,10},{10,9},{11,... | collective-permute-start | bytes 49160 | tf_op jit(solution)/shard_map/ppermute | solution.py:26
  89.6 3.9 %collective-permute-start.16 = (f32[32,128]{1,0:T(8,128)}, f32[32,128]{1,0:T(8,128)S(1)}, u32[]{:S(2)}, u32[]{:S(2)}) collective-permute-start(f32[32,128]{1,0:T(8,128)} %shard_map.99), channel_id=1, source_target_pairs={{0,1},{1,0},{2,3},{3,2},{4,5},{5,4},{6,7},{7,6},{8,9},{9,8},{10,11... | collective-permute-start | bytes 49160 | tf_op jit(solution)/shard_map/ppermute | solution.py:27
  93.0 0.6 copy-start.12
  93.6 0.6 copy-start.13

commit v2 on v1

--- a/solution.py
+++ b/solution.py
@@ -261,11 +261,13 @@
     out[...] = buf[...].reshape(out.shape).astype(BF16)
 
 
-def call(body, args, outs, scratch=()):
+def call(body, args, outs, scratch=(), first=False, last=False):
     vmem = pl.BlockSpec(memory_space=pltpu.VMEM)
+    if not first:
+        args = [pltpu.with_memory_space_constraint(a, pltpu.VMEM) for a in args]
     return pl.pallas_call(
         body,
-        out_shape=[jax.ShapeDtypeStruct(s, d) for s, d in outs],
+        out_shape=[jax.ShapeDtypeStruct(s, d) if last else pltpu.VMEM(s, d) for s, d in outs],
         in_specs=[vmem] * len(args),
         out_specs=[vmem] * len(outs),
         scratch_shapes=list(scratch),
@@ -292,6 +294,7 @@
         (features, edge_state, multiplicity, edge_in, edge_out, edge_bias),
         (h_t, e_t, ((3, rows, nz), F32), p_t, sx_t, sx_t),
         (pltpu.VMEM((3, ch, nodes), BF16), pltpu.VMEM((ch * rows, nz), F32)),
+        first=True,
     )
     for layer in range(layers):
         rxe, rxo = exchange((sxe, sxo), "gx")
@@ -323,6 +326,7 @@
                 (h, p, *got, node_in, node_out, node_bias),
                 ((features.shape, BF16),),
                 (pltpu.VMEM((ch * rows, nz), F32),),
+                last=True,
             )
     return out
 

time: 97.2 us -> 76.8 us (0.79)
  Pallas kernels: 28.1 us -> 10.7 us
  local copies, waits for them, and re-layouts: 5.59 us -> 3.62 us
    pallas_call x10, Pallas kernels: 28.1 us -> 10.7 us  [call(): pl.pallas_call(body, out_shape=[jax.ShapeDtypeStruct(s, d) if last else p...]
    unnamed x36 -> x20, local copies, waits for them, and re-layouts: 5.59 us -> 3.62 us
  transfers between devices with their start and end apart: 18 -> 18, of which waited for: 13 -> 14; matrix products, arithmetic and copies ran while one was open for 0% -> 0% of each run, Pallas kernels for 0% -> 0%
where the time goes in v2:
time: 76.8 us; the launch traced here: 76.6 us
  waiting for transfers between devices  31.3 us (41%)
  starting transfers between devices  30.8 us (40%)
  Pallas kernels  10.7 us (14%)
  local copies, waits for them, and re-layouts  3.62 us (5%)
    ppermute x9, waiting for transfers between devices, exchange(): got_odd = lax.ppermute(odd, axis, swap_pairs(count, 1))  28.6 us
    ppermute x9, starting transfers between devices, exchange(): got_odd = lax.ppermute(odd, axis, swap_pairs(count, 1))  24 us
    pallas_call x10, Pallas kernels, call(): pl.pallas_call(body, out_shape=[jax.ShapeDtypeStruct(s, d) if last else p...  10.7 us
    ppermute x9, starting transfers between devices, exchange(): got_even = lax.ppermute(even, axis, swap_pairs(count, 0))  6.79 us
    unnamed x20, local copies, waits for them, and re-layouts  3.62 us
    ppermute x9, waiting for transfers between devices, exchange(): got_even = lax.ppermute(even, axis, swap_pairs(count, 0))  2.68 us
  transfers between devices with their start and end apart: 18, of which 14 were waited for; matrix products, arithmetic and copies ran while one was open for 0% of the time, Pallas kernels for 0%

profile of v2, /device:TPU:32, one launch (start us, length us, event | category | flops | bytes accessed | tf_op | source)
XLA Modules:
  0.0 76.6 jit_solution(13610613014946146955)
XLA Ops:
  0.0 3.2 %shard_map.91 = (bf16[32,3072]{1,0:T(8,128)(2,1)S(1)}, bf16[3,32,3072]{2,1,0:T(8,128)(2,1)S(1)}, f32[3,24,128]{2,1,0:T(8,128)S(1)}, f32[32,3072]{1,0:T(8,128)S(1...) custom-call(bf16[32,3,8,128]{3,2,1,0:T(8,128)(2,1)} %f_ref.1, bf16[3,32,3,8,128]{4,3,2,1,0:T(8,128)(2,1)} %es_ref.1, ...), custom_call_target="tpu_custom_call" | custom-call | tf_op jit(solution)/shard_map/pallas_call | solution.py:268
  3.2 0.8 %copy-done.2 = bf16[3,32,3072]{2,1,0:T(8,128)(2,1)} copy-done((bf16[3,32,3072]{2,1,0:T(8,128)(2,1)}, bf16[3,32,3072]{2,1,0:T(8,128)(2,1)S(1)}, u32[]{:S(2)}) %copy-start.2) | copy-done | bytes 589848
  4.0 0.0 collective-permute-start
  4.0 3.1 %collective-permute-start.1 = (f32[32,1024]{1,0:T(8,128)S(1)}, f32[32,1024]{1,0:T(8,128)S(1)}, u32[]{:S(2)}, u32[]{:S(2)}) collective-permute-start(f32[32,1024]{1,0:T(8,128)S(1)} %get-tuple-element.31), channel_id=1, source_target_pairs={{32,64},{64,32},{96,128},{128,96},{160,192},{192,160},{224,0},{0,2... | collective-permute-start | bytes 393224 | tf_op jit(solution)/shard_map/ppermute | solution.py:26
  7.2 0.0 collective-permute-done.rxe
  7.2 2.6 %collective-permute-done.1.rxo = f32[32,1024]{1,0:T(8,128)S(1)} collective-permute-done((f32[32,1024]{1,0:T(8,128)S(1)}, f32[32,1024]{1,0:T(8,128)S(1)}, u32[]{:S(2)}, u32[]{:S(2)}) %collective-permute-start.1) | collective-permute-done | bytes 131104 | tf_op jit(solution)/shard_map/ppermute | solution.py:26
  9.9 3.4 %collective-permute-start.2 = (f32[32,384]{1,0:T(8,128)S(1)}, f32[32,384]{1,0:T(8,128)S(1)}, u32[]{:S(2)}, u32[]{:S(2)}) collective-permute-start(f32[32,384]{1,0:T(8,128)S(1)} %get-tuple-element.32), channel_id=1, source_target_pairs={{0,8},{8,0},{16,24},{24,16},{1,9},{9,1},{17,25},{25,17},{2,10},{10... | collective-permute-start | bytes 147464 | tf_op jit(solution)/shard_map/ppermute | solution.py:27
  13.2 3.7 %collective-permute-start.3 = (f32[32,384]{1,0:T(8,128)S(1)}, f32[32,384]{1,0:T(8,128)S(1)}, u32[]{:S(2)}, u32[]{:S(2)}) collective-permute-start(f32[32,384]{1,0:T(8,128)S(1)} %get-tuple-element.33), channel_id=1, source_target_pairs={{8,16},{16,8},{24,0},{0,24},{9,17},{17,9},{25,1},{1,25},{10,18},{1... | collective-permute-start | bytes 147464 | tf_op jit(solution)/shard_map/ppermute | solution.py:26
  16.9 0.0 collective-permute-done.2.rye
  16.9 3.0 %collective-permute-done.3.ryo = f32[32,384]{1,0:T(8,128)S(1)} collective-permute-done((f32[32,384]{1,0:T(8,128)S(1)}, f32[32,384]{1,0:T(8,128)S(1)}, u32[]{:S(2)}, u32[]{:S(2)}) %collective-permute-start.3) | collective-permute-done | bytes 49184 | tf_op jit(solution)/shard_map/ppermute | solution.py:26
  19.9 0.2 shard_map.93
  20.1 2.9 %collective-permute-start.5 = (f32[32,128]{1,0:T(8,128)S(1)}, f32[32,128]{1,0:T(8,128)S(1)}, u32[]{:S(2)}, u32[]{:S(2)}) collective-permute-start(f32[32,128]{1,0:T(8,128)S(1)} %shard_map.93), channel_id=1, source_target_pairs={{1,2},{2,1},{3,4},{4,3},{5,6},{6,5},{7,0},{0,7},{9,10},{10,9},{11,... | collective-permute-start | bytes 49160 | tf_op jit(solution)/shard_map/ppermute | solution.py:26
  23.0 0.2 collective-permute-start.4
  23.1 2.9 %collective-permute-done.5.rzo = f32[32,128]{1,0:T(8,128)S(1)} collective-permute-done((f32[32,128]{1,0:T(8,128)S(1)}, f32[32,128]{1,0:T(8,128)S(1)}, u32[]{:S(2)}, u32[]{:S(2)}) %collective-permute-start.5) | collective-permute-done | bytes 16416 | tf_op jit(solution)/shard_map/ppermute | solution.py:26
  26.0 0.7 collective-permute-done.4.rze
  26.7 0.6 copy-done.9
  27.4 0.0 copy-done.8
  27.4 1.1 %copy-done.3 = bf16[3,32,3072]{2,1,0:T(8,128)(2,1)S(1)} copy-done((bf16[3,32,3072]{2,1,0:T(8,128)(2,1)S(1)}, bf16[3,32,3072]{2,1,0:T(8,128)(2,1)}, u32[]{:S(2)}) %copy-start.3) | copy-done | bytes 589848
  28.5 2.6 %shard_map.94 = (bf16[32,3072]{1,0:T(8,128)(2,1)S(1)}, bf16[3,32,3072]{2,1,0:T(8,128)(2,1)S(1)}, f32[32,3072]{1,0:T(8,128)S(1)}, f32[32,1024]{1,0:T(8,128)S(1)}, f32[32,1024]{1,0:T(8,128)S(1)}) custom-call(bf16[32,3072]{1,0:T(8,128)(2,1)S(1)} %get-tuple-element.26.h_in, bf16[3,32,3072]{2,1,0:T(8,128)(2,1)S(1)} %copy-done.3, ...), custom_call_target="tpu_custom_call" | custom-call | tf_op jit(solution)/shard_map/pallas_call | solution.py:268
  31.1 0.1 collective-permute-start.6
  31.2 2.0 %collective-permute-start.7 = (f32[32,1024]{1,0:T(8,128)S(1)}, f32[32,1024]{1,0:T(8,128)S(1)}, u32[]{:S(2)}, u32[]{:S(2)}) collective-permute-start(f32[32,1024]{1,0:T(8,128)S(1)} %get-tuple-element.38), channel_id=1, source_target_pairs={{32,64},{64,32},{96,128},{128,96},{160,192},{192,160},{224,0},{0,2... | collective-permute-start | bytes 393224 | tf_op jit(solution)/shard_map/ppermute | solution.py:26
  33.3 0.0 collective-permute-done.6.rxe
  33.3 3.7 %collective-permute-done.7.rxo = f32[32,1024]{1,0:T(8,128)S(1)} collective-permute-done((f32[32,1024]{1,0:T(8,128)S(1)}, f32[32,1024]{1,0:T(8,128)S(1)}, u32[]{:S(2)}, u32[]{:S(2)}) %collective-permute-start.7) | collective-permute-done | bytes 131104 | tf_op jit(solution)/shard_map/ppermute | solution.py:26
  37.0 1.5 %collective-permute-start.8 = (f32[32,384]{1,0:T(8,128)S(1)}, f32[32,384]{1,0:T(8,128)S(1)}, u32[]{:S(2)}, u32[]{:S(2)}) collective-permute-start(f32[32,384]{1,0:T(8,128)S(1)} %get-tuple-element.39), channel_id=1, source_target_pairs={{0,8},{8,0},{16,24},{24,16},{1,9},{9,1},{17,25},{25,17},{2,10},{10... | collective-permute-start | bytes 147464 | tf_op jit(solution)/shard_map/ppermute | solution.py:27
  38.4 3.8 %collective-permute-start.9 = (f32[32,384]{1,0:T(8,128)S(1)}, f32[32,384]{1,0:T(8,128)S(1)}, u32[]{:S(2)}, u32[]{:S(2)}) collective-permute-start(f32[32,384]{1,0:T(8,128)S(1)} %get-tuple-element.40), channel_id=1, source_target_pairs={{8,16},{16,8},{24,0},{0,24},{9,17},{17,9},{25,1},{1,25},{10,18},{1... | collective-permute-start | bytes 147464 | tf_op jit(solution)/shard_map/ppermute | solution.py:26
  42.2 0.0 collective-permute-done.8.rye
  42.2 2.4 %collective-permute-done.9.ryo = f32[32,384]{1,0:T(8,128)S(1)} collective-permute-done((f32[32,384]{1,0:T(8,128)S(1)}, f32[32,384]{1,0:T(8,128)S(1)}, u32[]{:S(2)}, u32[]{:S(2)}) %collective-permute-start.9) | collective-permute-done | bytes 49184 | tf_op jit(solution)/shard_map/ppermute | solution.py:26
  44.6 0.2 shard_map.96
  44.8 2.7 %collective-permute-start.11 = (f32[32,128]{1,0:T(8,128)S(1)}, f32[32,128]{1,0:T(8,128)S(1)}, u32[]{:S(2)}, u32[]{:S(2)}) collective-permute-start(f32[32,128]{1,0:T(8,128)S(1)} %shard_map.96), channel_id=1, source_target_pairs={{1,2},{2,1},{3,4},{4,3},{5,6},{6,5},{7,0},{0,7},{9,10},{10,9},{11,... | collective-permute-start | bytes 49160 | tf_op jit(solution)/shard_map/ppermute | solution.py:26
  47.5 0.0 collective-permute-start.10
  47.5 3.2 %collective-permute-done.11.rzo = f32[32,128]{1,0:T(8,128)S(1)} collective-permute-done((f32[32,128]{1,0:T(8,128)S(1)}, f32[32,128]{1,0:T(8,128)S(1)}, u32[]{:S(2)}, u32[]{:S(2)}) %collective-permute-start.11) | collective-permute-done | bytes 16416 | tf_op jit(solution)/shard_map/ppermute | solution.py:26
  50.7 0.5 collective-permute-done.10.rze
  51.2 1.1 %copy-done.1 = bf16[3,32,3072]{2,1,0:T(8,128)(2,1)S(1)} copy-done((bf16[3,32,3072]{2,1,0:T(8,128)(2,1)S(1)}, bf16[3,32,3072]{2,1,0:T(8,128)(2,1)}, u32[]{:S(2)}) %copy-start.1) | copy-done | bytes 589848
  52.3 2.6 %shard_map.97 = (bf16[32,3072]{1,0:T(8,128)(2,1)S(1)}, f32[32,3072]{1,0:T(8,128)S(1)}, f32[32,1024]{1,0:T(8,128)S(1)}, f32[32,1024]{1,0:T(8,128)S(1)}) custom-call(bf16[32,3072]{1,0:T(8,128)(2,1)S(1)} %get-tuple-element.34.h_in, bf16[3,32,3072]{2,1,0:T(8,128)(2,1)S(1)} %copy-done.1, f32[3,24,128]{2,1,0:T(8,128)S(1)} %get-tuple-element.28.w_ref, ...), custom_call_target="tpu_custom_call" | custom-call | tf_op jit(solution)/shard_map/pallas_call | solution.py:268
  55.0 0.1 collective-permute-start.12
  55.1 0.3 collective-permute-start.13
  55.3 1.1 %collective-permute-done.12.rxe = f32[32,1024]{1,0:T(8,128)S(1)} collective-permute-done((f32[32,1024]{1,0:T(8,128)S(1)}, f32[32,1024]{1,0:T(8,128)S(1)}, u32[]{:S(2)}, u32[]{:S(2)}) %collective-permute-start.12) | collective-permute-done | bytes 131104 | tf_op jit(solution)/shard_map/ppermute | solution.py:27
  56.4 4.5 %collective-permute-done.13.rxo = f32[32,1024]{1,0:T(8,128)S(1)} collective-permute-done((f32[32,1024]{1,0:T(8,128)S(1)}, f32[32,1024]{1,0:T(8,128)S(1)}, u32[]{:S(2)}, u32[]{:S(2)}) %collective-permute-start.13) | collective-permute-done | bytes 131104 | tf_op jit(solution)/shard_map/ppermute | solution.py:26
  61.0 1.6 %collective-permute-start.14 = (f32[32,384]{1,0:T(8,128)S(1)}, f32[32,384]{1,0:T(8,128)S(1)}, u32[]{:S(2)}, u32[]{:S(2)}) collective-permute-start(f32[32,384]{1,0:T(8,128)S(1)} %get-tuple-element.45), channel_id=1, source_target_pairs={{0,8},{8,0},{16,24},{24,16},{1,9},{9,1},{17,25},{25,17},{2,10},{10... | collective-permute-start | bytes 147464 | tf_op jit(solution)/shard_map/ppermute | solution.py:27
  62.6 3.2 %collective-permute-start.15 = (f32[32,384]{1,0:T(8,128)S(1)}, f32[32,384]{1,0:T(8,128)S(1)}, u32[]{:S(2)}, u32[]{:S(2)}) collective-permute-start(f32[32,384]{1,0:T(8,128)S(1)} %get-tuple-element.46), channel_id=1, source_target_pairs={{8,16},{16,8},{24,0},{0,24},{9,17},{17,9},{25,1},{1,25},{10,18},{1... | collective-permute-start | bytes 147464 | tf_op jit(solution)/shard_map/ppermute | solution.py:26
  65.8 0.3 collective-permute-done.14.rye
  66.2 2.6 %collective-permute-done.15.ryo = f32[32,384]{1,0:T(8,128)S(1)} collective-permute-done((f32[32,384]{1,0:T(8,128)S(1)}, f32[32,384]{1,0:T(8,128)S(1)}, u32[]{:S(2)}, u32[]{:S(2)}) %collective-permute-start.15) | collective-permute-done | bytes 49184 | tf_op jit(solution)/shard_map/ppermute | solution.py:26
  68.8 0.2 shard_map.99
  69.0 2.3 %collective-permute-start.17 = (f32[32,128]{1,0:T(8,128)S(1)}, f32[32,128]{1,0:T(8,128)S(1)}, u32[]{:S(2)}, u32[]{:S(2)}) collective-permute-start(f32[32,128]{1,0:T(8,128)S(1)} %shard_map.99), channel_id=1, source_target_pairs={{1,2},{2,1},{3,4},{4,3},{5,6},{6,5},{7,0},{0,7},{9,10},{10,9},{11,... | collective-permute-start | bytes 49160 | tf_op jit(solution)/shard_map/ppermute | solution.py:26
  71.3 0.0 collective-permute-start.16
  71.3 3.6 %collective-permute-done.17.rzo = f32[32,128]{1,0:T(8,128)S(1)} collective-permute-done((f32[32,128]{1,0:T(8,128)S(1)}, f32[32,128]{1,0:T(8,128)S(1)}, u32[]{:S(2)}, u32[]{:S(2)}) %collective-permute-start.17) | collective-permute-done | bytes 16416 | tf_op jit(solution)/shard_map/ppermute | solution.py:26
  74.9 0.1 collective-permute-done.16.rze
  75.0 1.5 %shard_map.100 = bf16[32,3,8,128]{3,2,1,0:T(8,128)(2,1)} custom-call(bf16[32,3072]{1,0:T(8,128)(2,1)S(1)} %get-tuple-element.41.h_in, f32[32,3072]{1,0:T(8,128)S(1)} %get-tuple-element.42.p_ref.p_in, f32[32,1024]{1,0:T(8,128)S(1)} %collective-permute-done.12.rxe, f32[32,1024]{1,0:T(8,128)S(1)} %collective-permute-done.13.rxo, ...), custom_call_target="tpu_custom_call" | custom-call | tf_op jit(solution)/shard_map/pallas_call | solution.py:268
  (18 shorter events, 0.1 us)
Async XLA Ops:
  3.2 0.8 %copy-start.2 = (bf16[3,32,3072]{2,1,0:T(8,128)(2,1)}, bf16[3,32,3072]{2,1,0:T(8,128)(2,1)S(1)}, u32[]{:S(2)}) copy-start(bf16[3,32,3072]{2,1,0:T(8,128)(2,1)S(1)} %get-tuple-element.27.e_in) | copy-start | bytes 1769476
  4.0 3.1 %collective-permute-start = (f32[32,1024]{1,0:T(8,128)S(1)}, f32[32,1024]{1,0:T(8,128)S(1)}, u32[]{:S(2)}, u32[]{:S(2)}) collective-permute-start(f32[32,1024]{1,0:T(8,128)S(1)} %get-tuple-element.30), channel_id=1, source_target_pairs={{0,32},{32,0},{64,96},{96,64},{128,160},{160,128},{192,224},{224,1... | collective-permute-start | bytes 393224 | tf_op jit(solution)/shard_map/ppermute | solution.py:27
  4.0 5.8 %collective-permute-start.1 = (f32[32,1024]{1,0:T(8,128)S(1)}, f32[32,1024]{1,0:T(8,128)S(1)}, u32[]{:S(2)}, u32[]{:S(2)}) collective-permute-start(f32[32,1024]{1,0:T(8,128)S(1)} %get-tuple-element.31), channel_id=1, source_target_pairs={{32,64},{64,32},{96,128},{128,96},{160,192},{192,160},{224,0},{0,2... | collective-permute-start | bytes 393224 | tf_op jit(solution)/shard_map/ppermute | solution.py:26
  9.9 7.0 %collective-permute-start.2 = (f32[32,384]{1,0:T(8,128)S(1)}, f32[32,384]{1,0:T(8,128)S(1)}, u32[]{:S(2)}, u32[]{:S(2)}) collective-permute-start(f32[32,384]{1,0:T(8,128)S(1)} %get-tuple-element.32), channel_id=1, source_target_pairs={{0,8},{8,0},{16,24},{24,16},{1,9},{9,1},{17,25},{25,17},{2,10},{10... | collective-permute-start | bytes 147464 | tf_op jit(solution)/shard_map/ppermute | solution.py:27
  13.2 13.5 %copy-start.4 = (bf16[3,32,96]{2,1,0:T(8,128)(2,1)S(1)}, bf16[3,32,96]{2,1,0:T(8,128)(2,1)}, u32[]{:S(2)}) copy-start(bf16[3,32,96]{2,1,0:T(8,128)(2,1)} %win.5) | copy-start | bytes 55300
  13.2 13.5 %copy-start.5 = (bf16[3,32,32]{2,1,0:T(8,128)(2,1)S(1)}, bf16[3,32,32]{2,1,0:T(8,128)(2,1)}, u32[]{:S(2)}) copy-start(bf16[3,32,32]{2,1,0:T(8,128)(2,1)} %wout.5) | copy-start | bytes 18436
  13.2 13.5 %copy-start.6 = (bf16[3,32,64]{2,1,0:T(8,128)(2,1)S(1)}, bf16[3,32,64]{2,1,0:T(8,128)(2,1)}, u32[]{:S(2)}) copy-start(bf16[3,32,64]{2,1,0:T(8,128)(2,1)} %nin.5) | copy-start | bytes 36868
  13.2 13.5 %copy-start.7 = (bf16[3,32,32]{2,1,0:T(8,128)(2,1)S(1)}, bf16[3,32,32]{2,1,0:T(8,128)(2,1)}, u32[]{:S(2)}) copy-start(bf16[3,32,32]{2,1,0:T(8,128)(2,1)} %nout.5) | copy-start | bytes 18436
  13.2 6.6 %collective-permute-start.3 = (f32[32,384]{1,0:T(8,128)S(1)}, f32[32,384]{1,0:T(8,128)S(1)}, u32[]{:S(2)}, u32[]{:S(2)}) collective-permute-start(f32[32,384]{1,0:T(8,128)S(1)} %get-tuple-element.33), channel_id=1, source_target_pairs={{8,16},{16,8},{24,0},{0,24},{9,17},{17,9},{25,1},{1,25},{10,18},{1... | collective-permute-start | bytes 147464 | tf_op jit(solution)/shard_map/ppermute | solution.py:26
  20.1 5.9 %collective-permute-start.5 = (f32[32,128]{1,0:T(8,128)S(1)}, f32[32,128]{1,0:T(8,128)S(1)}, u32[]{:S(2)}, u32[]{:S(2)}) collective-permute-start(f32[32,128]{1,0:T(8,128)S(1)} %shard_map.93), channel_id=1, source_target_pairs={{1,2},{2,1},{3,4},{4,3},{5,6},{6,5},{7,0},{0,7},{9,10},{10,9},{11,... | collective-permute-start | bytes 49160 | tf_op jit(solution)/shard_map/ppermute | solution.py:26
  23.0 3.7 %collective-permute-start.4 = (f32[32,128]{1,0:T(8,128)S(1)}, f32[32,128]{1,0:T(8,128)S(1)}, u32[]{:S(2)}, u32[]{:S(2)}) collective-permute-start(f32[32,128]{1,0:T(8,128)S(1)} %shard_map.93), channel_id=1, source_target_pairs={{0,1},{1,0},{2,3},{3,2},{4,5},{5,4},{6,7},{7,6},{8,9},{9,8},{10,11... | collective-permute-start | bytes 49160 | tf_op jit(solution)/shard_map/ppermute | solution.py:27
  26.7 0.7 copy-start.9
  26.7 0.7 copy-start.8
  27.4 1.1 %copy-start.3 = (bf16[3,32,3072]{2,1,0:T(8,128)(2,1)S(1)}, bf16[3,32,3072]{2,1,0:T(8,128)(2,1)}, u32[]{:S(2)}) copy-start(bf16[3,32,3072]{2,1,0:T(8,128)(2,1)} %copy-done.2) | copy-start | bytes 1769476
  31.1 13.7 %copy-start = (bf16[3,32,3072]{2,1,0:T(8,128)(2,1)}, bf16[3,32,3072]{2,1,0:T(8,128)(2,1)S(1)}, u32[]{:S(2)}) copy-start(bf16[3,32,3072]{2,1,0:T(8,128)(2,1)S(1)} %get-tuple-element.35.e_in) | copy-start | bytes 1769476
  31.1 2.1 %collective-permute-start.6 = (f32[32,1024]{1,0:T(8,128)S(1)}, f32[32,1024]{1,0:T(8,128)S(1)}, u32[]{:S(2)}, u32[]{:S(2)}) collective-permute-start(f32[32,1024]{1,0:T(8,128)S(1)} %get-tuple-element.37), channel_id=1, source_target_pairs={{0,32},{32,0},{64,96},{96,64},{128,160},{160,128},{192,224},{224,1... | collective-permute-start | bytes 393224 | tf_op jit(solution)/shard_map/ppermute | solution.py:27
  31.2 5.7 %collective-permute-start.7 = (f32[32,1024]{1,0:T(8,128)S(1)}, f32[32,1024]{1,0:T(8,128)S(1)}, u32[]{:S(2)}, u32[]{:S(2)}) collective-permute-start(f32[32,1024]{1,0:T(8,128)S(1)} %get-tuple-element.38), channel_id=1, source_target_pairs={{32,64},{64,32},{96,128},{128,96},{160,192},{192,160},{224,0},{0,2... | collective-permute-start | bytes 393224 | tf_op jit(solution)/shard_map/ppermute | solution.py:26
  37.0 5.2 %collective-permute-start.8 = (f32[32,384]{1,0:T(8,128)S(1)}, f32[32,384]{1,0:T(8,128)S(1)}, u32[]{:S(2)}, u32[]{:S(2)}) collective-permute-start(f32[32,384]{1,0:T(8,128)S(1)} %get-tuple-element.39), channel_id=1, source_target_pairs={{0,8},{8,0},{16,24},{24,16},{1,9},{9,1},{17,25},{25,17},{2,10},{10... | collective-permute-start | bytes 147464 | tf_op jit(solution)/shard_map/ppermute | solution.py:27
  38.4 6.2 %collective-permute-start.9 = (f32[32,384]{1,0:T(8,128)S(1)}, f32[32,384]{1,0:T(8,128)S(1)}, u32[]{:S(2)}, u32[]{:S(2)}) collective-permute-start(f32[32,384]{1,0:T(8,128)S(1)} %get-tuple-element.40), channel_id=1, source_target_pairs={{8,16},{16,8},{24,0},{0,24},{9,17},{17,9},{25,1},{1,25},{10,18},{1... | collective-permute-start | bytes 147464 | tf_op jit(solution)/shard_map/ppermute | solution.py:26
  44.8 5.9 %collective-permute-start.11 = (f32[32,128]{1,0:T(8,128)S(1)}, f32[32,128]{1,0:T(8,128)S(1)}, u32[]{:S(2)}, u32[]{:S(2)}) collective-permute-start(f32[32,128]{1,0:T(8,128)S(1)} %shard_map.96), channel_id=1, source_target_pairs={{1,2},{2,1},{3,4},{4,3},{5,6},{6,5},{7,0},{0,7},{9,10},{10,9},{11,... | collective-permute-start | bytes 49160 | tf_op jit(solution)/shard_map/ppermute | solution.py:26
  47.5 3.7 %collective-permute-start.10 = (f32[32,128]{1,0:T(8,128)S(1)}, f32[32,128]{1,0:T(8,128)S(1)}, u32[]{:S(2)}, u32[]{:S(2)}) collective-permute-start(f32[32,128]{1,0:T(8,128)S(1)} %shard_map.96), channel_id=1, source_target_pairs={{0,1},{1,0},{2,3},{3,2},{4,5},{5,4},{6,7},{7,6},{8,9},{9,8},{10,11... | collective-permute-start | bytes 49160 | tf_op jit(solution)/shard_map/ppermute | solution.py:27
  51.2 1.1 %copy-start.1 = (bf16[3,32,3072]{2,1,0:T(8,128)(2,1)S(1)}, bf16[3,32,3072]{2,1,0:T(8,128)(2,1)}, u32[]{:S(2)}) copy-start(bf16[3,32,3072]{2,1,0:T(8,128)(2,1)} %copy-done) | copy-start | bytes 1769476
  55.0 1.4 %collective-permute-start.12 = (f32[32,1024]{1,0:T(8,128)S(1)}, f32[32,1024]{1,0:T(8,128)S(1)}, u32[]{:S(2)}, u32[]{:S(2)}) collective-permute-start(f32[32,1024]{1,0:T(8,128)S(1)} %get-tuple-element.43), channel_id=1, source_target_pairs={{0,32},{32,0},{64,96},{96,64},{128,160},{160,128},{192,224},{224,1... | collective-permute-start | bytes 393224 | tf_op jit(solution)/shard_map/ppermute | solution.py:27
  55.1 5.9 %collective-permute-start.13 = (f32[32,1024]{1,0:T(8,128)S(1)}, f32[32,1024]{1,0:T(8,128)S(1)}, u32[]{:S(2)}, u32[]{:S(2)}) collective-permute-start(f32[32,1024]{1,0:T(8,128)S(1)} %get-tuple-element.44), channel_id=1, source_target_pairs={{32,64},{64,32},{96,128},{128,96},{160,192},{192,160},{224,0},{0,2... | collective-permute-start | bytes 393224 | tf_op jit(solution)/shard_map/ppermute | solution.py:26
  61.0 5.2 %collective-permute-start.14 = (f32[32,384]{1,0:T(8,128)S(1)}, f32[32,384]{1,0:T(8,128)S(1)}, u32[]{:S(2)}, u32[]{:S(2)}) collective-permute-start(f32[32,384]{1,0:T(8,128)S(1)} %get-tuple-element.45), channel_id=1, source_target_pairs={{0,8},{8,0},{16,24},{24,16},{1,9},{9,1},{17,25},{25,17},{2,10},{10... | collective-permute-start | bytes 147464 | tf_op jit(solution)/shard_map/ppermute | solution.py:27
  62.6 6.2 %collective-permute-start.15 = (f32[32,384]{1,0:T(8,128)S(1)}, f32[32,384]{1,0:T(8,128)S(1)}, u32[]{:S(2)}, u32[]{:S(2)}) collective-permute-start(f32[32,384]{1,0:T(8,128)S(1)} %get-tuple-element.46), channel_id=1, source_target_pairs={{8,16},{16,8},{24,0},{0,24},{9,17},{17,9},{25,1},{1,25},{10,18},{1... | collective-permute-start | bytes 147464 | tf_op jit(solution)/shard_map/ppermute | solution.py:26
  69.0 5.9 %collective-permute-start.17 = (f32[32,128]{1,0:T(8,128)S(1)}, f32[32,128]{1,0:T(8,128)S(1)}, u32[]{:S(2)}, u32[]{:S(2)}) collective-permute-start(f32[32,128]{1,0:T(8,128)S(1)} %shard_map.99), channel_id=1, source_target_pairs={{1,2},{2,1},{3,4},{4,3},{5,6},{6,5},{7,0},{0,7},{9,10},{10,9},{11,... | collective-permute-start | bytes 49160 | tf_op jit(solution)/shard_map/ppermute | solution.py:26
  71.3 3.7 %collective-permute-start.16 = (f32[32,128]{1,0:T(8,128)S(1)}, f32[32,128]{1,0:T(8,128)S(1)}, u32[]{:S(2)}, u32[]{:S(2)}) collective-permute-start(f32[32,128]{1,0:T(8,128)S(1)} %shard_map.99), channel_id=1, source_target_pairs={{0,1},{1,0},{2,3},{3,2},{4,5},{5,4},{6,7},{7,6},{8,9},{9,8},{10,11... | collective-permute-start | bytes 49160 | tf_op jit(solution)/shard_map/ppermute | solution.py:27

commit v3 on v1

v3 whole, which is shorter than its diff:
```python
import functools

import jax
import jax.numpy as jnp
from jax import lax
from jax.experimental import pallas as pl
from jax.experimental.pallas import tpu as pltpu
from jax.sharding import PartitionSpec as P

F32 = jnp.float32
BF16 = jnp.bfloat16
LANES = 128
AXES = ("gx", "gy", "gz")


def even_pairs(count):
    return [(i, i ^ 1) for i in range(count)]


def odd_pairs(axis, spare):
    sizes = [lax.axis_size(a) for a in AXES]
    at, other = AXES.index(axis), AXES.index(spare)
    pairs = []
    for i in range(sizes[0]):
        for j in range(sizes[1]):
            for k in range(sizes[2]):
                here = [i, j, k]
                there = list(here)
                if 0 < here[at] < sizes[at] - 1:
                    there[at] = ((here[at] + 1) ^ 1) - 1
                else:
                    there[other] = here[other] ^ 1
                flat = [(v[0] * sizes[1] + v[1]) * sizes[2] + v[2] for v in (here, there)]
                pairs.append(tuple(flat))
    return pairs


def exchange(even, odd, axis, spare):
    got_even = lax.ppermute(even, axis, even_pairs(lax.axis_size(axis)))
    got_odd = lax.ppermute(odd, AXES, odd_pairs(axis, spare))
    return got_even, got_odd


def silu(v):
    return v / (1.0 + jnp.exp(-v))


def column(row):
    width = row.shape[1]
    eye = lax.broadcasted_iota(jnp.int32, (width, width), 0) == lax.broadcasted_iota(
        jnp.int32, (width, width), 1
    )
    return jnp.sum(jnp.where(eye, row, 0.0), axis=1, keepdims=True)


def tile(values, k):
    return values[:, k * LANES : (k + 1) * LANES]


def turn(values, shift):
    shift %= LANES
    return pltpu.roll(values, shift, 1) if shift else values


def place(axis, got_even, got_odd):
    position, count = lax.axis_index(axis), lax.axis_size(axis)
    is_even = position % 2 == 0
    low = jnp.where(is_even, got_odd, got_even)
    high = jnp.where(is_even, got_even, got_odd)
    low = jnp.where(position > 0, low, 0.0)
    high = jnp.where(position < count - 1, high, 0.0)
    return low, high


def lanes_of(rows=32):
    return lax.broadcasted_iota(jnp.int32, (rows, LANES), 1)


def perceptron(w_in, bias, w_out, pieces):
    stacked = jnp.concatenate([p.astype(BF16) for p in pieces], axis=0)
    pre = jnp.dot(w_in, stacked, preferred_element_type=F32) + bias
    return jnp.dot(w_out, silu(pre).astype(BF16), preferred_element_type=F32)


def rim_edges(sizes, h, e, w, w_in, w_out, bias):
    nx, ny = sizes
    lane = lanes_of()
    at, y_at = lane % 4, (lane // 4) % ny
    x_step = 4 * ny
    outer = len(h) == 5
    a, b, d, t = h[:4]
    o = h[4] if outer else jnp.zeros_like(a)
    ahead_z = [
        jnp.where(at < 3, turn(a, -1), 0.0),
        jnp.where(at < 3, turn(b, -1), d),
        jnp.where(at < 2, turn(d, -1), jnp.where(at == 2, o, turn(o, 2))),
        jnp.where(at == 0, a, jnp.where(at < 3, turn(t, -1), 0.0)),
    ]
    if outer:
        ahead_z.append(jnp.where(at == 0, t, jnp.where(at == 3, turn(t, 2), 0.0)))
    ahead_x = [jnp.where(lane < x_step * (nx - 1), turn(v, -x_step), 0.0) for v in h]
    ahead_y = [jnp.where(y_at < ny - 1, turn(v, -4), 0.0) for v in h]
    cur = jnp.concatenate(h, axis=1)
    updated, weighted = [], []
    for k, shifted in enumerate((ahead_x, ahead_y, ahead_z)):
        edge = jnp.concatenate(e[k], axis=1)
        msg = perceptron(w_in, bias, w_out, [cur, jnp.concatenate(shifted, axis=1), edge])
        updated.append(edge + msg)
        weighted.append([tile(msg, i) * w[i][k : k + 1, :] for i in range(len(h))])
    wx, wy, wz = weighted
    wo = wz[4] if outer else jnp.zeros_like(a)
    behind = [
        jnp.where(at == 0, wz[3], turn(wz[0], 1)),
        jnp.where(at == 0, 0.0, turn(wz[1], 1)),
        jnp.where(at == 3, wz[1], jnp.where(at == 0, 0.0, turn(wz[2], 1))),
        jnp.where(at == 0, wo, jnp.where(at == 1, turn(wo, -2), turn(wz[3], 1))),
    ]
    sums = [
        wx[i] + wy[i] + wz[i] + turn(wx[i], x_step) + turn(wy[i], 4) + behind[i] for i in range(4)
    ]
    return updated, sums


def quarters(lane, parts):
    q = lane // 32
    return jnp.where(
        q == 0, parts[0], jnp.where(q == 1, parts[1], jnp.where(q == 2, parts[2], parts[3]))
    )


def rim_x_faces(sums):
    lane = lanes_of()
    low = quarters(lane, [turn(v, 32 * i) for i, v in enumerate(sums)])
    high = quarters(lane, [turn(v, 32 * i - 64) for i, v in enumerate(sums)])
    return low, high


def rim_add_x(sums, low, high):
    q = lanes_of() // 32
    return [
        v
        + jnp.where(q == 0, turn(low, -32 * i), 0.0)
        + jnp.where(q == 2, turn(high, 64 - 32 * i), 0.0)
        for i, v in enumerate(sums)
    ]


def rim_y_faces(sums):
    group = (lanes_of() // 4) % 8
    packed = jnp.zeros_like(sums[0])
    for i, v in enumerate(sums):
        packed = jnp.where(group == i, turn(v, 4 * i), packed)
        packed = jnp.where(group == 4 + i, turn(v, 4 * i - 12), packed)
    return packed


def rim_add_y(sums, low, high):
    group = (lanes_of() // 4) % 8
    return [
        v
        + jnp.where(group == 0, turn(low, -16 - 4 * i), 0.0)
        + jnp.where(group == 7, turn(high, 28 - 4 * i), 0.0)
        for i, v in enumerate(sums)
    ]


def rim_join_z(sums):
    a, b, d, t = sums
    at = lanes_of() % 4
    return [
        a + jnp.where(at == 3, turn(d, 3), 0.0),
        b + jnp.where(at == 0, turn(t, -3), 0.0),
        d + jnp.where(at == 0, turn(a, -3), 0.0),
        t + jnp.where(at == 3, turn(b, 3), 0.0),
    ]


def edge_stage(sizes, last, h_ref, slab_of, w_ref, w_in, w_out, bias, p_ref, done):
    nx, ny = sizes
    lane = lanes_of()
    span = ny * LANES
    zero_tile = jnp.zeros((32, LANES), BF16)
    prev_x = None
    for x in range(nx):
        cur = h_ref[:, x * span : (x + 1) * span]
        ahead_x = h_ref[:, (x + 1) * span : (x + 2) * span] if x + 1 < nx else jnp.zeros_like(cur)
        ahead_y = jnp.concatenate([cur[:, LANES:], zero_tile], axis=1)
        ahead_z = jnp.concatenate(
            [
                jnp.where(lane < LANES - 1, turn(tile(cur, y).astype(F32), -1), 0.0).astype(BF16)
                for y in range(ny)
            ],
            axis=1,
        )
        edges, edges_out = slab_of(x)
        weighted = []
        for d, shifted in enumerate((ahead_x, ahead_y, ahead_z)):
            edge = edges[d, :, x * span : (x + 1) * span]
            msg = perceptron(w_in, bias, w_out, [cur, shifted, edge])
            if not last:
                edges_out[d, :, x * span : (x + 1) * span] = (edge.astype(F32) + msg).astype(BF16)
            weighted.append([tile(msg, y) * w_ref[x * ny + y, d : d + 1, :] for y in range(ny)])
        wx, wy, wz = weighted
        for y in range(ny):
            acc = wx[y] + wy[y] + wz[y] + turn(wz[y], 1)
            if y > 0:
                acc = acc + wy[y - 1]
            if x > 0:
                acc = acc + prev_x[y]
            p_ref[:, (x * ny + y) * LANES : (x * ny + y + 1) * LANES] = acc
        prev_x = wx
        done(x)


def write_x_faces(sizes, p_ref, sums, sxe, sxo):
    nx, ny = sizes
    span = ny * LANES
    low_rim, high_rim = rim_x_faces(sums)
    is_even = lax.axis_index("gx") % 2 == 0
    sxe[:, span:] = jnp.where(is_even, high_rim, low_rim)
    sxo[:, span:] = jnp.where(is_even, low_rim, high_rim)
    low = slice(0, span)
    high = slice((nx - 1) * span, nx * span)

    @pl.when(is_even)
    def _():
        sxe[:, :span] = p_ref[:, high]
        sxo[:, :span] = p_ref[:, low]

    @pl.when(jnp.logical_not(is_even))
    def _():
        sxe[:, :span] = p_ref[:, low]
        sxo[:, :span] = p_ref[:, high]


def unpack_kernel(sizes, f_ref, es_ref, m_ref, h_ref, e_ref, w_ref, own_ref, sze, szo, buf):
    nx, ny = sizes
    rows = nx * ny
    counts = m_ref[...]
    fluid = counts[1, 1:2, 1:2] > 0
    lane = lax.broadcasted_iota(jnp.int32, (ny, LANES), 1)
    sub = lax.broadcasted_iota(jnp.int32, (ny, LANES), 0)
    for x in range(nx):
        here = counts[x]
        shares = []
        for d in range(3):
            if d == 0:
                there = counts[x + 1] if x + 1 < nx else jnp.zeros_like(here)
            elif d == 1:
                there = jnp.where(sub < ny - 1, pltpu.roll(here, ny - 1, 0), 0)
            else:
                there = jnp.where(lane < LANES - 1, pltpu.roll(here, LANES - 1, 1), 0)
            shared = jnp.minimum(here, there)
            share = 1.0 / jnp.maximum(shared, 1).astype(F32)
            shares.append(jnp.where(fluid & (shared > 0), share, 0.0))
        for y in range(ny):
            for d in range(3):
                w_ref[x * ny + y, d : d + 1, :] = shares[d][y : y + 1, :]
            w_ref[x * ny + y, 3:8, :] = jnp.zeros((5, LANES), F32)

    def collect(first, size, row_of):
        group = lanes_of(size) // 4
        found = [jnp.zeros((size, LANES), F32)] * 4
        for k in range(rows):
            turned = turn(row_of(k), 4 * k)
            for i, shift in enumerate((-1, 0, 1, -2)):
                found[i] = jnp.where(group == (k + shift) % 32, turned, found[i])
        for i, shift in enumerate((4, 0, -4, 8)):
            own_ref[i, first : first + size, :] = turn(found[i], shift)

    for field in range(4):
        source = f_ref[...] if field == 0 else es_ref[field - 1]
        buf[field] = source.astype(F32).reshape(buf.shape[1:])

        def row_of(k, field=field):
            t = buf[field, pl.ds(k, 32, stride=rows), :]
            if field == 0:
                h_ref[:, k * LANES : (k + 1) * LANES] = t.astype(BF16)
            else:
                e_ref[field - 1, :, k * LANES : (k + 1) * LANES] = t.astype(BF16)
            return t

        collect(32 * field, 32, row_of)
    collect(128, 8, lambda k: w_ref[k])
    is_even = lax.axis_index("gz") % 2 == 0
    sze[...] = jnp.where(is_even, own_ref[0], own_ref[1])
    szo[...] = jnp.where(is_even, own_ref[1], own_ref[0])


def first_edges(sizes, h_ref, e_ref, w_ref, win, wout, bias, e_out, p_ref, buf, sems):
    span = sizes[1] * LANES

    def copy_of(x):
        part = pl.ds(x * span, span)
        return pltpu.make_async_copy(buf.at[:, :, part], e_out.at[:, :, part], sems.at[x])

    edge_stage(
        sizes, False, h_ref, lambda x: (e_ref, buf), w_ref, win[0], wout[0], column(bias[0:1, :]),
        p_ref, lambda x: copy_of(x).start(),
    )
    for x in range(sizes[0]):
        copy_of(x).wait()


def first_rim(
    sizes, p_ref, own_ref, rze, rzo, win, wout, bias, hr_out, er_out, wr_out, pr_out, sxe, sxo
):
    at = lanes_of(own_ref.shape[1]) % 4
    own_a, own_b, upper, lower = (own_ref[i] for i in range(4))
    prev, nxt = place("gz", rze[...], rzo[...])
    tiles = [
        own_a,
        own_b,
        jnp.where(at == 3, turn(upper, 3), nxt),
        jnp.where(at == 0, turn(lower, -3), prev),
        jnp.where(
            at == 0,
            turn(lower, -2),
            jnp.where(at == 1, upper, jnp.where(at == 2, turn(nxt, -1), turn(prev, 3))),
        ),
    ]
    h = [t[0:32] for t in tiles]
    e = [[t[32 * (d + 1) : 32 * (d + 2)] for t in tiles] for d in range(3)]
    w = [t[128:136] for t in tiles]
    updated, sums = rim_edges(sizes, h, e, w, win[0], wout[0], column(bias[0:1, :]))
    for i in range(4):
        hr_out[:, i * LANES : (i + 1) * LANES] = h[i].astype(BF16)
        wr_out[:, i * LANES : (i + 1) * LANES] = w[i]
    for d in range(3):
        er_out[d] = updated[d][:, : 4 * LANES].astype(BF16)
    write_x_faces(sizes, p_ref, sums, sxe, sxo)
    for i in range(4):
        pr_out[:, i * LANES : (i + 1) * LANES] = sums[i]


def y_faces(sizes, p_ref, pr_ref, rxe, rxo, sye, syo, pr_out):
    nx, ny = sizes
    low_x, high_x = place("gx", rxe[...], rxo[...])
    faces = []
    for y in (0, ny - 1):
        pieces = []
        for x in range(nx):
            t = p_ref[:, (x * ny + y) * LANES : (x * ny + y + 1) * LANES]
            if x == 0:
                t = t + tile(low_x, y)
            if x == nx - 1:
                t = t + tile(high_x, y)
            pieces.append(t)
        faces.append(jnp.concatenate(pieces, axis=1))
    low, high = faces
    sums = rim_add_x([tile(pr_ref, i) for i in range(4)], tile(low_x, ny), tile(high_x, ny))
    packed = rim_y_faces(sums)
    for i in range(4):
        pr_out[:, i * LANES : (i + 1) * LANES] = sums[i]
    is_even = lax.axis_index("gy") % 2 == 0
    sye[:, : nx * LANES] = jnp.where(is_even, high, low)
    syo[:, : nx * LANES] = jnp.where(is_even, low, high)
    sye[:, nx * LANES :] = packed
    syo[:, nx * LANES :] = packed


def node_stage(
    sizes, layer, h_in, p_ref, hr_in, pr_ref, rxe, rxo, rye, ryo, nin, nout, nbias, write
):
    nx, ny = sizes
    low_x, high_x = place("gx", rxe[...], rxo[...])
    low_y, high_y = place("gy", rye[...], ryo[...])
    w_in, w_out = nin[layer], nout[layer]
    b = column(nbias[layer : layer + 1, :])
    sums = rim_add_y([tile(pr_ref, i) for i in range(4)], tile(low_y, nx), tile(high_y, nx))
    rim = rim_join_z(sums)
    cur = hr_in[...]
    rim_h = cur.astype(F32) + perceptron(w_in, b, w_out, [cur, jnp.concatenate(rim, axis=1)])
    for x in range(nx):
        pieces = []
        for y in range(ny):
            t = p_ref[:, (x * ny + y) * LANES : (x * ny + y + 1) * LANES]
            if x == 0:
                t = t + tile(low_x, y)
            if x == nx - 1:
                t = t + tile(high_x, y)
            if y == 0:
                t = t + tile(low_y, x)
            if y == ny - 1:
                t = t + tile(high_y, x)
            pieces.append(t.astype(BF16))
        span = slice(x * ny * LANES, (x + 1) * ny * LANES)
        cur = h_in[:, span]
        res = perceptron(w_in, b, w_out, [cur, jnp.concatenate(pieces, axis=1)])
        write(x, cur.astype(F32) + res)
    return rim_h


def middle_kernel(sizes, layer, last, h_in, p_in, hr_in, er_in, wr_in, pr_in, rxe, rxo, rye, ryo,
                  nin, nout, nbias, win, wout, bias, e_in, w_in, *rest):
    nx, ny = sizes
    span = ny * LANES
    if last:
        h_out, p_out, hr_out, pr_out, sxe, sxo, e_buf, w_buf, sems = rest
        e_out = er_out = e_new = None
    else:
        e_out, h_out, p_out, hr_out, er_out, pr_out, sxe, sxo, e_buf, w_buf, sems, e_new = rest

    def fetch(x):
        part = pl.ds(x * span, span)
        return pltpu.make_async_copy(e_in.at[:, :, part], e_buf.at[:, :, part], sems.at[x])

    def store(x):
        part = pl.ds(x * span, span)
        return pltpu.make_async_copy(e_new.at[:, :, part], e_out.at[:, :, part], sems.at[nx + 1 + x])

    fetch_w = pltpu.make_async_copy(w_in, w_buf, sems.at[nx])
    fetch_w.start()
    for x in range(nx):
        fetch(x).start()

    def write(x, value):
        h_out[:, x * span : (x + 1) * span] = value.astype(BF16)

    rim_h = node_stage(
        sizes, layer, h_in, p_in, hr_in, pr_in, rxe, rxo, rye, ryo, nin, nout, nbias, write
    ).astype(BF16)
    hr_out[...] = rim_h
    layer += 1
    b = column(bias[layer : layer + 1, :])
    updated, sums = rim_edges(
        sizes,
        [tile(rim_h, i).astype(F32) for i in range(4)],
        [[tile(er_in[d], i).astype(F32) for i in range(4)] for d in range(3)],
        [tile(wr_in, i) for i in range(4)],
        win[layer], wout[layer], b,
    )
    for i in range(4):
        pr_out[:, i * LANES : (i + 1) * LANES] = sums[i]
    if not last:
        for d in range(3):
            er_out[d] = updated[d].astype(BF16)
    fetch_w.wait()

    def slab_of(x):
        fetch(x).wait()
        return e_buf, e_new

    edge_stage(
        sizes, last, h_out, slab_of, w_buf, win[layer], wout[layer], b, p_out,
        (lambda x: None) if last else (lambda x: store(x).start()),
    )
    write_x_faces(sizes, p_out, sums, sxe, sxo)
    if not last:
        for x in range(nx):
            store(x).wait()


def last_kernel(
    sizes, layer, h_in, p_in, hr_in, pr_in, rxe, rxo, rye, ryo, nin, nout, nbias, out, res, buf
):
    nx, ny = sizes
    rows = nx * ny

    def write(x, value):
        res[:, x * ny * LANES : (x + 1) * ny * LANES] = value

    rim_h = node_stage(
        sizes, layer, h_in, p_in, hr_in, pr_in, rxe, rxo, rye, ryo, nin, nout, nbias, write
    )
    lane = lanes_of()
    upper = turn(tile(rim_h, 0), -4)
    lower = tile(rim_h, 1)
    for k in range(rows):
        t = res[:, k * LANES : (k + 1) * LANES]
        t = jnp.where(lane < 3, turn(lower, -4 * k), t)
        t = jnp.where(lane >= LANES - 3, turn(upper, -4 * k), t)
        buf[pl.ds(k, 32, stride=rows), :] = t
    out[...] = buf[...].reshape(out.shape).astype(BF16)


def call(body, fast, slow, outs, scratch=(), flops=0):
    vmem = pl.BlockSpec(memory_space=pltpu.VMEM)
    anywhere = pl.BlockSpec(memory_space=pl.ANY)
    fast = [pltpu.with_memory_space_constraint(a, pltpu.VMEM) for a in fast]
    slow_spec = anywhere if fast else vmem
    return pl.pallas_call(
        body,
        out_shape=[
            pltpu.VMEM(s, d) if where == "fast" else jax.ShapeDtypeStruct(s, d)
            for s, d, where in outs
        ],
        in_specs=[vmem] * len(fast) + [slow_spec] * len(slow),
        out_specs=[anywhere if where == "slow" else vmem for _, _, where in outs],
        scratch_shapes=list(scratch),
        cost_estimate=pl.CostEstimate(flops=flops, bytes_accessed=0, transcendentals=0),
    )(*fast, *slow)


def on_device(
    features, edge_state, multiplicity, edge_in, edge_out, edge_bias, node_in, node_out, node_bias
):
    ch, nx, ny, nz = features.shape
    layers = edge_in.shape[0]
    sizes = (nx, ny)
    rows = nx * ny
    nodes = rows * nz
    h_t = ((ch, nodes), BF16, "fast")
    p_t = ((ch, nodes), F32, "fast")
    e_shape = (3, ch, nodes)
    e_t = (e_shape, BF16, "slow")
    w_shape = (rows, 8, nz)
    sx_t = ((ch, (ny + 1) * nz), F32, "fast")
    sy_t = ((ch, (nx + 1) * nz), F32, "fast")
    hr_t = ((ch, 4 * LANES), BF16, "fast")
    er_t = ((3, ch, 4 * LANES), BF16, "fast")
    wr_t = ((8, 4 * LANES), F32, "fast")
    pr_t = ((ch, 4 * LANES), F32, "fast")
    z_rows = 4 * ch + 8
    sz_t = ((z_rows, LANES), F32, "fast")
    e_scratch = pltpu.VMEM(e_shape, BF16)
    work = 2 * 5 * 3 * ch * ch * nodes

    h, e0, w, own, sze, szo = call(
        functools.partial(unpack_kernel, sizes),
        (),
        (features, edge_state, multiplicity),
        (h_t, (e_shape, BF16, "fast"), (w_shape, F32, "fast"), ((4, z_rows, LANES), F32, "fast"),
         sz_t, sz_t),
        (pltpu.VMEM((4, ch * rows, nz), F32),),
    )
    rze, rzo = exchange(sze, szo, "gz", "gx")
    e, p = call(
        functools.partial(first_edges, sizes),
        (h, e0, w, edge_in, edge_out, edge_bias),
        (),
        (e_t, p_t),
        (e_scratch, pltpu.SemaphoreType.DMA((nx,))),
        flops=4 * work,
    )
    hr, er, wr, pr, sxe, sxo = call(
        functools.partial(first_rim, sizes),
        (p, own, rze, rzo, edge_in, edge_out, edge_bias),
        (),
        (hr_t, er_t, wr_t, pr_t, sx_t, sx_t),
    )
    for layer in range(layers):
        rxe, rxo = exchange(sxe, sxo, "gx", "gz")
        sye, syo, pr = call(
            functools.partial(y_faces, sizes), (p, pr, rxe, rxo), (), (sy_t, sy_t, pr_t)
        )
        rye, ryo = exchange(sye, syo, "gy", "gx")
        got = (rxe, rxo, rye, ryo)
        node = (node_in, node_out, node_bias)
        if layer + 1 < layers:
            last = layer + 2 == layers
            outs = (h_t, p_t, hr_t, pr_t, sx_t, sx_t) if last else (
                e_t, h_t, p_t, hr_t, er_t, pr_t, sx_t, sx_t)
            scratch = (e_scratch, pltpu.VMEM(w_shape, F32), pltpu.SemaphoreType.DMA((2 * nx + 1,)))
            res = call(
                functools.partial(middle_kernel, sizes, layer, last),
                (h, p, hr, er, wr, pr, *got, *node, edge_in, edge_out, edge_bias),
                (e, w),
                outs,
                scratch if last else scratch + (e_scratch,),
            )
            if last:
                h, p, hr, pr, sxe, sxo = res
            else:
                e, h, p, hr, er, pr, sxe, sxo = res
        else:
            (out,) = call(
                functools.partial(last_kernel, sizes, layer),
                (h, p, hr, pr, *got, *node),
                (),
                ((features.shape, BF16, "out"),),
                (pltpu.VMEM((ch, nodes), F32), pltpu.VMEM((ch * rows, nz), F32)),
            )
    return out


def solution(mesh):
    placed = (
        P(None, "gx", "gy", "gz"),
        P(None, None, "gx", "gy", "gz"),
        P("gx", "gy", "gz"),
        P(),
        P(),
        P(),
        P(),
        P(),
        P(),
    )
    return jax.shard_map(
        on_device, mesh=mesh, in_specs=placed, out_specs=P(None, "gx", "gy", "gz"), check_vma=False
    )
```

time: 97.2 us -> 63.8 us (0.66)
  the two profiles are of different devices: /device:TPU:32 before, /device:TPU:68 now
where the time goes in v3:
time: 63.8 us; the launch traced here: 63 us
  waiting for transfers between devices  23.3 us (37%)
  starting transfers between devices  20 us (31%)
  Pallas kernels  18.1 us (28%)
  local copies, waits for them, and re-layouts  1.37 us (2%)
    ppermute x7, waiting for transfers between devices, exchange(): got_odd = lax.ppermute(odd, AXES, odd_pairs(axis, spare))  19.2 us
    pallas_call x9, Pallas kernels, call(): pl.pallas_call(body, out_shape=[pltpu.VMEM(s, d) if where == 'fast' else...  18.1 us
    ppermute x7, starting transfers between devices, exchange(): got_odd = lax.ppermute(odd, AXES, odd_pairs(axis, spare))  18 us
    ppermute x7, waiting for transfers between devices, exchange(): got_even = lax.ppermute(even, axis, even_pairs(lax.axis_size(axis)))  4.15 us
    ppermute x7, starting transfers between devices, exchange(): got_even = lax.ppermute(even, axis, even_pairs(lax.axis_size(axis)))  2.04 us
    unnamed x14, local copies, waits for them, and re-layouts  1.37 us
  transfers between devices with their start and end apart: 14, of which 10 were waited for; matrix products, arithmetic and copies ran while one was open for 0% of the time, Pallas kernels for 4%

profile of v3, /device:TPU:68, one launch (start us, length us, event | category | flops | bytes accessed | tf_op | source)
XLA Modules:
  0.0 63.0 jit_solution(11629503908744780695)
XLA Ops:
  0.0 0.0 copy-start.2
  0.0 0.0 copy-start.1
  0.0 2.1 %shard_map.91 = (bf16[32,3072]{1,0:T(8,128)(2,1)S(1)}, bf16[3,32,3072]{2,1,0:T(8,128)(2,1)S(1)}, f32[24,8,128]{2,1,0:T(8,128)S(1)}, f32[4,136,128]{2,1,0:T(8,128...) custom-call(bf16[32,3,8,128]{3,2,1,0:T(8,128)(2,1)} %f_ref.1, bf16[3,32,3,8,128]{4,3,2,1,0:T(8,128)(2,1)} %es_ref.1, ...), custom_call_target="tpu_custom_call" | custom-call | tf_op jit(solution)/shard_map/pallas_call | solution.py:482
  2.2 0.0 copy-start
  2.2 1.3 %collective-permute-start = (f32[136,128]{1,0:T(8,128)S(1)}, f32[136,128]{1,0:T(8,128)S(1)}, u32[]{:S(2)}, u32[]{:S(2)}) collective-permute-start(f32[136,128]{1,0:T(8,128)S(1)} %get-tuple-element.47), channel_id=1, source_target_pairs={{0,1},{1,0},{2,3},{3,2},{4,5},{5,4},{6,7},{7,6},{8,9},{9,8},{10,11... | collective-permute-start | bytes 208904 | tf_op jit(solution)/shard_map/ppermute | solution.py:39
  3.5 0.0 collective-permute-start.1
  3.5 0.0 copy-start.5
  3.5 0.0 copy-done.2
  3.5 0.0 copy-done.1
  3.5 0.7 %copy-done.5 = f32[3,32]{1,0:T(4,128)S(1)} copy-done((f32[3,32]{1,0:T(4,128)S(1)}, f32[3,32]{1,0:T(4,128)}, u32[]{:S(2)}) %copy-start.5) | copy-done | bytes 408
  4.1 2.6 %shard_map.92 = (bf16[3,32,3072]{2,1,0:T(8,128)(2,1)}, f32[32,3072]{1,0:T(8,128)S(1)}) custom-call(bf16[32,3072]{1,0:T(8,128)(2,1)S(1)} %get-tuple-element.42.h_ref.h_in, bf16[3,32,3072]{2,1,0:T(8,128)(2,1)S(1)} %get-tuple-element.43.e_ref, f32[24,8,128]{2,1,0:T(8,128)S(1)} %get-tuple-element.44.w_ref.w_in, bf16[3,32,96]{2,1,0:T(8,128)(2,1)S(1)} %copy-done.1, ...), custom_call_target="tpu_custom_call" | custom-call | flops 377487360 | tf_op jit(solution)/shard_map/pallas_call | solution.py:482
  6.7 0.0 copy-done
  6.7 0.0 collective-permute-done.rze
  6.8 1.0 %collective-permute-done.1.rzo = f32[136,128]{1,0:T(8,128)S(1)} collective-permute-done((f32[136,128]{1,0:T(8,128)S(1)}, f32[136,128]{1,0:T(8,128)S(1)}, u32[]{:S(2)}, u32[]{:S(2)}) %collective-permute-start.1) | collective-permute-done | bytes 69664 | tf_op jit(solution)/shard_map/ppermute | solution.py:40
  7.8 0.9 %shard_map.93 = (bf16[32,512]{1,0:T(8,128)(2,1)S(1)}, bf16[3,32,512]{2,1,0:T(8,128)(2,1)S(1)}, f32[8,512]{1,0:T(8,128)S(1)}, f32[32,512]{1,0:T(8,128)S(1)}, f32[...) custom-call(f32[32,3072]{1,0:T(8,128)S(1)} %get-tuple-element.45.p_ref.p_in, f32[4,136,128]{2,1,0:T(8,128)S(1)} %get-tuple-element.46.own_ref, ...), custom_call_target="tpu_custom_call" | custom-call | tf_op jit(solution)/shard_map/pallas_call | solution.py:482
  8.6 0.1 collective-permute-start.2
  8.7 3.0 %collective-permute-start.3 = (f32[32,1152]{1,0:T(8,128)S(1)}, f32[32,1152]{1,0:T(8,128)S(1)}, u32[]{:S(2)}, u32[]{:S(2)}) collective-permute-start(f32[32,1152]{1,0:T(8,128)S(1)} %get-tuple-element.54), channel_id=1, source_target_pairs={{0,1},{1,0},{2,3},{3,2},{4,5},{5,4},{6,7},{7,6},{8,9},{9,8},{10,11... | collective-permute-start | bytes 442376 | tf_op jit(solution)/shard_map/ppermute | solution.py:40
  11.8 0.0 collective-permute-done.2.rxe
  11.8 3.1 %collective-permute-done.3.rxo = f32[32,1152]{1,0:T(8,128)S(1)} collective-permute-done((f32[32,1152]{1,0:T(8,128)S(1)}, f32[32,1152]{1,0:T(8,128)S(1)}, u32[]{:S(2)}, u32[]{:S(2)}) %collective-permute-start.3) | collective-permute-done | bytes 147488 | tf_op jit(solution)/shard_map/ppermute | solution.py:40
  14.9 0.2 shard_map.94
  15.1 0.1 collective-permute-start.4
  15.2 5.9 %collective-permute-start.5 = (f32[32,512]{1,0:T(8,128)S(1)}, f32[32,512]{1,0:T(8,128)S(1)}, u32[]{:S(2)}, u32[]{:S(2)}) collective-permute-start(f32[32,512]{1,0:T(8,128)S(1)} %get-tuple-element.57), channel_id=1, source_target_pairs={{0,32},{1,33},{2,34},{3,35},{4,36},{5,37},{6,38},{7,39},{8,16},{9,... | collective-permute-start | bytes 196616 | tf_op jit(solution)/shard_map/ppermute | solution.py:40
  21.1 0.0 collective-permute-done.4.rye
  21.1 2.9 %collective-permute-done.5.ryo = f32[32,512]{1,0:T(8,128)S(1)} collective-permute-done((f32[32,512]{1,0:T(8,128)S(1)}, f32[32,512]{1,0:T(8,128)S(1)}, u32[]{:S(2)}, u32[]{:S(2)}) %collective-permute-start.5) | collective-permute-done | bytes 65568 | tf_op jit(solution)/shard_map/ppermute | solution.py:40
  24.0 0.0 copy-done.3
  24.0 0.0 copy-done.4
  24.0 0.7 %copy-done.6 = f32[3,32]{1,0:T(4,128)S(1)} copy-done((f32[3,32]{1,0:T(4,128)S(1)}, f32[3,32]{1,0:T(4,128)}, u32[]{:S(2)}) %copy-start.6) | copy-done | bytes 408
  24.7 5.5 %shard_map.95 = (bf16[3,32,3072]{2,1,0:T(8,128)(2,1)}, bf16[32,3072]{1,0:T(8,128)(2,1)S(1)}, f32[32,3072]{1,0:T(8,128)S(1)}, bf16[32,512]{1,0:T(8,128)(2,1)S(1)}...) custom-call(bf16[32,3072]{1,0:T(8,128)(2,1)S(1)} %get-tuple-element., ...), custom_call_target="tpu_custom_call" | custom-call | tf_op jit(solution)/shard_map/pallas_call | solution.py:482
  30.2 0.1 collective-permute-start.6
  30.3 1.5 %collective-permute-start.7 = (f32[32,1152]{1,0:T(8,128)S(1)}, f32[32,1152]{1,0:T(8,128)S(1)}, u32[]{:S(2)}, u32[]{:S(2)}) collective-permute-start(f32[32,1152]{1,0:T(8,128)S(1)} %get-tuple-element.65), channel_id=1, source_target_pairs={{0,1},{1,0},{2,3},{3,2},{4,5},{5,4},{6,7},{7,6},{8,9},{9,8},{10,11... | collective-permute-start | bytes 442376 | tf_op jit(solution)/shard_map/ppermute | solution.py:40
  31.8 0.0 collective-permute-done.6.rxe
  31.8 3.7 %collective-permute-done.7.rxo = f32[32,1152]{1,0:T(8,128)S(1)} collective-permute-done((f32[32,1152]{1,0:T(8,128)S(1)}, f32[32,1152]{1,0:T(8,128)S(1)}, u32[]{:S(2)}, u32[]{:S(2)}) %collective-permute-start.7) | collective-permute-done | bytes 147488 | tf_op jit(solution)/shard_map/ppermute | solution.py:40
  35.5 0.2 shard_map.96
  35.7 0.1 collective-permute-start.8
  35.8 3.6 %collective-permute-start.9 = (f32[32,512]{1,0:T(8,128)S(1)}, f32[32,512]{1,0:T(8,128)S(1)}, u32[]{:S(2)}, u32[]{:S(2)}) collective-permute-start(f32[32,512]{1,0:T(8,128)S(1)} %get-tuple-element.68), channel_id=1, source_target_pairs={{0,32},{1,33},{2,34},{3,35},{4,36},{5,37},{6,38},{7,39},{8,16},{9,... | collective-permute-start | bytes 196616 | tf_op jit(solution)/shard_map/ppermute | solution.py:40
  39.4 1.6 %collective-permute-done.8.rye = f32[32,512]{1,0:T(8,128)S(1)} collective-permute-done((f32[32,512]{1,0:T(8,128)S(1)}, f32[32,512]{1,0:T(8,128)S(1)}, u32[]{:S(2)}, u32[]{:S(2)}) %collective-permute-start.8) | collective-permute-done | bytes 65568 | tf_op jit(solution)/shard_map/ppermute | solution.py:39
  41.0 2.0 %collective-permute-done.9.ryo = f32[32,512]{1,0:T(8,128)S(1)} collective-permute-done((f32[32,512]{1,0:T(8,128)S(1)}, f32[32,512]{1,0:T(8,128)S(1)}, u32[]{:S(2)}, u32[]{:S(2)}) %collective-permute-start.9) | collective-permute-done | bytes 65568 | tf_op jit(solution)/shard_map/ppermute | solution.py:40
  43.0 4.8 %shard_map.97 = (bf16[32,3072]{1,0:T(8,128)(2,1)S(1)}, f32[32,3072]{1,0:T(8,128)S(1)}, bf16[32,512]{1,0:T(8,128)(2,1)S(1)}, f32[32,512]{1,0:T(8,128)S(1)}, f32[3...) custom-call(bf16[32,3072]{1,0:T(8,128)(2,1)S(1)} %get-tuple-element.59.h_in, f32[32,3072]{1,0:T(8,128)S(1)} %get-tuple-element.60.p_ref.p_in, ...), custom_call_target="tpu_custom_call" | custom-call | tf_op jit(solution)/shard_map/pallas_call | solution.py:482
  47.8 0.3 collective-permute-start.10
  48.1 0.9 %collective-permute-start.11 = (f32[32,1152]{1,0:T(8,128)S(1)}, f32[32,1152]{1,0:T(8,128)S(1)}, u32[]{:S(2)}, u32[]{:S(2)}) collective-permute-start(f32[32,1152]{1,0:T(8,128)S(1)} %get-tuple-element.75), channel_id=1, source_target_pairs={{0,1},{1,0},{2,3},{3,2},{4,5},{5,4},{6,7},{7,6},{8,9},{9,8},{10,11... | collective-permute-start | bytes 442376 | tf_op jit(solution)/shard_map/ppermute | solution.py:40
  49.0 0.5 collective-permute-done.10.rxe
  49.5 3.9 %collective-permute-done.11.rxo = f32[32,1152]{1,0:T(8,128)S(1)} collective-permute-done((f32[32,1152]{1,0:T(8,128)S(1)}, f32[32,1152]{1,0:T(8,128)S(1)}, u32[]{:S(2)}, u32[]{:S(2)}) %collective-permute-start.11) | collective-permute-done | bytes 147488 | tf_op jit(solution)/shard_map/ppermute | solution.py:40
  53.3 0.2 shard_map.98
  53.5 0.1 collective-permute-start.12
  53.6 3.0 %collective-permute-start.13 = (f32[32,512]{1,0:T(8,128)S(1)}, f32[32,512]{1,0:T(8,128)S(1)}, u32[]{:S(2)}, u32[]{:S(2)}) collective-permute-start(f32[32,512]{1,0:T(8,128)S(1)} %get-tuple-element.78), channel_id=1, source_target_pairs={{0,32},{1,33},{2,34},{3,35},{4,36},{5,37},{6,38},{7,39},{8,16},{9,... | collective-permute-start | bytes 196616 | tf_op jit(solution)/shard_map/ppermute | solution.py:40
  56.6 2.1 %collective-permute-done.12.rye = f32[32,512]{1,0:T(8,128)S(1)} collective-permute-done((f32[32,512]{1,0:T(8,128)S(1)}, f32[32,512]{1,0:T(8,128)S(1)}, u32[]{:S(2)}, u32[]{:S(2)}) %collective-permute-start.12) | collective-permute-done | bytes 65568 | tf_op jit(solution)/shard_map/ppermute | solution.py:39
  58.8 2.6 %collective-permute-done.13.ryo = f32[32,512]{1,0:T(8,128)S(1)} collective-permute-done((f32[32,512]{1,0:T(8,128)S(1)}, f32[32,512]{1,0:T(8,128)S(1)}, u32[]{:S(2)}, u32[]{:S(2)}) %collective-permute-start.13) | collective-permute-done | bytes 65568 | tf_op jit(solution)/shard_map/ppermute | solution.py:40
  61.3 1.6 %shard_map.99 = bf16[32,3,8,128]{3,2,1,0:T(8,128)(2,1)} custom-call(bf16[32,3072]{1,0:T(8,128)(2,1)S(1)} %get-tuple-element.70.h_in, f32[32,3072]{1,0:T(8,128)S(1)} %get-tuple-element.71.p_ref.p_in, bf16[32,512]{1,0:T(8,128)(2,1)S(1)} %get-tuple-element.72.hr_in, f32[32,512]{1,0:T(8,128)S(1)} %get-tuple-element.76.pr_in, ...), custom_call_target="tpu_custom_call" | custom-call | tf_op jit(solution)/shard_map/pallas_call | solution.py:482
  (3 shorter events, 0.0 us)
Async XLA Ops:
  0.0 3.5 %copy-start.2 = (bf16[3,32,32]{2,1,0:T(8,128)(2,1)S(1)}, bf16[3,32,32]{2,1,0:T(8,128)(2,1)}, u32[]{:S(2)}) copy-start(bf16[3,32,32]{2,1,0:T(8,128)(2,1)} %wout.7) | copy-start | bytes 18436
  0.0 3.5 %copy-start.1 = (bf16[3,32,96]{2,1,0:T(8,128)(2,1)S(1)}, bf16[3,32,96]{2,1,0:T(8,128)(2,1)}, u32[]{:S(2)}) copy-start(bf16[3,32,96]{2,1,0:T(8,128)(2,1)} %win.7) | copy-start | bytes 55300
  2.2 4.6 %copy-start = (f32[24,8,128]{2,1,0:T(8,128)}, f32[24,8,128]{2,1,0:T(8,128)S(1)}, u32[]{:S(2)}) copy-start(f32[24,8,128]{2,1,0:T(8,128)S(1)} %get-tuple-element.44.w_ref.w_in) | copy-start | bytes 294916
  2.2 4.6 %collective-permute-start = (f32[136,128]{1,0:T(8,128)S(1)}, f32[136,128]{1,0:T(8,128)S(1)}, u32[]{:S(2)}, u32[]{:S(2)}) collective-permute-start(f32[136,128]{1,0:T(8,128)S(1)} %get-tuple-element.47), channel_id=1, source_target_pairs={{0,1},{1,0},{2,3},{3,2},{4,5},{5,4},{6,7},{7,6},{8,9},{9,8},{10,11... | collective-permute-start | bytes 208904 | tf_op jit(solution)/shard_map/ppermute | solution.py:39
  3.5 4.3 %collective-permute-start.1 = (f32[136,128]{1,0:T(8,128)S(1)}, f32[136,128]{1,0:T(8,128)S(1)}, u32[]{:S(2)}, u32[]{:S(2)}) collective-permute-start(f32[136,128]{1,0:T(8,128)S(1)} %get-tuple-element.48), channel_id=1, source_target_pairs={{0,32},{1,2},{2,1},{3,4},{4,3},{5,6},{6,5},{7,39},{8,40},{9,10},{1... | collective-permute-start | bytes 208904 | tf_op jit(solution)/shard_map/ppermute | solution.py:40
  3.5 0.7 %copy-start.5 = (f32[3,32]{1,0:T(4,128)S(1)}, f32[3,32]{1,0:T(4,128)}, u32[]{:S(2)}) copy-start(f32[3,32]{1,0:T(4,128)} %bias.7) | copy-start | bytes 1156
  8.6 3.1 %collective-permute-start.2 = (f32[32,1152]{1,0:T(8,128)S(1)}, f32[32,1152]{1,0:T(8,128)S(1)}, u32[]{:S(2)}, u32[]{:S(2)}) collective-permute-start(f32[32,1152]{1,0:T(8,128)S(1)} %get-tuple-element.53), channel_id=1, source_target_pairs={{0,32},{32,0},{64,96},{96,64},{128,160},{160,128},{192,224},{224,1... | collective-permute-start | bytes 442376 | tf_op jit(solution)/shard_map/ppermute | solution.py:39
  8.7 6.1 %collective-permute-start.3 = (f32[32,1152]{1,0:T(8,128)S(1)}, f32[32,1152]{1,0:T(8,128)S(1)}, u32[]{:S(2)}, u32[]{:S(2)}) collective-permute-start(f32[32,1152]{1,0:T(8,128)S(1)} %get-tuple-element.54), channel_id=1, source_target_pairs={{0,1},{1,0},{2,3},{3,2},{4,5},{5,4},{6,7},{7,6},{8,9},{9,8},{10,11... | collective-permute-start | bytes 442376 | tf_op jit(solution)/shard_map/ppermute | solution.py:40
  14.9 9.1 %copy-start.3 = (bf16[3,32,64]{2,1,0:T(8,128)(2,1)S(1)}, bf16[3,32,64]{2,1,0:T(8,128)(2,1)}, u32[]{:S(2)}) copy-start(bf16[3,32,64]{2,1,0:T(8,128)(2,1)} %nin.5) | copy-start | bytes 36868
  14.9 9.1 %copy-start.4 = (bf16[3,32,32]{2,1,0:T(8,128)(2,1)S(1)}, bf16[3,32,32]{2,1,0:T(8,128)(2,1)}, u32[]{:S(2)}) copy-start(bf16[3,32,32]{2,1,0:T(8,128)(2,1)} %nout.5) | copy-start | bytes 18436
  15.1 6.0 %collective-permute-start.4 = (f32[32,512]{1,0:T(8,128)S(1)}, f32[32,512]{1,0:T(8,128)S(1)}, u32[]{:S(2)}, u32[]{:S(2)}) collective-permute-start(f32[32,512]{1,0:T(8,128)S(1)} %get-tuple-element.56), channel_id=1, source_target_pairs={{0,8},{8,0},{16,24},{24,16},{1,9},{9,1},{17,25},{25,17},{2,10},{10... | collective-permute-start | bytes 196616 | tf_op jit(solution)/shard_map/ppermute | solution.py:39
  15.2 8.8 %collective-permute-start.5 = (f32[32,512]{1,0:T(8,128)S(1)}, f32[32,512]{1,0:T(8,128)S(1)}, u32[]{:S(2)}, u32[]{:S(2)}) collective-permute-start(f32[32,512]{1,0:T(8,128)S(1)} %get-tuple-element.57), channel_id=1, source_target_pairs={{0,32},{1,33},{2,34},{3,35},{4,36},{5,37},{6,38},{7,39},{8,16},{9,... | collective-permute-start | bytes 196616 | tf_op jit(solution)/shard_map/ppermute | solution.py:40
  24.0 0.7 %copy-start.6 = (f32[3,32]{1,0:T(4,128)S(1)}, f32[3,32]{1,0:T(4,128)}, u32[]{:S(2)}) copy-start(f32[3,32]{1,0:T(4,128)} %nbias.5) | copy-start | bytes 1156
  30.2 1.6 %collective-permute-start.6 = (f32[32,1152]{1,0:T(8,128)S(1)}, f32[32,1152]{1,0:T(8,128)S(1)}, u32[]{:S(2)}, u32[]{:S(2)}) collective-permute-start(f32[32,1152]{1,0:T(8,128)S(1)} %get-tuple-element.64), channel_id=1, source_target_pairs={{0,32},{32,0},{64,96},{96,64},{128,160},{160,128},{192,224},{224,1... | collective-permute-start | bytes 442376 | tf_op jit(solution)/shard_map/ppermute | solution.py:39
  30.3 5.2 %collective-permute-start.7 = (f32[32,1152]{1,0:T(8,128)S(1)}, f32[32,1152]{1,0:T(8,128)S(1)}, u32[]{:S(2)}, u32[]{:S(2)}) collective-permute-start(f32[32,1152]{1,0:T(8,128)S(1)} %get-tuple-element.65), channel_id=1, source_target_pairs={{0,1},{1,0},{2,3},{3,2},{4,5},{5,4},{6,7},{7,6},{8,9},{9,8},{10,11... | collective-permute-start | bytes 442376 | tf_op jit(solution)/shard_map/ppermute | solution.py:40
  35.7 5.3 %collective-permute-start.8 = (f32[32,512]{1,0:T(8,128)S(1)}, f32[32,512]{1,0:T(8,128)S(1)}, u32[]{:S(2)}, u32[]{:S(2)}) collective-permute-start(f32[32,512]{1,0:T(8,128)S(1)} %get-tuple-element.67), channel_id=1, source_target_pairs={{0,8},{8,0},{16,24},{24,16},{1,9},{9,1},{17,25},{25,17},{2,10},{10... | collective-permute-start | bytes 196616 | tf_op jit(solution)/shard_map/ppermute | solution.py:39
  35.8 7.2 %collective-permute-start.9 = (f32[32,512]{1,0:T(8,128)S(1)}, f32[32,512]{1,0:T(8,128)S(1)}, u32[]{:S(2)}, u32[]{:S(2)}) collective-permute-start(f32[32,512]{1,0:T(8,128)S(1)} %get-tuple-element.68), channel_id=1, source_target_pairs={{0,32},{1,33},{2,34},{3,35},{4,36},{5,37},{6,38},{7,39},{8,16},{9,... | collective-permute-start | bytes 196616 | tf_op jit(solution)/shard_map/ppermute | solution.py:40
  47.8 1.6 %collective-permute-start.10 = (f32[32,1152]{1,0:T(8,128)S(1)}, f32[32,1152]{1,0:T(8,128)S(1)}, u32[]{:S(2)}, u32[]{:S(2)}) collective-permute-start(f32[32,1152]{1,0:T(8,128)S(1)} %get-tuple-element.74), channel_id=1, source_target_pairs={{0,32},{32,0},{64,96},{96,64},{128,160},{160,128},{192,224},{224,1... | collective-permute-start | bytes 442376 | tf_op jit(solution)/shard_map/ppermute | solution.py:39
  48.1 5.2 %collective-permute-start.11 = (f32[32,1152]{1,0:T(8,128)S(1)}, f32[32,1152]{1,0:T(8,128)S(1)}, u32[]{:S(2)}, u32[]{:S(2)}) collective-permute-start(f32[32,1152]{1,0:T(8,128)S(1)} %get-tuple-element.75), channel_id=1, source_target_pairs={{0,1},{1,0},{2,3},{3,2},{4,5},{5,4},{6,7},{7,6},{8,9},{9,8},{10,11... | collective-permute-start | bytes 442376 | tf_op jit(solution)/shard_map/ppermute | solution.py:40
  53.5 5.3 %collective-permute-start.12 = (f32[32,512]{1,0:T(8,128)S(1)}, f32[32,512]{1,0:T(8,128)S(1)}, u32[]{:S(2)}, u32[]{:S(2)}) collective-permute-start(f32[32,512]{1,0:T(8,128)S(1)} %get-tuple-element.77), channel_id=1, source_target_pairs={{0,8},{8,0},{16,24},{24,16},{1,9},{9,1},{17,25},{25,17},{2,10},{10... | collective-permute-start | bytes 196616 | tf_op jit(solution)/shard_map/ppermute | solution.py:39
  53.6 7.7 %collective-permute-start.13 = (f32[32,512]{1,0:T(8,128)S(1)}, f32[32,512]{1,0:T(8,128)S(1)}, u32[]{:S(2)}, u32[]{:S(2)}) collective-permute-start(f32[32,512]{1,0:T(8,128)S(1)} %get-tuple-element.78), channel_id=1, source_target_pairs={{0,32},{1,33},{2,34},{3,35},{4,36},{5,37},{6,38},{7,39},{8,16},{9,... | collective-permute-start | bytes 196616 | tf_op jit(solution)/shard_map/ppermute | solution.py:40

commit v4 on v3

--- a/solution.py
+++ b/solution.py
@@ -42,7 +42,8 @@
 
 
 def silu(v):
-    return v / (1.0 + jnp.exp(-v))
+    half = 0.5 * v
+    return half + half * jnp.tanh(half)
 
 
 def column(row):
@@ -175,41 +176,55 @@
     ]
 
 
-def edge_stage(sizes, last, h_ref, slab_of, w_ref, w_in, w_out, bias, p_ref, done):
-    nx, ny = sizes
+def span_of(first, count):
+    return slice(first * LANES, (first + count) * LANES)
+
+
+def ahead_along_z(values):
     lane = lanes_of()
-    span = ny * LANES
-    zero_tile = jnp.zeros((32, LANES), BF16)
+    return jnp.concatenate(
+        [
+            jnp.where(lane < LANES - 1, turn(tile(values, k).astype(F32), -1), 0.0).astype(BF16)
+            for k in range(values.shape[1] // LANES)
+        ],
+        axis=1,
+    )
+
+
+def edge_rows(sizes, first, count, last, h_ref, e_in, e_out, w_ref, w_in, w_out, bias, p_ref):
+    nx, ny = sizes
+    whole = first + count == ny
     prev_x = None
     for x in range(nx):
-        cur = h_ref[:, x * span : (x + 1) * span]
-        ahead_x = h_ref[:, (x + 1) * span : (x + 2) * span] if x + 1 < nx else jnp.zeros_like(cur)
-        ahead_y = jnp.concatenate([cur[:, LANES:], zero_tile], axis=1)
-        ahead_z = jnp.concatenate(
-            [
-                jnp.where(lane < LANES - 1, turn(tile(cur, y).astype(F32), -1), 0.0).astype(BF16)
-                for y in range(ny)
-            ],
-            axis=1,
-        )
-        edges, edges_out = slab_of(x)
+        k0 = x * ny + first
+        rows = span_of(k0, count)
+        cur = h_ref[:, rows]
+        ahead_x = h_ref[:, span_of(k0 + ny, count)] if x + 1 < nx else jnp.zeros_like(cur)
+        ahead_y = cur[:, LANES:]
+        if whole:
+            ahead_y = jnp.concatenate([ahead_y, jnp.zeros((32, LANES), BF16)], axis=1)
         weighted = []
-        for d, shifted in enumerate((ahead_x, ahead_y, ahead_z)):
-            edge = edges[d, :, x * span : (x + 1) * span]
-            msg = perceptron(w_in, bias, w_out, [cur, shifted, edge])
+        for d, shifted in enumerate((ahead_x, ahead_y, ahead_along_z(cur))):
+            n = shifted.shape[1]
+            part = slice(k0 * LANES, k0 * LANES + n)
+            edge = e_in[d, :, part]
+            msg = perceptron(w_in, bias, w_out, [cur[:, :n], shifted, edge])
             if not last:
-                edges_out[d, :, x * span : (x + 1) * span] = (edge.astype(F32) + msg).astype(BF16)
-            weighted.append([tile(msg, y) * w_ref[x * ny + y, d : d + 1, :] for y in range(ny)])
+                e_out[d, :, part] = (edge.astype(F32) + msg).astype(BF16)
+            weighted.append(
+                [tile(msg, i) * w_ref[k0 + i, d : d + 1, :] for i in range(n // LANES)]
+            )
         wx, wy, wz = weighted
-        for y in range(ny):
-            acc = wx[y] + wy[y] + wz[y] + turn(wz[y], 1)
-            if y > 0:
-                acc = acc + wy[y - 1]
+        for i in range(count):
+            acc = wx[i] + wz[i] + turn(wz[i], 1)
+            if i < len(wy):
+                acc = acc + wy[i]
+            if i > 0:
+                acc = acc + wy[i - 1]
             if x > 0:
-                acc = acc + prev_x[y]
-            p_ref[:, (x * ny + y) * LANES : (x * ny + y + 1) * LANES] = acc
+                acc = acc + prev_x[i]
+            p_ref[:, span_of(k0 + i, 1)] = acc
         prev_x = wx
-        done(x)
 
 
 def write_x_faces(sizes, p_ref, sums, sxe, sxo):
@@ -233,9 +248,18 @@
         sxo[:, :span] = p_ref[:, high]
 
 
-def unpack_kernel(sizes, f_ref, es_ref, m_ref, h_ref, e_ref, w_ref, own_ref, sze, szo, buf):
+def unpack_kernel(
+    sizes, f_in, es_in, m_in, h_ref, e_ref, w_ref, own_ref, sze, szo, buf, f_ref, es_ref, m_ref, sems
+):
     nx, ny = sizes
     rows = nx * ny
+    fetches = [pltpu.make_async_copy(m_in, m_ref, sems.at[0])]
+    fetches.append(pltpu.make_async_copy(f_in, f_ref, sems.at[1]))
+    for d in range(3):
+        fetches.append(pltpu.make_async_copy(es_in.at[d], es_ref.at[d], sems.at[2 + d]))
+    for fetch in fetches:
+        fetch.start()
+    fetches[0].wait()
     counts = m_ref[...]
     fluid = counts[1, 1:2, 1:2] > 0
     lane = lax.broadcasted_iota(jnp.int32, (ny, LANES), 1)
@@ -269,6 +293,7 @@
             own_ref[i, first : first + size, :] = turn(found[i], shift)
 
     for field in range(4):
+        fetches[1 + field].wait()
         source = f_ref[...] if field == 0 else es_ref[field - 1]
         buf[field] = source.astype(F32).reshape(buf.shape[1:])
 
@@ -287,19 +312,11 @@
     szo[...] = jnp.where(is_even, own_ref[1], own_ref[0])
 
 
-def first_edges(sizes, h_ref, e_ref, w_ref, win, wout, bias, e_out, p_ref, buf, sems):
-    span = sizes[1] * LANES
-
-    def copy_of(x):
-        part = pl.ds(x * span, span)
-        return pltpu.make_async_copy(buf.at[:, :, part], e_out.at[:, :, part], sems.at[x])
-
-    edge_stage(
-        sizes, False, h_ref, lambda x: (e_ref, buf), w_ref, win[0], wout[0], column(bias[0:1, :]),
-        p_ref, lambda x: copy_of(x).start(),
-    )
-    for x in range(sizes[0]):
-        copy_of(x).wait()
+def first_edges(sizes, h_ref, e_ref, w_ref, win, wout, bias, e_out, p_ref):
+    edge_rows(
+        sizes, 0, sizes[1], False, h_ref, e_ref, e_out, w_ref, win[0], wout[0], column(bias[0:1, :]),
+        p_ref,
+    )
 
 
 def first_rim(
@@ -359,135 +376,200 @@
     syo[:, nx * LANES :] = packed
 
 
-def node_stage(
-    sizes, layer, h_in, p_ref, hr_in, pr_ref, rxe, rxo, rye, ryo, nin, nout, nbias, write
-):
-    nx, ny = sizes
-    low_x, high_x = place("gx", rxe[...], rxo[...])
-    low_y, high_y = place("gy", rye[...], ryo[...])
+def incoming(sizes, p_ref, faces_x, faces_y, x, y):
+    nx, ny = sizes
+    t = p_ref[:, span_of(x * ny + y, 1)]
+    if x == 0:
+        t = t + tile(faces_x[0], y)
+    if x == nx - 1:
+        t = t + tile(faces_x[1], y)
+    if y == 0:
+        t = t + tile(faces_y[0], x)
+    if y == ny - 1:
+        t = t + tile(faces_y[1], x)
+    return t.astype(BF16)
+
+
+def inner_nodes(sizes, layer, h_in, p_in, rxe, rxo, nin, nout, nbias, write):
+    nx, ny = sizes
+    faces_x = place("gx", rxe[...], rxo[...])
     w_in, w_out = nin[layer], nout[layer]
     b = column(nbias[layer : layer + 1, :])
-    sums = rim_add_y([tile(pr_ref, i) for i in range(4)], tile(low_y, nx), tile(high_y, nx))
-    rim = rim_join_z(sums)
-    cur = hr_in[...]
-    rim_h = cur.astype(F32) + perceptron(w_in, b, w_out, [cur, jnp.concatenate(rim, axis=1)])
     for x in range(nx):
-        pieces = []
-        for y in range(ny):
-            t = p_ref[:, (x * ny + y) * LANES : (x * ny + y + 1) * LANES]
-            if x == 0:
-                t = t + tile(low_x, y)
-            if x == nx - 1:
-                t = t + tile(high_x, y)
-            if y == 0:
-                t = t + tile(low_y, x)
-            if y == ny - 1:
-                t = t + tile(high_y, x)
-            pieces.append(t.astype(BF16))
-        span = slice(x * ny * LANES, (x + 1) * ny * LANES)
-        cur = h_in[:, span]
+        pieces = [incoming(sizes, p_in, faces_x, None, x, y) for y in range(1, ny - 1)]
+        rows = span_of(x * ny + 1, ny - 2)
+        cur = h_in[:, rows]
         res = perceptron(w_in, b, w_out, [cur, jnp.concatenate(pieces, axis=1)])
-        write(x, cur.astype(F32) + res)
-    return rim_h
-
-
-def middle_kernel(sizes, layer, last, h_in, p_in, hr_in, er_in, wr_in, pr_in, rxe, rxo, rye, ryo,
-                  nin, nout, nbias, win, wout, bias, e_in, w_in, *rest):
-    nx, ny = sizes
-    span = ny * LANES
+        write(rows, cur.astype(F32) + res)
+
+
+def outer_nodes(sizes, layer, h_in, p_in, hr_in, pr_in, rxe, rxo, rye, ryo, nin, nout, nbias):
+    nx, ny = sizes
+    faces_x = place("gx", rxe[...], rxo[...])
+    faces_y = place("gy", rye[...], ryo[...])
+    w_in, w_out = nin[layer], nout[layer]
+    b = column(nbias[layer : layer + 1, :])
+    sums = [tile(pr_in, i) for i in range(4)]
+    rim = rim_join_z(rim_add_y(sums, tile(faces_y[0], nx), tile(faces_y[1], nx)))
+    outer = [(x, y) for x in range(nx) for y in (0, ny - 1)]
+    cur = jnp.concatenate(
+        [hr_in[...]] + [h_in[:, span_of(x * ny + y, 1)] for x, y in outer], axis=1
+    )
+    inc = jnp.concatenate(
+        [t.astype(BF16) for t in rim]
+        + [incoming(sizes, p_in, faces_x, faces_y, x, y) for x, y in outer],
+        axis=1,
+    )
+    new = cur.astype(F32) + perceptron(w_in, b, w_out, [cur, inc])
+    return new[:, : 4 * LANES], new[:, 4 * LANES :]
+
+
+def inner_kernel(
+    sizes, layer, last, h_in, p_in, rxe, rxo, syo, nin, nout, nbias, win, wout, bias, e_in, w_in,
+    h_out, p_out, e_out, w_out, syo_out, sems,
+):
+    ny = sizes[1]
+    fetch_e = pltpu.make_async_copy(e_in, e_out, sems.at[0])
+    fetch_w = pltpu.make_async_copy(w_in, w_out, sems.at[1])
+    fetch_e.start()
+    fetch_w.start()
+    syo_out[...] = syo[...]
+
+    def write(rows, value):
+        h_out[:, rows] = value.astype(BF16)
+
+    inner_nodes(sizes, layer, h_in, p_in, rxe, rxo, nin, nout, nbias, write)
+    layer += 1
+    fetch_e.wait()
+    fetch_w.wait()
+    edge_rows(
+        sizes, 1, ny - 2, last, h_out, e_out, e_out, w_out, win[layer], wout[layer],
+        column(bias[layer : layer + 1, :]), p_out,
+    )
+
+
+def outer_kernel(
+    sizes, layer, last, h_in, p_in, hr_in, er_in, wr_in, pr_in, rxe, rxo, rye, ryo, nin, nout, nbias,
+    win, wout, bias, w_ref, h_new, p_new, e_new, *outs,
+):
+    nx, ny = sizes
     if last:
-        h_out, p_out, hr_out, pr_out, sxe, sxo, e_buf, w_buf, sems = rest
-        e_out = er_out = e_new = None
+        h_out, p_out, hr_out, pr_out, sxe, sxo = outs
     else:
-        e_out, h_out, p_out, hr_out, er_out, pr_out, sxe, sxo, e_buf, w_buf, sems, e_new = rest
-
-    def fetch(x):
-        part = pl.ds(x * span, span)
-        return pltpu.make_async_copy(e_in.at[:, :, part], e_buf.at[:, :, part], sems.at[x])
-
-    def store(x):
-        part = pl.ds(x * span, span)
-        return pltpu.make_async_copy(e_new.at[:, :, part], e_out.at[:, :, part], sems.at[nx + 1 + x])
-
-    fetch_w = pltpu.make_async_copy(w_in, w_buf, sems.at[nx])
-    fetch_w.start()
-    for x in range(nx):
-        fetch(x).start()
-
-    def write(x, value):
-        h_out[:, x * span : (x + 1) * span] = value.astype(BF16)
-
-    rim_h = node_stage(
-        sizes, layer, h_in, p_in, hr_in, pr_in, rxe, rxo, rye, ryo, nin, nout, nbias, write
-    ).astype(BF16)
+        h_out, p_out, e_out, hr_out, er_out, pr_out, sxe, sxo = outs
+    rim_h, edge_h = outer_nodes(
+        sizes, layer, h_in, p_in, hr_in, pr_in, rxe, rxo, rye, ryo, nin, nout, nbias
+    )
+    rim_h, edge_h = rim_h.astype(BF16), edge_h.astype(BF16)
     hr_out[...] = rim_h
+    outer = [(x, y) for x in range(nx) for y in (0, ny - 1)]
+    for i, (x, y) in enumerate(outer):
+        h_out[:, span_of(x * ny + y, 1)] = tile(edge_h, i)
     layer += 1
     b = column(bias[layer : layer + 1, :])
+    w_in, w_out = win[layer], wout[layer]
     updated, sums = rim_edges(
         sizes,
         [tile(rim_h, i).astype(F32) for i in range(4)],
         [[tile(er_in[d], i).astype(F32) for i in range(4)] for d in range(3)],
         [tile(wr_in, i) for i in range(4)],
-        win[layer], wout[layer], b,
+        w_in, w_out, b,
     )
     for i in range(4):
         pr_out[:, i * LANES : (i + 1) * LANES] = sums[i]
     if not last:
         for d in range(3):
             er_out[d] = updated[d].astype(BF16)
-    fetch_w.wait()
-
-    def slab_of(x):
-        fetch(x).wait()
-        return e_buf, e_new
-
-    edge_stage(
-        sizes, last, h_out, slab_of, w_buf, win[layer], wout[layer], b, p_out,
-        (lambda x: None) if last else (lambda x: store(x).start()),
-    )
+    zero = jnp.zeros((32, LANES), BF16)
+    mine = {place_of: tile(edge_h, i) for i, place_of in enumerate(outer)}
+    cross = [(x, y) for x in range(nx) for y in (0, ny - 2, ny - 1)]
+    from_y, to_y = [], []
+    for x, y in cross:
+        from_y.append(mine[x, y] if (x, y) in mine else h_new[:, span_of(x * ny + y, 1)])
+        to_y.append(
+            h_new[:, span_of(x * ny + 1, 1)] if y == 0 else mine[x, ny - 1] if y == ny - 2 else zero
+        )
+    ahead_x = jnp.concatenate([edge_h[:, 2 * LANES :], zero, zero], axis=1)
+    weighted = []
+    for d, (at, cur, ahead) in enumerate((
+        (outer, edge_h, ahead_x),
+        (cross, jnp.concatenate(from_y, axis=1), jnp.concatenate(to_y, axis=1)),
+        (outer, edge_h, ahead_along_z(edge_h)),
+    )):
+        edge = jnp.concatenate([e_new[d, :, span_of(x * ny + y, 1)] for x, y in at], axis=1)
+        msg = perceptron(w_in, b, w_out, [cur, ahead, edge])
+        if not last:
+            value = (edge.astype(F32) + msg).astype(BF16)
+            for i, (x, y) in enumerate(at):
+                e_out[d, :, span_of(x * ny + y, 1)] = tile(value, i)
+        weighted.append(
+            {
+                (x, y): tile(msg, i) * w_ref[x * ny + y, d : d + 1, :]
+                for i, (x, y) in enumerate(at)
+            }
+        )
+    wx, wy, wz = weighted
+    for x in range(nx):
+        for y in (0, ny - 1):
+            acc = wx[x, y] + wz[x, y] + turn(wz[x, y], 1) + wy[x, y]
+            if x > 0:
+                acc = acc + wx[x - 1, y]
+            if y > 0:
+                acc = acc + wy[x, y - 1]
+            p_out[:, span_of(x * ny + y, 1)] = acc
+        for y, add in ((1, wy[x, 0]), (ny - 2, wy[x, ny - 2])):
+            p_out[:, span_of(x * ny + y, 1)] = p_new[:, span_of(x * ny + y, 1)] + add
     write_x_faces(sizes, p_out, sums, sxe, sxo)
-    if not last:
-        for x in range(nx):
-            store(x).wait()
+
+
+def last_inner(sizes, layer, h_in, p_in, rxe, rxo, syo, nin, nout, nbias, res, syo_out):
+    syo_out[...] = syo[...]
+
+    def write(rows, value):
+        res[:, rows] = value
+
+    inner_nodes(sizes, layer, h_in, p_in, rxe, rxo, nin, nout, nbias, write)
 
 
 def last_kernel(
-    sizes, layer, h_in, p_in, hr_in, pr_in, rxe, rxo, rye, ryo, nin, nout, nbias, out, res, buf
+    sizes, layer, h_in, p_in, hr_in, pr_in, rxe, rxo, rye, ryo, nin, nout, nbias, res, out, buf
 ):
     nx, ny = sizes
     rows = nx * ny
-
-    def write(x, value):
-        res[:, x * ny * LANES : (x + 1) * ny * LANES] = value
-
-    rim_h = node_stage(
-        sizes, layer, h_in, p_in, hr_in, pr_in, rxe, rxo, rye, ryo, nin, nout, nbias, write
+    rim_h, edge_h = outer_nodes(
+        sizes, layer, h_in, p_in, hr_in, pr_in, rxe, rxo, rye, ryo, nin, nout, nbias
     )
     lane = lanes_of()
     upper = turn(tile(rim_h, 0), -4)
     lower = tile(rim_h, 1)
     for k in range(rows):
-        t = res[:, k * LANES : (k + 1) * LANES]
+        x, y = divmod(k, ny)
+        inside = 0 < y < ny - 1
+        t = res[:, span_of(k, 1)] if inside else tile(edge_h, 2 * x + (y > 0))
         t = jnp.where(lane < 3, turn(lower, -4 * k), t)
         t = jnp.where(lane >= LANES - 3, turn(upper, -4 * k), t)
         buf[pl.ds(k, 32, stride=rows), :] = t
     out[...] = buf[...].reshape(out.shape).astype(BF16)
 
 
-def call(body, fast, slow, outs, scratch=(), flops=0):
+def call(body, fast, slow, outs, scratch=(), flops=0, aliases=()):
     vmem = pl.BlockSpec(memory_space=pltpu.VMEM)
     anywhere = pl.BlockSpec(memory_space=pl.ANY)
     fast = [pltpu.with_memory_space_constraint(a, pltpu.VMEM) for a in fast]
-    slow_spec = anywhere if fast else vmem
+    if not fast:
+        anywhere = pl.BlockSpec(memory_space=pltpu.HBM)
+        slow = [pltpu.with_memory_space_constraint(a, pltpu.HBM) for a in slow]
     return pl.pallas_call(
         body,
         out_shape=[
             pltpu.VMEM(s, d) if where == "fast" else jax.ShapeDtypeStruct(s, d)
             for s, d, where in outs
         ],
-        in_specs=[vmem] * len(fast) + [slow_spec] * len(slow),
-        out_specs=[anywhere if where == "slow" else vmem for _, _, where in outs],
+        in_specs=[vmem] * len(fast) + [anywhere] * len(slow),
+        out_specs=[vmem] * len(outs),
         scratch_shapes=list(scratch),
+        input_output_aliases=dict(aliases),
+        compiler_params=pltpu.CompilerParams(vmem_limit_bytes=12 * 2**20),
         cost_estimate=pl.CostEstimate(flops=flops, bytes_accessed=0, transcendentals=0),
     )(*fast, *slow)
 
@@ -503,8 +585,8 @@
     h_t = ((ch, nodes), BF16, "fast")
     p_t = ((ch, nodes), F32, "fast")
     e_shape = (3, ch, nodes)
-    e_t = (e_shape, BF16, "slow")
-    w_shape = (rows, 8, nz)
+    e_t = (e_shape, BF16, "fast")
+    w_t = ((rows, 8, nz), F32, "fast")
     sx_t = ((ch, (ny + 1) * nz), F32, "fast")
     sy_t = ((ch, (nx + 1) * nz), F32, "fast")
     hr_t = ((ch, 4 * LANES), BF16, "fast")
@@ -513,63 +595,80 @@
     pr_t = ((ch, 4 * LANES), F32, "fast")
     z_rows = 4 * ch + 8
     sz_t = ((z_rows, LANES), F32, "fast")
-    e_scratch = pltpu.VMEM(e_shape, BF16)
-    work = 2 * 5 * 3 * ch * ch * nodes
+    work = 4 * 2 * 5 * 3 * ch * ch * nodes
 
     h, e0, w, own, sze, szo = call(
         functools.partial(unpack_kernel, sizes),
         (),
         (features, edge_state, multiplicity),
-        (h_t, (e_shape, BF16, "fast"), (w_shape, F32, "fast"), ((4, z_rows, LANES), F32, "fast"),
-         sz_t, sz_t),
-        (pltpu.VMEM((4, ch * rows, nz), F32),),
+        (h_t, e_t, w_t, ((4, z_rows, LANES), F32, "fast"), sz_t, sz_t),
+        (
+            pltpu.VMEM((4, ch * rows, nz), F32),
+            pltpu.VMEM(features.shape, BF16),
+            pltpu.VMEM(edge_state.shape, BF16),
+            pltpu.VMEM(multiplicity.shape, jnp.int32),
+            pltpu.SemaphoreType.DMA((5,)),
+        ),
     )
     rze, rzo = exchange(sze, szo, "gz", "gx")
+    edge = (edge_in, edge_out, edge_bias)
+    node = (node_in, node_out, node_bias)
     e, p = call(
-        functools.partial(first_edges, sizes),
-        (h, e0, w, edge_in, edge_out, edge_bias),
-        (),
-        (e_t, p_t),
-        (e_scratch, pltpu.SemaphoreType.DMA((nx,))),
-        flops=4 * work,
+        functools.partial(first_edges, sizes), (h, e0, w, *edge), (), (e_t, p_t), flops=work
     )
     hr, er, wr, pr, sxe, sxo = call(
         functools.partial(first_rim, sizes),
-        (p, own, rze, rzo, edge_in, edge_out, edge_bias),
+        (p, own, rze, rzo, *edge),
         (),
         (hr_t, er_t, wr_t, pr_t, sx_t, sx_t),
     )
     for layer in range(layers):
-        rxe, rxo = exchange(sxe, sxo, "gx", "gz")
+        got_x = exchange(sxe, sxo, "gx", "gz")
         sye, syo, pr = call(
-            functools.partial(y_faces, sizes), (p, pr, rxe, rxo), (), (sy_t, sy_t, pr_t)
+            functools.partial(y_faces, sizes), (p, pr, *got_x), (), (sy_t, sy_t, pr_t)
         )
-        rye, ryo = exchange(sye, syo, "gy", "gx")
-        got = (rxe, rxo, rye, ryo)
-        node = (node_in, node_out, node_bias)
+        even = lax.ppermute(sye, "gy", even_pairs(lax.axis_size("gy")))
         if layer + 1 < layers:
             last = layer + 2 == layers
-            outs = (h_t, p_t, hr_t, pr_t, sx_t, sx_t) if last else (
-                e_t, h_t, p_t, hr_t, er_t, pr_t, sx_t, sx_t)
-            scratch = (e_scratch, pltpu.VMEM(w_shape, F32), pltpu.SemaphoreType.DMA((2 * nx + 1,)))
-            res = call(
-                functools.partial(middle_kernel, sizes, layer, last),
-                (h, p, hr, er, wr, pr, *got, *node, edge_in, edge_out, edge_bias),
+            h_new, p_new, e_new, w_new, syo = call(
+                functools.partial(inner_kernel, sizes, layer, last),
+                (h, p, *got_x, syo, *node, *edge),
                 (e, w),
-                outs,
-                scratch if last else scratch + (e_scratch,),
+                (h_t, p_t, e_t, w_t, sy_t),
+                (pltpu.SemaphoreType.DMA((2,)),),
+                flops=work,
+            )
+        else:
+            res, syo = call(
+                functools.partial(last_inner, sizes, layer),
+                (h, p, *got_x, syo, *node),
+                (),
+                (((ch, nodes), F32, "fast"), sy_t),
+                flops=work,
+            )
+        got = (*got_x, even, lax.ppermute(syo, AXES, odd_pairs("gy", "gx")))
+        if layer + 1 < layers:
+            outs = (hr_t, pr_t, sx_t, sx_t) if last else (e_t, hr_t, er_t, pr_t, sx_t, sx_t)
+            args = (h, p, hr, er, wr, pr, *got, *node, *edge, w_new, h_new, p_new, e_new)
+            n = len(args)
+            moved = call(
+                functools.partial(outer_kernel, sizes, layer, last),
+                args,
+                (),
+                (h_t, p_t, *outs),
+                aliases=((n - 3, 0), (n - 2, 1)) + (() if last else ((n - 1, 2),)),
             )
             if last:
-                h, p, hr, pr, sxe, sxo = res
+                h, p, hr, pr, sxe, sxo = moved
             else:
-                e, h, p, hr, er, pr, sxe, sxo = res
+                h, p, e, hr, er, pr, sxe, sxo = moved
         else:
             (out,) = call(
                 functools.partial(last_kernel, sizes, layer),
-                (h, p, hr, pr, *got, *node),
+                (h, p, hr, pr, *got, *node, res),
                 (),
                 ((features.shape, BF16, "out"),),
-                (pltpu.VMEM((ch, nodes), F32), pltpu.VMEM((ch * rows, nz), F32)),
+                (pltpu.VMEM((ch * rows, nz), F32),),
             )
     return out
 

time: 63.8 us -> 61 us (0.956)
  Pallas kernels: 18.1 us -> 15.8 us
  waiting for transfers between devices: 23.3 us -> 24 us
    ppermute x0 -> x6, starting transfers between devices: none -> 12.1 us  [the longest x3 11.8 us: on_device(): got = (*got_x, even, lax.ppermute(syo, AXES, odd_pairs('gy', 'gx')))]
    ppermute x7 -> x4, starting transfers between devices: 18 us -> 5.99 us  [exchange(): got_odd = lax.ppermute(odd, AXES, odd_pairs(axis, spare))]
    ppermute x0 -> x6, waiting for transfers between devices: none -> 11.6 us  [the longest x3 9.81 us: on_device(): got = (*got_x, even, lax.ppermute(syo, AXES, odd_pairs('gy', 'gx')))]
    ppermute x7 -> x4, waiting for transfers between devices: 19.2 us -> 11.8 us  [exchange(): got_odd = lax.ppermute(odd, AXES, odd_pairs(axis, spare))]
    ppermute x7 -> x4, waiting for transfers between devices: 4.15 us -> 0.58 us  [exchange(): got_even = lax.ppermute(even, axis, even_pairs(lax.axis_size(axis)))]
    pallas_call x9 -> x12, Pallas kernels: 18.1 us -> 15.8 us  [call(): pl.pallas_call(body, out_shape=[pltpu.VMEM(s, d) if where == 'fast' else...]
    ppermute x7 -> x4, starting transfers between devices: 2.04 us -> 1.56 us  [exchange(): got_even = lax.ppermute(even, axis, even_pairs(lax.axis_size(axis)))]
    unnamed x14 -> x12, local copies, waits for them, and re-layouts: 1.37 us -> 1.26 us
  transfers between devices with their start and end apart: 14 -> 14, of which waited for: 10 -> 9; matrix products, arithmetic and copies ran while one was open for 0% -> 0% of each run, Pallas kernels for 4% -> 12%
where the time goes in v4:
time: 61 us; the launch traced here: 60.8 us
  waiting for transfers between devices  24 us (39%)
  starting transfers between devices  19.6 us (32%)
  Pallas kernels  15.8 us (26%)
  local copies, waits for them, and re-layouts  1.26 us (2%)
    pallas_call x12, Pallas kernels, call(): pl.pallas_call(body, out_shape=[pltpu.VMEM(s, d) if where == 'fast' else...  15.8 us
    ppermute x4, waiting for transfers between devices, exchange(): got_odd = lax.ppermute(odd, AXES, odd_pairs(axis, spare))  11.8 us
    ppermute x3, starting transfers between devices, on_device(): got = (*got_x, even, lax.ppermute(syo, AXES, odd_pairs('gy', 'gx')))  11.8 us
    ppermute x3, waiting for transfers between devices, on_device(): got = (*got_x, even, lax.ppermute(syo, AXES, odd_pairs('gy', 'gx')))  9.81 us
    ppermute x4, starting transfers between devices, exchange(): got_odd = lax.ppermute(odd, AXES, odd_pairs(axis, spare))  5.99 us
    ppermute x3, waiting for transfers between devices, on_device(): even = lax.ppermute(sye, 'gy', even_pairs(lax.axis_size('gy')))  1.76 us
    ppermute x4, starting transfers between devices, exchange(): got_even = lax.ppermute(even, axis, even_pairs(lax.axis_size(axis)))  1.56 us
    unnamed x12, local copies, waits for them, and re-layouts  1.26 us
  transfers between devices with their start and end apart: 14, of which 9 were waited for; matrix products, arithmetic and copies ran while one was open for 0% of the time, Pallas kernels for 12%

profile of v4, /device:TPU:68, one launch (start us, length us, event | category | flops | bytes accessed | tf_op | source)
XLA Modules:
  0.0 60.8 jit_solution(6157022301559400540)
XLA Ops:
  0.0 0.0 copy-start.1
  0.0 2.1 %shard_map.91 = (bf16[32,3072]{1,0:T(8,128)(2,1)S(1)}, bf16[3,32,3072]{2,1,0:T(8,128)(2,1)S(1)}, f32[24,8,128]{2,1,0:T(8,128)S(1)}, f32[4,136,128]{2,1,0:T(8,128...) custom-call(bf16[32,3,8,128]{3,2,1,0:T(8,128)(2,1)} %f_in.1, bf16[3,32,3,8,128]{4,3,2,1,0:T(8,128)(2,1)} %es_in.1, ...), custom_call_target="tpu_custom_call" | custom-call | tf_op jit(solution)/shard_map/pallas_call | solution.py:562
  2.1 1.3 %collective-permute-start = (f32[136,128]{1,0:T(8,128)S(1)}, f32[136,128]{1,0:T(8,128)S(1)}, u32[]{:S(2)}, u32[]{:S(2)}) collective-permute-start(f32[136,128]{1,0:T(8,128)S(1)} %get-tuple-element.59), channel_id=1, source_target_pairs={{0,1},{1,0},{2,3},{3,2},{4,5},{5,4},{6,7},{7,6},{8,9},{9,8},{10,11... | collective-permute-start | bytes 208904 | tf_op jit(solution)/shard_map/ppermute | solution.py:39
  3.4 0.0 collective-permute-start.1
  3.4 0.0 copy-done.1
  3.4 0.0 copy-done
  3.4 0.7 %copy-done.4 = f32[3,32]{1,0:T(4,128)S(1)} copy-done((f32[3,32]{1,0:T(4,128)S(1)}, f32[3,32]{1,0:T(4,128)}, u32[]{:S(2)}) %copy-start.4) | copy-done | bytes 408
  4.1 1.8 %shard_map.92 = (bf16[3,32,3072]{2,1,0:T(8,128)(2,1)S(1)}, f32[32,3072]{1,0:T(8,128)S(1)}) custom-call(bf16[32,3072]{1,0:T(8,128)(2,1)S(1)} %get-tuple-element.54.h_ref.h_in, bf16[3,32,3072]{2,1,0:T(8,128)(2,1)S(1)} %get-tuple-element.55.e_ref, f32[24,8,128]{2,1,0:T(8,128)S(1)} %get-tuple-element.56.w_ref.w_in, bf16[3,32,96]{2,1,0:T(8,128)(2,1)S(1)} %copy-done, ...), custom_call_target="tpu_custom_call" | custom-call | flops 377487360 | tf_op jit(solution)/shard_map/pallas_call | solution.py:562
  6.0 0.6 collective-permute-done.rze
  6.5 1.2 %collective-permute-done.1.rzo = f32[136,128]{1,0:T(8,128)S(1)} collective-permute-done((f32[136,128]{1,0:T(8,128)S(1)}, f32[136,128]{1,0:T(8,128)S(1)}, u32[]{:S(2)}, u32[]{:S(2)}) %collective-permute-start.1) | collective-permute-done | bytes 69664 | tf_op jit(solution)/shard_map/ppermute | solution.py:40
  7.7 0.9 %shard_map.93 = (bf16[32,512]{1,0:T(8,128)(2,1)S(1)}, bf16[3,32,512]{2,1,0:T(8,128)(2,1)S(1)}, f32[8,512]{1,0:T(8,128)S(1)}, f32[32,512]{1,0:T(8,128)S(1)}, f32[...) custom-call(f32[32,3072]{1,0:T(8,128)S(1)} %get-tuple-element.57.p_ref.p_in, f32[4,136,128]{2,1,0:T(8,128)S(1)} %get-tuple-element.58.own_ref, ...), custom_call_target="tpu_custom_call" | custom-call | tf_op jit(solution)/shard_map/pallas_call | solution.py:562
  8.6 0.1 collective-permute-start.2
  8.7 3.0 %collective-permute-start.3 = (f32[32,1152]{1,0:T(8,128)S(1)}, f32[32,1152]{1,0:T(8,128)S(1)}, u32[]{:S(2)}, u32[]{:S(2)}) collective-permute-start(f32[32,1152]{1,0:T(8,128)S(1)} %get-tuple-element.66), channel_id=1, source_target_pairs={{0,1},{1,0},{2,3},{3,2},{4,5},{5,4},{6,7},{7,6},{8,9},{9,8},{10,11... | collective-permute-start | bytes 442376 | tf_op jit(solution)/shard_map/ppermute | solution.py:40
  11.7 0.0 collective-permute-done.2.rxe
  11.7 3.1 %collective-permute-done.3.rxo = f32[32,1152]{1,0:T(8,128)S(1)} collective-permute-done((f32[32,1152]{1,0:T(8,128)S(1)}, f32[32,1152]{1,0:T(8,128)S(1)}, u32[]{:S(2)}, u32[]{:S(2)}) %collective-permute-start.3) | collective-permute-done | bytes 147488 | tf_op jit(solution)/shard_map/ppermute | solution.py:40
  14.9 0.2 shard_map.94
  15.0 0.0 copy-start.5
  15.1 0.1 collective-permute-start.4
  15.2 0.4 copy-done.2
  15.6 0.0 copy-done.3
  15.6 0.1 copy-done.5
  15.7 2.5 %shard_map.95 = (bf16[32,3072]{1,0:T(8,128)(2,1)S(1)}, f32[32,3072]{1,0:T(8,128)S(1)}, bf16[3,32,3072]{2,1,0:T(8,128)(2,1)S(1)}, f32[24,8,128]{2,1,0:T(8,128)S(1)}, f32[32,512]{1,0:T(8,128)S(1)}) custom-call(bf16[32,3072]{1,0:T(8,128)(2,1)S(1)} %get-tuple-element.54.h_ref.h_in, f32[32,3072]{1,0:T(8,128)S(1)} %get-tuple-element.57.p_ref.p_in, ...), custom_call_target="tpu_custom_call" | custom-call | flops 377487360 | tf_op jit(solution)/shard_map/pallas_call | solution.py:562
  18.3 5.5 %collective-permute-start.5 = (f32[32,512]{1,0:T(8,128)S(1)}, f32[32,512]{1,0:T(8,128)S(1)}, u32[]{:S(2)}, u32[]{:S(2)}) collective-permute-start(f32[32,512]{1,0:T(8,128)S(1)} %get-tuple-element.71), channel_id=1, source_target_pairs={{0,32},{1,33},{2,34},{3,35},{4,36},{5,37},{6,38},{7,39},{8,16},{9,... | collective-permute-start | bytes 196616 | tf_op jit(solution)/shard_map/ppermute | solution.py:649
  23.7 0.0 collective-permute-done.4.rye
  23.7 2.9 %collective-permute-done.5.ryo = f32[32,512]{1,0:T(8,128)S(1)} collective-permute-done((f32[32,512]{1,0:T(8,128)S(1)}, f32[32,512]{1,0:T(8,128)S(1)}, u32[]{:S(2)}, u32[]{:S(2)}) %collective-permute-start.5) | collective-permute-done | bytes 65568 | tf_op jit(solution)/shard_map/ppermute | solution.py:649
  26.7 1.7 %shard_map.96 = (bf16[32,3072]{1,0:T(8,128)(2,1)S(1)}, f32[32,3072]{1,0:T(8,128)S(1)}, bf16[3,32,3072]{2,1,0:T(8,128)(2,1)S(1)}, bf16[32,512]{1,0:T(8,128)(2,1)S...) custom-call(bf16[32,3072]{1,0:T(8,128)(2,1)S(1)} %get-tuple-element., ...), custom_call_target="tpu_custom_call", output_to_operand_aliasing={{0}: (17, {}), {1}: (18, {}), {2}: (19, {})} | custom-call | tf_op jit(solution)/shard_map/pallas_call | solution.py:562
  28.4 0.1 collective-permute-start.6
  28.5 1.6 %collective-permute-start.7 = (f32[32,1152]{1,0:T(8,128)S(1)}, f32[32,1152]{1,0:T(8,128)S(1)}, u32[]{:S(2)}, u32[]{:S(2)}) collective-permute-start(f32[32,1152]{1,0:T(8,128)S(1)} %get-tuple-element.82), channel_id=1, source_target_pairs={{0,1},{1,0},{2,3},{3,2},{4,5},{5,4},{6,7},{7,6},{8,9},{9,8},{10,11... | collective-permute-start | bytes 442376 | tf_op jit(solution)/shard_map/ppermute | solution.py:40
  30.1 0.0 collective-permute-done.6.rxe
  30.1 3.6 %collective-permute-done.7.rxo = f32[32,1152]{1,0:T(8,128)S(1)} collective-permute-done((f32[32,1152]{1,0:T(8,128)S(1)}, f32[32,1152]{1,0:T(8,128)S(1)}, u32[]{:S(2)}, u32[]{:S(2)}) %collective-permute-start.7) | collective-permute-done | bytes 147488 | tf_op jit(solution)/shard_map/ppermute | solution.py:40
  33.7 0.2 shard_map.97
  33.9 0.1 collective-permute-start.8
  34.0 2.6 %shard_map.98 = (bf16[32,3072]{1,0:T(8,128)(2,1)S(1)}, f32[32,3072]{1,0:T(8,128)S(1)}, bf16[3,32,3072]{2,1,0:T(8,128)(2,1)S(1)}, f32[24,8,128]{2,1,0:T(8,128)S(1)}, f32[32,512]{1,0:T(8,128)S(1)}) custom-call(bf16[32,3072]{1,0:T(8,128)(2,1)S(1)} %get-tuple-element.76.h_in, f32[32,3072]{1,0:T(8,128)S(1)} %get-tuple-element.77.p_ref.p_in, ...), custom_call_target="tpu_custom_call" | custom-call | flops 377487360 | tf_op jit(solution)/shard_map/pallas_call | solution.py:562
  36.5 3.5 %collective-permute-start.9 = (f32[32,512]{1,0:T(8,128)S(1)}, f32[32,512]{1,0:T(8,128)S(1)}, u32[]{:S(2)}, u32[]{:S(2)}) collective-permute-start(f32[32,512]{1,0:T(8,128)S(1)} %get-tuple-element.87), channel_id=1, source_target_pairs={{0,32},{1,33},{2,34},{3,35},{4,36},{5,37},{6,38},{7,39},{8,16},{9,... | collective-permute-start | bytes 196616 | tf_op jit(solution)/shard_map/ppermute | solution.py:649
  40.1 0.0 collective-permute-done.8.rye
  40.1 3.7 %collective-permute-done.9.ryo = f32[32,512]{1,0:T(8,128)S(1)} collective-permute-done((f32[32,512]{1,0:T(8,128)S(1)}, f32[32,512]{1,0:T(8,128)S(1)}, u32[]{:S(2)}, u32[]{:S(2)}) %collective-permute-start.9) | collective-permute-done | bytes 65568 | tf_op jit(solution)/shard_map/ppermute | solution.py:649
  43.8 1.7 %shard_map.99 = (bf16[32,3072]{1,0:T(8,128)(2,1)S(1)}, f32[32,3072]{1,0:T(8,128)S(1)}, bf16[32,512]{1,0:T(8,128)(2,1)S(1)}, f32[32,512]{1,0:T(8,128)S(1)}, f32[3...) custom-call(bf16[32,3072]{1,0:T(8,128)(2,1)S(1)} %get-tuple-element.76.h_in, ...), custom_call_target="tpu_custom_call", output_to_operand_aliasing={{0}: (17, {}), {1}: (18, {})} | custom-call | tf_op jit(solution)/shard_map/pallas_call | solution.py:562
  45.4 0.1 collective-permute-start.10
  45.5 1.4 %collective-permute-start.11 = (f32[32,1152]{1,0:T(8,128)S(1)}, f32[32,1152]{1,0:T(8,128)S(1)}, u32[]{:S(2)}, u32[]{:S(2)}) collective-permute-start(f32[32,1152]{1,0:T(8,128)S(1)} %get-tuple-element.97), channel_id=1, source_target_pairs={{0,1},{1,0},{2,3},{3,2},{4,5},{5,4},{6,7},{7,6},{8,9},{9,8},{10,11... | collective-permute-start | bytes 442376 | tf_op jit(solution)/shard_map/ppermute | solution.py:40
  46.9 0.0 collective-permute-done.10.rxe
  46.9 3.9 %collective-permute-done.11.rxo = f32[32,1152]{1,0:T(8,128)S(1)} collective-permute-done((f32[32,1152]{1,0:T(8,128)S(1)}, f32[32,1152]{1,0:T(8,128)S(1)}, u32[]{:S(2)}, u32[]{:S(2)}) %collective-permute-start.11) | collective-permute-done | bytes 147488 | tf_op jit(solution)/shard_map/ppermute | solution.py:40
  50.8 0.2 shard_map.100
  51.0 0.1 collective-permute-start.12
  51.1 0.6 %shard_map.101 = (f32[32,3072]{1,0:T(8,128)S(1)}, f32[32,512]{1,0:T(8,128)S(1)}) custom-call(bf16[32,3072]{1,0:T(8,128)(2,1)S(1)} %get-tuple-element.92.h_in, f32[32,3072]{1,0:T(8,128)S(1)} %get-tuple-element.93.p_ref.p_in, f32[32,1152]{1,0:T(8,128)S(1)} %collective-permute-done.10.rxe, f32[32,1152]{1,0:T(8,128)S(1)} %collective-permute-done.11.rxo, ...), custom_call_target="tpu_custom_call" | custom-call | flops 377487360 | tf_op jit(solution)/shard_map/pallas_call | solution.py:562
  51.7 2.8 %collective-permute-start.13 = (f32[32,512]{1,0:T(8,128)S(1)}, f32[32,512]{1,0:T(8,128)S(1)}, u32[]{:S(2)}, u32[]{:S(2)}) collective-permute-start(f32[32,512]{1,0:T(8,128)S(1)} %get-tuple-element.101), channel_id=1, source_target_pairs={{0,32},{1,33},{2,34},{3,35},{4,36},{5,37},{6,38},{7,39},{8,16},{9,... | collective-permute-start | bytes 196616 | tf_op jit(solution)/shard_map/ppermute | solution.py:649
  54.4 1.8 %collective-permute-done.12.rye = f32[32,512]{1,0:T(8,128)S(1)} collective-permute-done((f32[32,512]{1,0:T(8,128)S(1)}, f32[32,512]{1,0:T(8,128)S(1)}, u32[]{:S(2)}, u32[]{:S(2)}) %collective-permute-start.12) | collective-permute-done | bytes 65568 | tf_op jit(solution)/shard_map/ppermute | solution.py:630
  56.2 3.2 %collective-permute-done.13.ryo = f32[32,512]{1,0:T(8,128)S(1)} collective-permute-done((f32[32,512]{1,0:T(8,128)S(1)}, f32[32,512]{1,0:T(8,128)S(1)}, u32[]{:S(2)}, u32[]{:S(2)}) %collective-permute-start.13) | collective-permute-done | bytes 65568 | tf_op jit(solution)/shard_map/ppermute | solution.py:649
  59.4 1.4 %shard_map.102 = bf16[32,3,8,128]{3,2,1,0:T(8,128)(2,1)} custom-call(bf16[32,3072]{1,0:T(8,128)(2,1)S(1)} %get-tuple-element.92.h_in, f32[32,3072]{1,0:T(8,128)S(1)} %get-tuple-element.93.p_ref.p_in, bf16[32,512]{1,0:T(8,128)(2,1)S(1)} %get-tuple-element.94.hr_in, f32[32,512]{1,0:T(8,128)S(1)} %get-tuple-element.98.pr_in, ...), custom_call_target="tpu_custom_call" | custom-call | tf_op jit(solution)/shard_map/pallas_call | solution.py:562
  (4 shorter events, 0.0 us)
Async XLA Ops:
  0.0 3.4 %copy-start.1 = (bf16[3,32,32]{2,1,0:T(8,128)(2,1)S(1)}, bf16[3,32,32]{2,1,0:T(8,128)(2,1)}, u32[]{:S(2)}) copy-start(bf16[3,32,32]{2,1,0:T(8,128)(2,1)} %wout.11) | copy-start | bytes 18436
  0.0 3.4 %copy-start = (bf16[3,32,96]{2,1,0:T(8,128)(2,1)S(1)}, bf16[3,32,96]{2,1,0:T(8,128)(2,1)}, u32[]{:S(2)}) copy-start(bf16[3,32,96]{2,1,0:T(8,128)(2,1)} %win.11) | copy-start | bytes 55300
  2.1 4.4 %collective-permute-start = (f32[136,128]{1,0:T(8,128)S(1)}, f32[136,128]{1,0:T(8,128)S(1)}, u32[]{:S(2)}, u32[]{:S(2)}) collective-permute-start(f32[136,128]{1,0:T(8,128)S(1)} %get-tuple-element.59), channel_id=1, source_target_pairs={{0,1},{1,0},{2,3},{3,2},{4,5},{5,4},{6,7},{7,6},{8,9},{9,8},{10,11... | collective-permute-start | bytes 208904 | tf_op jit(solution)/shard_map/ppermute | solution.py:39
  3.4 4.3 %collective-permute-start.1 = (f32[136,128]{1,0:T(8,128)S(1)}, f32[136,128]{1,0:T(8,128)S(1)}, u32[]{:S(2)}, u32[]{:S(2)}) collective-permute-start(f32[136,128]{1,0:T(8,128)S(1)} %get-tuple-element.60), channel_id=1, source_target_pairs={{0,32},{1,2},{2,1},{3,4},{4,3},{5,6},{6,5},{7,39},{8,40},{9,10},{1... | collective-permute-start | bytes 208904 | tf_op jit(solution)/shard_map/ppermute | solution.py:40
  3.4 0.7 %copy-start.4 = (f32[3,32]{1,0:T(4,128)S(1)}, f32[3,32]{1,0:T(4,128)}, u32[]{:S(2)}) copy-start(f32[3,32]{1,0:T(4,128)} %bias.11) | copy-start | bytes 1156
  8.6 3.1 %collective-permute-start.2 = (f32[32,1152]{1,0:T(8,128)S(1)}, f32[32,1152]{1,0:T(8,128)S(1)}, u32[]{:S(2)}, u32[]{:S(2)}) collective-permute-start(f32[32,1152]{1,0:T(8,128)S(1)} %get-tuple-element.65), channel_id=1, source_target_pairs={{0,32},{32,0},{64,96},{96,64},{128,160},{160,128},{192,224},{224,1... | collective-permute-start | bytes 442376 | tf_op jit(solution)/shard_map/ppermute | solution.py:39
  8.7 6.1 %collective-permute-start.3 = (f32[32,1152]{1,0:T(8,128)S(1)}, f32[32,1152]{1,0:T(8,128)S(1)}, u32[]{:S(2)}, u32[]{:S(2)}) collective-permute-start(f32[32,1152]{1,0:T(8,128)S(1)} %get-tuple-element.66), channel_id=1, source_target_pairs={{0,1},{1,0},{2,3},{3,2},{4,5},{5,4},{6,7},{7,6},{8,9},{9,8},{10,11... | collective-permute-start | bytes 442376 | tf_op jit(solution)/shard_map/ppermute | solution.py:40
  14.9 0.7 %copy-start.2 = (bf16[3,32,64]{2,1,0:T(8,128)(2,1)S(1)}, bf16[3,32,64]{2,1,0:T(8,128)(2,1)}, u32[]{:S(2)}) copy-start(bf16[3,32,64]{2,1,0:T(8,128)(2,1)} %nin.11) | copy-start | bytes 36868
  14.9 0.8 %copy-start.3 = (bf16[3,32,32]{2,1,0:T(8,128)(2,1)S(1)}, bf16[3,32,32]{2,1,0:T(8,128)(2,1)}, u32[]{:S(2)}) copy-start(bf16[3,32,32]{2,1,0:T(8,128)(2,1)} %nout.11) | copy-start | bytes 18436
  15.0 0.7 %copy-start.5 = (f32[3,32]{1,0:T(4,128)S(1)}, f32[3,32]{1,0:T(4,128)}, u32[]{:S(2)}) copy-start(f32[3,32]{1,0:T(4,128)} %nbias.11) | copy-start | bytes 1156
  15.1 8.7 %collective-permute-start.4 = (f32[32,512]{1,0:T(8,128)S(1)}, f32[32,512]{1,0:T(8,128)S(1)}, u32[]{:S(2)}, u32[]{:S(2)}) collective-permute-start(f32[32,512]{1,0:T(8,128)S(1)} %get-tuple-element.68), channel_id=1, source_target_pairs={{0,8},{8,0},{16,24},{24,16},{1,9},{9,1},{17,25},{25,17},{2,10},{10... | collective-permute-start | bytes 196616 | tf_op jit(solution)/shard_map/ppermute | solution.py:630
  18.3 8.4 %collective-permute-start.5 = (f32[32,512]{1,0:T(8,128)S(1)}, f32[32,512]{1,0:T(8,128)S(1)}, u32[]{:S(2)}, u32[]{:S(2)}) collective-permute-start(f32[32,512]{1,0:T(8,128)S(1)} %get-tuple-element.71), channel_id=1, source_target_pairs={{0,32},{1,33},{2,34},{3,35},{4,36},{5,37},{6,38},{7,39},{8,16},{9,... | collective-permute-start | bytes 196616 | tf_op jit(solution)/shard_map/ppermute | solution.py:649
  28.4 1.7 %collective-permute-start.6 = (f32[32,1152]{1,0:T(8,128)S(1)}, f32[32,1152]{1,0:T(8,128)S(1)}, u32[]{:S(2)}, u32[]{:S(2)}) collective-permute-start(f32[32,1152]{1,0:T(8,128)S(1)} %get-tuple-element.81), channel_id=1, source_target_pairs={{0,32},{32,0},{64,96},{96,64},{128,160},{160,128},{192,224},{224,1... | collective-permute-start | bytes 442376 | tf_op jit(solution)/shard_map/ppermute | solution.py:39
  28.5 5.2 %collective-permute-start.7 = (f32[32,1152]{1,0:T(8,128)S(1)}, f32[32,1152]{1,0:T(8,128)S(1)}, u32[]{:S(2)}, u32[]{:S(2)}) collective-permute-start(f32[32,1152]{1,0:T(8,128)S(1)} %get-tuple-element.82), channel_id=1, source_target_pairs={{0,1},{1,0},{2,3},{3,2},{4,5},{5,4},{6,7},{7,6},{8,9},{9,8},{10,11... | collective-permute-start | bytes 442376 | tf_op jit(solution)/shard_map/ppermute | solution.py:40
  33.9 6.2 %collective-permute-start.8 = (f32[32,512]{1,0:T(8,128)S(1)}, f32[32,512]{1,0:T(8,128)S(1)}, u32[]{:S(2)}, u32[]{:S(2)}) collective-permute-start(f32[32,512]{1,0:T(8,128)S(1)} %get-tuple-element.84), channel_id=1, source_target_pairs={{0,8},{8,0},{16,24},{24,16},{1,9},{9,1},{17,25},{25,17},{2,10},{10... | collective-permute-start | bytes 196616 | tf_op jit(solution)/shard_map/ppermute | solution.py:630
  36.5 7.2 %collective-permute-start.9 = (f32[32,512]{1,0:T(8,128)S(1)}, f32[32,512]{1,0:T(8,128)S(1)}, u32[]{:S(2)}, u32[]{:S(2)}) collective-permute-start(f32[32,512]{1,0:T(8,128)S(1)} %get-tuple-element.87), channel_id=1, source_target_pairs={{0,32},{1,33},{2,34},{3,35},{4,36},{5,37},{6,38},{7,39},{8,16},{9,... | collective-permute-start | bytes 196616 | tf_op jit(solution)/shard_map/ppermute | solution.py:649
  45.4 1.5 %collective-permute-start.10 = (f32[32,1152]{1,0:T(8,128)S(1)}, f32[32,1152]{1,0:T(8,128)S(1)}, u32[]{:S(2)}, u32[]{:S(2)}) collective-permute-start(f32[32,1152]{1,0:T(8,128)S(1)} %get-tuple-element.96), channel_id=1, source_target_pairs={{0,32},{32,0},{64,96},{96,64},{128,160},{160,128},{192,224},{224,1... | collective-permute-start | bytes 442376 | tf_op jit(solution)/shard_map/ppermute | solution.py:39
  45.5 5.2 %collective-permute-start.11 = (f32[32,1152]{1,0:T(8,128)S(1)}, f32[32,1152]{1,0:T(8,128)S(1)}, u32[]{:S(2)}, u32[]{:S(2)}) collective-permute-start(f32[32,1152]{1,0:T(8,128)S(1)} %get-tuple-element.97), channel_id=1, source_target_pairs={{0,1},{1,0},{2,3},{3,2},{4,5},{5,4},{6,7},{7,6},{8,9},{9,8},{10,11... | collective-permute-start | bytes 442376 | tf_op jit(solution)/shard_map/ppermute | solution.py:40
  51.0 5.3 %collective-permute-start.12 = (f32[32,512]{1,0:T(8,128)S(1)}, f32[32,512]{1,0:T(8,128)S(1)}, u32[]{:S(2)}, u32[]{:S(2)}) collective-permute-start(f32[32,512]{1,0:T(8,128)S(1)} %get-tuple-element.99), channel_id=1, source_target_pairs={{0,8},{8,0},{16,24},{24,16},{1,9},{9,1},{17,25},{25,17},{2,10},{10... | collective-permute-start | bytes 196616 | tf_op jit(solution)/shard_map/ppermute | solution.py:630
  51.7 7.7 %collective-permute-start.13 = (f32[32,512]{1,0:T(8,128)S(1)}, f32[32,512]{1,0:T(8,128)S(1)}, u32[]{:S(2)}, u32[]{:S(2)}) collective-permute-start(f32[32,512]{1,0:T(8,128)S(1)} %get-tuple-element.101), channel_id=1, source_target_pairs={{0,32},{1,33},{2,34},{3,35},{4,36},{5,37},{6,38},{7,39},{8,16},{9,... | collective-permute-start | bytes 196616 | tf_op jit(solution)/shard_map/ppermute | solution.py:649

commit v5 on v4

--- a/solution.py
+++ b/solution.py
@@ -425,15 +425,14 @@
 
 
 def inner_kernel(
-    sizes, layer, last, h_in, p_in, rxe, rxo, syo, nin, nout, nbias, win, wout, bias, e_in, w_in,
-    h_out, p_out, e_out, w_out, syo_out, sems,
+    sizes, layer, last, h_in, p_in, rxe, rxo, nin, nout, nbias, win, wout, bias, e_in, w_in,
+    h_out, p_out, e_out, w_out, sems,
 ):
     ny = sizes[1]
     fetch_e = pltpu.make_async_copy(e_in, e_out, sems.at[0])
     fetch_w = pltpu.make_async_copy(w_in, w_out, sems.at[1])
     fetch_e.start()
     fetch_w.start()
-    syo_out[...] = syo[...]
 
     def write(rows, value):
         h_out[:, rows] = value.astype(BF16)
@@ -522,9 +521,7 @@
     write_x_faces(sizes, p_out, sums, sxe, sxo)
 
 
-def last_inner(sizes, layer, h_in, p_in, rxe, rxo, syo, nin, nout, nbias, res, syo_out):
-    syo_out[...] = syo[...]
-
+def last_inner(sizes, layer, h_in, p_in, rxe, rxo, nin, nout, nbias, res):
     def write(rows, value):
         res[:, rows] = value
 
@@ -627,26 +624,25 @@
         sye, syo, pr = call(
             functools.partial(y_faces, sizes), (p, pr, *got_x), (), (sy_t, sy_t, pr_t)
         )
-        even = lax.ppermute(sye, "gy", even_pairs(lax.axis_size("gy")))
+        got = (*got_x, *exchange(sye, syo, "gy", "gx"))
         if layer + 1 < layers:
             last = layer + 2 == layers
-            h_new, p_new, e_new, w_new, syo = call(
+            h_new, p_new, e_new, w_new = call(
                 functools.partial(inner_kernel, sizes, layer, last),
-                (h, p, *got_x, syo, *node, *edge),
+                (h, p, *got_x, *node, *edge),
                 (e, w),
-                (h_t, p_t, e_t, w_t, sy_t),
+                (h_t, p_t, e_t, w_t),
                 (pltpu.SemaphoreType.DMA((2,)),),
                 flops=work,
             )
         else:
-            res, syo = call(
+            (res,) = call(
                 functools.partial(last_inner, sizes, layer),
-                (h, p, *got_x, syo, *node),
+                (h, p, *got_x, *node),
                 (),
-                (((ch, nodes), F32, "fast"), sy_t),
+                (((ch, nodes), F32, "fast"),),
                 flops=work,
             )
-        got = (*got_x, even, lax.ppermute(syo, AXES, odd_pairs("gy", "gx")))
         if layer + 1 < layers:
             outs = (hr_t, pr_t, sx_t, sx_t) if last else (e_t, hr_t, er_t, pr_t, sx_t, sx_t)
             args = (h, p, hr, er, wr, pr, *got, *node, *edge, w_new, h_new, p_new, e_new)

time: 61 us -> 55.2 us (0.905)
  waiting for transfers between devices: 24 us -> 17.8 us
  starting transfers between devices: 19.6 us -> 20.4 us
    ppermute x4 -> x7, starting transfers between devices: 5.99 us -> 18.5 us  [exchange(): got_odd = lax.ppermute(odd, AXES, odd_pairs(axis, spare))]
    ppermute x6 -> x0, starting transfers between devices: 12.1 us -> none  [the longest x3 11.8 us: on_device(): got = (*got_x, even, lax.ppermute(syo, AXES, odd_pairs('gy', 'gx')))]
    ppermute x6 -> x0, waiting for transfers between devices: 11.6 us -> none  [the longest x3 9.81 us: on_device(): got = (*got_x, even, lax.ppermute(syo, AXES, odd_pairs('gy', 'gx')))]
    ppermute x4 -> x7, waiting for transfers between devices: 11.8 us -> 15.5 us  [exchange(): got_odd = lax.ppermute(odd, AXES, odd_pairs(axis, spare))]
    ppermute x4 -> x7, waiting for transfers between devices: 0.58 us -> 2.35 us  [exchange(): got_even = lax.ppermute(even, axis, even_pairs(lax.axis_size(axis)))]
    ppermute x4 -> x7, starting transfers between devices: 1.56 us -> 1.84 us  [exchange(): got_even = lax.ppermute(even, axis, even_pairs(lax.axis_size(axis)))]
  transfers between devices with their start and end apart: 14 -> 14, of which waited for: 9 -> 10; matrix products, arithmetic and copies ran while one was open for 0% -> 0% of each run, Pallas kernels for 12% -> 14%
where the time goes in v5:
time: 55.2 us; the launch traced here: 54.8 us
  starting transfers between devices  20.4 us (37%)
  waiting for transfers between devices  17.8 us (32%)
  Pallas kernels  15.8 us (29%)
  local copies, waits for them, and re-layouts  0.69 us (1%)
    ppermute x7, starting transfers between devices, exchange(): got_odd = lax.ppermute(odd, AXES, odd_pairs(axis, spare))  18.5 us
    pallas_call x12, Pallas kernels, call(): pl.pallas_call(body, out_shape=[pltpu.VMEM(s, d) if where == 'fast' else...  15.8 us
    ppermute x7, waiting for transfers between devices, exchange(): got_odd = lax.ppermute(odd, AXES, odd_pairs(axis, spare))  15.5 us
    ppermute x7, waiting for transfers between devices, exchange(): got_even = lax.ppermute(even, axis, even_pairs(lax.axis_size(axis)))  2.35 us
    ppermute x7, starting transfers between devices, exchange(): got_even = lax.ppermute(even, axis, even_pairs(lax.axis_size(axis)))  1.84 us
  transfers between devices with their start and end apart: 14, of which 10 were waited for; matrix products, arithmetic and copies ran while one was open for 0% of the time, Pallas kernels for 14%

profile of v5, /device:TPU:68, one launch (start us, length us, event | category | flops | bytes accessed | tf_op | source)
XLA Modules:
  0.0 54.8 jit_solution(12549986302548491639)
XLA Ops:
  0.0 0.0 copy-start.1
  0.0 2.1 %shard_map.91 = (bf16[32,3072]{1,0:T(8,128)(2,1)S(1)}, bf16[3,32,3072]{2,1,0:T(8,128)(2,1)S(1)}, f32[24,8,128]{2,1,0:T(8,128)S(1)}, f32[4,136,128]{2,1,0:T(8,128...) custom-call(bf16[32,3,8,128]{3,2,1,0:T(8,128)(2,1)} %f_in.1, bf16[3,32,3,8,128]{4,3,2,1,0:T(8,128)(2,1)} %es_in.1, ...), custom_call_target="tpu_custom_call" | custom-call | tf_op jit(solution)/shard_map/pallas_call | solution.py:559
  2.1 1.3 %collective-permute-start = (f32[136,128]{1,0:T(8,128)S(1)}, f32[136,128]{1,0:T(8,128)S(1)}, u32[]{:S(2)}, u32[]{:S(2)}) collective-permute-start(f32[136,128]{1,0:T(8,128)S(1)} %get-tuple-element.55), channel_id=1, source_target_pairs={{0,1},{1,0},{2,3},{3,2},{4,5},{5,4},{6,7},{7,6},{8,9},{9,8},{10,11... | collective-permute-start | bytes 208904 | tf_op jit(solution)/shard_map/ppermute | solution.py:39
  3.4 0.0 collective-permute-start.1
  3.4 0.0 copy-done.1
  3.4 0.0 copy-done
  3.4 0.7 %copy-done.4 = f32[3,32]{1,0:T(4,128)S(1)} copy-done((f32[3,32]{1,0:T(4,128)S(1)}, f32[3,32]{1,0:T(4,128)}, u32[]{:S(2)}) %copy-start.4) | copy-done | bytes 408
  4.1 1.8 %shard_map.92 = (bf16[3,32,3072]{2,1,0:T(8,128)(2,1)S(1)}, f32[32,3072]{1,0:T(8,128)S(1)}) custom-call(bf16[32,3072]{1,0:T(8,128)(2,1)S(1)} %get-tuple-element.50.h_ref.h_in, bf16[3,32,3072]{2,1,0:T(8,128)(2,1)S(1)} %get-tuple-element.51.e_ref, f32[24,8,128]{2,1,0:T(8,128)S(1)} %get-tuple-element.52.w_ref.w_in, bf16[3,32,96]{2,1,0:T(8,128)(2,1)S(1)} %copy-done, ...), custom_call_target="tpu_custom_call" | custom-call | flops 377487360 | tf_op jit(solution)/shard_map/pallas_call | solution.py:559
  6.0 0.6 %collective-permute-done.rze = f32[136,128]{1,0:T(8,128)S(1)} collective-permute-done((f32[136,128]{1,0:T(8,128)S(1)}, f32[136,128]{1,0:T(8,128)S(1)}, u32[]{:S(2)}, u32[]{:S(2)}) %collective-permute-start) | collective-permute-done | bytes 69664 | tf_op jit(solution)/shard_map/ppermute | solution.py:39
  6.5 1.2 %collective-permute-done.1.rzo = f32[136,128]{1,0:T(8,128)S(1)} collective-permute-done((f32[136,128]{1,0:T(8,128)S(1)}, f32[136,128]{1,0:T(8,128)S(1)}, u32[]{:S(2)}, u32[]{:S(2)}) %collective-permute-start.1) | collective-permute-done | bytes 69664 | tf_op jit(solution)/shard_map/ppermute | solution.py:40
  7.7 0.9 %shard_map.93 = (bf16[32,512]{1,0:T(8,128)(2,1)S(1)}, bf16[3,32,512]{2,1,0:T(8,128)(2,1)S(1)}, f32[8,512]{1,0:T(8,128)S(1)}, f32[32,512]{1,0:T(8,128)S(1)}, f32[...) custom-call(f32[32,3072]{1,0:T(8,128)S(1)} %get-tuple-element.53.p_ref.p_in, f32[4,136,128]{2,1,0:T(8,128)S(1)} %get-tuple-element.54.own_ref, ...), custom_call_target="tpu_custom_call" | custom-call | tf_op jit(solution)/shard_map/pallas_call | solution.py:559
  8.6 0.1 collective-permute-start.2
  8.7 3.0 %collective-permute-start.3 = (f32[32,1152]{1,0:T(8,128)S(1)}, f32[32,1152]{1,0:T(8,128)S(1)}, u32[]{:S(2)}, u32[]{:S(2)}) collective-permute-start(f32[32,1152]{1,0:T(8,128)S(1)} %get-tuple-element.62), channel_id=1, source_target_pairs={{0,1},{1,0},{2,3},{3,2},{4,5},{5,4},{6,7},{7,6},{8,9},{9,8},{10,11... | collective-permute-start | bytes 442376 | tf_op jit(solution)/shard_map/ppermute | solution.py:40
  11.7 0.0 collective-permute-done.2.rxe
  11.7 3.1 %collective-permute-done.3.rxo = f32[32,1152]{1,0:T(8,128)S(1)} collective-permute-done((f32[32,1152]{1,0:T(8,128)S(1)}, f32[32,1152]{1,0:T(8,128)S(1)}, u32[]{:S(2)}, u32[]{:S(2)}) %collective-permute-start.3) | collective-permute-done | bytes 147488 | tf_op jit(solution)/shard_map/ppermute | solution.py:40
  14.9 0.2 shard_map.94
  15.0 0.0 copy-start.5
  15.1 0.1 collective-permute-start.4
  15.2 5.9 %collective-permute-start.5 = (f32[32,512]{1,0:T(8,128)S(1)}, f32[32,512]{1,0:T(8,128)S(1)}, u32[]{:S(2)}, u32[]{:S(2)}) collective-permute-start(f32[32,512]{1,0:T(8,128)S(1)} %get-tuple-element.65), channel_id=1, source_target_pairs={{0,32},{1,33},{2,34},{3,35},{4,36},{5,37},{6,38},{7,39},{8,16},{9,... | collective-permute-start | bytes 196616 | tf_op jit(solution)/shard_map/ppermute | solution.py:40
  21.1 0.0 copy-done.2
  21.1 0.0 copy-done.3
  21.1 0.0 copy-done.5
  21.1 2.5 %shard_map.95 = (bf16[32,3072]{1,0:T(8,128)(2,1)S(1)}, f32[32,3072]{1,0:T(8,128)S(1)}, bf16[3,32,3072]{2,1,0:T(8,128)(2,1)S(1)}, f32[24,8,128]{2,1,0:T(8,128)S(1)}) custom-call(bf16[32,3072]{1,0:T(8,128)(2,1)S(1)} %get-tuple-element.50.h_ref.h_in, f32[32,3072]{1,0:T(8,128)S(1)} %get-tuple-element.53.p_ref.p_in, f32[32,1152]{1,0:T(8,128)S(1)} %collective-permute-done.2.rxe, ...), custom_call_target="tpu_custom_call" | custom-call | flops 377487360 | tf_op jit(solution)/shard_map/pallas_call | solution.py:559
  23.7 0.0 collective-permute-done.4.rye
  23.7 0.3 collective-permute-done.5.ryo
  24.0 1.7 %shard_map.96 = (bf16[32,3072]{1,0:T(8,128)(2,1)S(1)}, f32[32,3072]{1,0:T(8,128)S(1)}, bf16[3,32,3072]{2,1,0:T(8,128)(2,1)S(1)}, bf16[32,512]{1,0:T(8,128)(2,1)S...) custom-call(bf16[32,3072]{1,0:T(8,128)(2,1)S(1)} %get-tuple-element., ...), custom_call_target="tpu_custom_call", output_to_operand_aliasing={{0}: (17, {}), {1}: (18, {}), {2}: (19, {})} | custom-call | tf_op jit(solution)/shard_map/pallas_call | solution.py:559
  25.6 0.1 collective-permute-start.6
  25.7 1.8 %collective-permute-start.7 = (f32[32,1152]{1,0:T(8,128)S(1)}, f32[32,1152]{1,0:T(8,128)S(1)}, u32[]{:S(2)}, u32[]{:S(2)}) collective-permute-start(f32[32,1152]{1,0:T(8,128)S(1)} %get-tuple-element.77), channel_id=1, source_target_pairs={{0,1},{1,0},{2,3},{3,2},{4,5},{5,4},{6,7},{7,6},{8,9},{9,8},{10,11... | collective-permute-start | bytes 442376 | tf_op jit(solution)/shard_map/ppermute | solution.py:40
  27.6 0.0 collective-permute-done.6.rxe
  27.6 3.4 %collective-permute-done.7.rxo = f32[32,1152]{1,0:T(8,128)S(1)} collective-permute-done((f32[32,1152]{1,0:T(8,128)S(1)}, f32[32,1152]{1,0:T(8,128)S(1)}, u32[]{:S(2)}, u32[]{:S(2)}) %collective-permute-start.7) | collective-permute-done | bytes 147488 | tf_op jit(solution)/shard_map/ppermute | solution.py:40
  31.0 0.2 shard_map.97
  31.2 0.1 collective-permute-start.8
  31.3 3.6 %collective-permute-start.9 = (f32[32,512]{1,0:T(8,128)S(1)}, f32[32,512]{1,0:T(8,128)S(1)}, u32[]{:S(2)}, u32[]{:S(2)}) collective-permute-start(f32[32,512]{1,0:T(8,128)S(1)} %get-tuple-element.80), channel_id=1, source_target_pairs={{0,32},{1,33},{2,34},{3,35},{4,36},{5,37},{6,38},{7,39},{8,16},{9,... | collective-permute-start | bytes 196616 | tf_op jit(solution)/shard_map/ppermute | solution.py:40
  34.9 2.5 %shard_map.98 = (bf16[32,3072]{1,0:T(8,128)(2,1)S(1)}, f32[32,3072]{1,0:T(8,128)S(1)}, bf16[3,32,3072]{2,1,0:T(8,128)(2,1)S(1)}, f32[24,8,128]{2,1,0:T(8,128)S(1)}) custom-call(bf16[32,3072]{1,0:T(8,128)(2,1)S(1)} %get-tuple-element.71.h_in, f32[32,3072]{1,0:T(8,128)S(1)} %get-tuple-element.72.p_ref.p_in, f32[32,1152]{1,0:T(8,128)S(1)} %collective-permute-done.6.rxe, ...), custom_call_target="tpu_custom_call" | custom-call | flops 377487360 | tf_op jit(solution)/shard_map/pallas_call | solution.py:559
  37.4 0.0 collective-permute-done.8.rye
  37.4 1.0 %collective-permute-done.9.ryo = f32[32,512]{1,0:T(8,128)S(1)} collective-permute-done((f32[32,512]{1,0:T(8,128)S(1)}, f32[32,512]{1,0:T(8,128)S(1)}, u32[]{:S(2)}, u32[]{:S(2)}) %collective-permute-start.9) | collective-permute-done | bytes 65568 | tf_op jit(solution)/shard_map/ppermute | solution.py:40
  38.4 1.7 %shard_map.99 = (bf16[32,3072]{1,0:T(8,128)(2,1)S(1)}, f32[32,3072]{1,0:T(8,128)S(1)}, bf16[32,512]{1,0:T(8,128)(2,1)S(1)}, f32[32,512]{1,0:T(8,128)S(1)}, f32[3...) custom-call(bf16[32,3072]{1,0:T(8,128)(2,1)S(1)} %get-tuple-element.71.h_in, ...), custom_call_target="tpu_custom_call", output_to_operand_aliasing={{0}: (17, {}), {1}: (18, {})} | custom-call | tf_op jit(solution)/shard_map/pallas_call | solution.py:559
  40.1 0.1 collective-permute-start.10
  40.2 1.1 %collective-permute-start.11 = (f32[32,1152]{1,0:T(8,128)S(1)}, f32[32,1152]{1,0:T(8,128)S(1)}, u32[]{:S(2)}, u32[]{:S(2)}) collective-permute-start(f32[32,1152]{1,0:T(8,128)S(1)} %get-tuple-element.91), channel_id=1, source_target_pairs={{0,1},{1,0},{2,3},{3,2},{4,5},{5,4},{6,7},{7,6},{8,9},{9,8},{10,11... | collective-permute-start | bytes 442376 | tf_op jit(solution)/shard_map/ppermute | solution.py:40
  41.3 0.2 collective-permute-done.10.rxe
  41.6 3.9 %collective-permute-done.11.rxo = f32[32,1152]{1,0:T(8,128)S(1)} collective-permute-done((f32[32,1152]{1,0:T(8,128)S(1)}, f32[32,1152]{1,0:T(8,128)S(1)}, u32[]{:S(2)}, u32[]{:S(2)}) %collective-permute-start.11) | collective-permute-done | bytes 147488 | tf_op jit(solution)/shard_map/ppermute | solution.py:40
  45.4 0.2 shard_map.100
  45.6 0.1 collective-permute-start.12
  45.7 3.0 %collective-permute-start.13 = (f32[32,512]{1,0:T(8,128)S(1)}, f32[32,512]{1,0:T(8,128)S(1)}, u32[]{:S(2)}, u32[]{:S(2)}) collective-permute-start(f32[32,512]{1,0:T(8,128)S(1)} %get-tuple-element.94), channel_id=1, source_target_pairs={{0,32},{1,33},{2,34},{3,35},{4,36},{5,37},{6,38},{7,39},{8,16},{9,... | collective-permute-start | bytes 196616 | tf_op jit(solution)/shard_map/ppermute | solution.py:40
  48.7 0.6 %shard_map.101.res = f32[32,3072]{1,0:T(8,128)S(1)} custom-call(bf16[32,3072]{1,0:T(8,128)(2,1)S(1)} %get-tuple-element.86.h_in, f32[32,3072]{1,0:T(8,128)S(1)} %get-tuple-element.87.p_ref.p_in, f32[32,1152]{1,0:T(8,128)S(1)} %collective-permute-done.10.rxe, f32[32,1152]{1,0:T(8,128)S(1)} %collective-permute-done.11.rxo, bf16[3,32,64]{2,1,0:T(8,128)(2,1)S(1)} %copy-done.2, ...), custom_call_target="tpu_custom_call" | custom-call | flops 377487360 | tf_op jit(solution)/shard_map/pallas_call | solution.py:559
  49.3 1.5 %collective-permute-done.12.rye = f32[32,512]{1,0:T(8,128)S(1)} collective-permute-done((f32[32,512]{1,0:T(8,128)S(1)}, f32[32,512]{1,0:T(8,128)S(1)}, u32[]{:S(2)}, u32[]{:S(2)}) %collective-permute-start.12) | collective-permute-done | bytes 65568 | tf_op jit(solution)/shard_map/ppermute | solution.py:39
  50.9 2.6 %collective-permute-done.13.ryo = f32[32,512]{1,0:T(8,128)S(1)} collective-permute-done((f32[32,512]{1,0:T(8,128)S(1)}, f32[32,512]{1,0:T(8,128)S(1)}, u32[]{:S(2)}, u32[]{:S(2)}) %collective-permute-start.13) | collective-permute-done | bytes 65568 | tf_op jit(solution)/shard_map/ppermute | solution.py:40
  53.4 1.4 %shard_map.102 = bf16[32,3,8,128]{3,2,1,0:T(8,128)(2,1)} custom-call(bf16[32,3072]{1,0:T(8,128)(2,1)S(1)} %get-tuple-element.86.h_in, f32[32,3072]{1,0:T(8,128)S(1)} %get-tuple-element.87.p_ref.p_in, bf16[32,512]{1,0:T(8,128)(2,1)S(1)} %get-tuple-element.88.hr_in, f32[32,512]{1,0:T(8,128)S(1)} %get-tuple-element.92.pr_in, ...), custom_call_target="tpu_custom_call" | custom-call | tf_op jit(solution)/shard_map/pallas_call | solution.py:559
  (4 shorter events, 0.0 us)
Async XLA Ops:
  0.0 3.4 %copy-start.1 = (bf16[3,32,32]{2,1,0:T(8,128)(2,1)S(1)}, bf16[3,32,32]{2,1,0:T(8,128)(2,1)}, u32[]{:S(2)}) copy-start(bf16[3,32,32]{2,1,0:T(8,128)(2,1)} %wout.11) | copy-start | bytes 18436
  0.0 3.4 %copy-start = (bf16[3,32,96]{2,1,0:T(8,128)(2,1)S(1)}, bf16[3,32,96]{2,1,0:T(8,128)(2,1)}, u32[]{:S(2)}) copy-start(bf16[3,32,96]{2,1,0:T(8,128)(2,1)} %win.11) | copy-start | bytes 55300
  2.1 4.4 %collective-permute-start = (f32[136,128]{1,0:T(8,128)S(1)}, f32[136,128]{1,0:T(8,128)S(1)}, u32[]{:S(2)}, u32[]{:S(2)}) collective-permute-start(f32[136,128]{1,0:T(8,128)S(1)} %get-tuple-element.55), channel_id=1, source_target_pairs={{0,1},{1,0},{2,3},{3,2},{4,5},{5,4},{6,7},{7,6},{8,9},{9,8},{10,11... | collective-permute-start | bytes 208904 | tf_op jit(solution)/shard_map/ppermute | solution.py:39
  3.4 4.3 %collective-permute-start.1 = (f32[136,128]{1,0:T(8,128)S(1)}, f32[136,128]{1,0:T(8,128)S(1)}, u32[]{:S(2)}, u32[]{:S(2)}) collective-permute-start(f32[136,128]{1,0:T(8,128)S(1)} %get-tuple-element.56), channel_id=1, source_target_pairs={{0,32},{1,2},{2,1},{3,4},{4,3},{5,6},{6,5},{7,39},{8,40},{9,10},{1... | collective-permute-start | bytes 208904 | tf_op jit(solution)/shard_map/ppermute | solution.py:40
  3.4 0.7 %copy-start.4 = (f32[3,32]{1,0:T(4,128)S(1)}, f32[3,32]{1,0:T(4,128)}, u32[]{:S(2)}) copy-start(f32[3,32]{1,0:T(4,128)} %bias.11) | copy-start | bytes 1156
  8.6 3.1 %collective-permute-start.2 = (f32[32,1152]{1,0:T(8,128)S(1)}, f32[32,1152]{1,0:T(8,128)S(1)}, u32[]{:S(2)}, u32[]{:S(2)}) collective-permute-start(f32[32,1152]{1,0:T(8,128)S(1)} %get-tuple-element.61), channel_id=1, source_target_pairs={{0,32},{32,0},{64,96},{96,64},{128,160},{160,128},{192,224},{224,1... | collective-permute-start | bytes 442376 | tf_op jit(solution)/shard_map/ppermute | solution.py:39
  8.7 6.1 %collective-permute-start.3 = (f32[32,1152]{1,0:T(8,128)S(1)}, f32[32,1152]{1,0:T(8,128)S(1)}, u32[]{:S(2)}, u32[]{:S(2)}) collective-permute-start(f32[32,1152]{1,0:T(8,128)S(1)} %get-tuple-element.62), channel_id=1, source_target_pairs={{0,1},{1,0},{2,3},{3,2},{4,5},{5,4},{6,7},{7,6},{8,9},{9,8},{10,11... | collective-permute-start | bytes 442376 | tf_op jit(solution)/shard_map/ppermute | solution.py:40
  14.9 6.2 %copy-start.2 = (bf16[3,32,64]{2,1,0:T(8,128)(2,1)S(1)}, bf16[3,32,64]{2,1,0:T(8,128)(2,1)}, u32[]{:S(2)}) copy-start(bf16[3,32,64]{2,1,0:T(8,128)(2,1)} %nin.11) | copy-start | bytes 36868
  14.9 6.2 %copy-start.3 = (bf16[3,32,32]{2,1,0:T(8,128)(2,1)S(1)}, bf16[3,32,32]{2,1,0:T(8,128)(2,1)}, u32[]{:S(2)}) copy-start(bf16[3,32,32]{2,1,0:T(8,128)(2,1)} %nout.11) | copy-start | bytes 18436
  15.0 6.1 %copy-start.5 = (f32[3,32]{1,0:T(4,128)S(1)}, f32[3,32]{1,0:T(4,128)}, u32[]{:S(2)}) copy-start(f32[3,32]{1,0:T(4,128)} %nbias.11) | copy-start | bytes 1156
  15.1 8.6 %collective-permute-start.4 = (f32[32,512]{1,0:T(8,128)S(1)}, f32[32,512]{1,0:T(8,128)S(1)}, u32[]{:S(2)}, u32[]{:S(2)}) collective-permute-start(f32[32,512]{1,0:T(8,128)S(1)} %get-tuple-element.64), channel_id=1, source_target_pairs={{0,8},{8,0},{16,24},{24,16},{1,9},{9,1},{17,25},{25,17},{2,10},{10... | collective-permute-start | bytes 196616 | tf_op jit(solution)/shard_map/ppermute | solution.py:39
  15.2 8.8 %collective-permute-start.5 = (f32[32,512]{1,0:T(8,128)S(1)}, f32[32,512]{1,0:T(8,128)S(1)}, u32[]{:S(2)}, u32[]{:S(2)}) collective-permute-start(f32[32,512]{1,0:T(8,128)S(1)} %get-tuple-element.65), channel_id=1, source_target_pairs={{0,32},{1,33},{2,34},{3,35},{4,36},{5,37},{6,38},{7,39},{8,16},{9,... | collective-permute-start | bytes 196616 | tf_op jit(solution)/shard_map/ppermute | solution.py:40
  25.6 1.9 %collective-permute-start.6 = (f32[32,1152]{1,0:T(8,128)S(1)}, f32[32,1152]{1,0:T(8,128)S(1)}, u32[]{:S(2)}, u32[]{:S(2)}) collective-permute-start(f32[32,1152]{1,0:T(8,128)S(1)} %get-tuple-element.76), channel_id=1, source_target_pairs={{0,32},{32,0},{64,96},{96,64},{128,160},{160,128},{192,224},{224,1... | collective-permute-start | bytes 442376 | tf_op jit(solution)/shard_map/ppermute | solution.py:39
  25.7 5.2 %collective-permute-start.7 = (f32[32,1152]{1,0:T(8,128)S(1)}, f32[32,1152]{1,0:T(8,128)S(1)}, u32[]{:S(2)}, u32[]{:S(2)}) collective-permute-start(f32[32,1152]{1,0:T(8,128)S(1)} %get-tuple-element.77), channel_id=1, source_target_pairs={{0,1},{1,0},{2,3},{3,2},{4,5},{5,4},{6,7},{7,6},{8,9},{9,8},{10,11... | collective-permute-start | bytes 442376 | tf_op jit(solution)/shard_map/ppermute | solution.py:40
  31.2 6.3 %collective-permute-start.8 = (f32[32,512]{1,0:T(8,128)S(1)}, f32[32,512]{1,0:T(8,128)S(1)}, u32[]{:S(2)}, u32[]{:S(2)}) collective-permute-start(f32[32,512]{1,0:T(8,128)S(1)} %get-tuple-element.79), channel_id=1, source_target_pairs={{0,8},{8,0},{16,24},{24,16},{1,9},{9,1},{17,25},{25,17},{2,10},{10... | collective-permute-start | bytes 196616 | tf_op jit(solution)/shard_map/ppermute | solution.py:39
  31.3 7.2 %collective-permute-start.9 = (f32[32,512]{1,0:T(8,128)S(1)}, f32[32,512]{1,0:T(8,128)S(1)}, u32[]{:S(2)}, u32[]{:S(2)}) collective-permute-start(f32[32,512]{1,0:T(8,128)S(1)} %get-tuple-element.80), channel_id=1, source_target_pairs={{0,32},{1,33},{2,34},{3,35},{4,36},{5,37},{6,38},{7,39},{8,16},{9,... | collective-permute-start | bytes 196616 | tf_op jit(solution)/shard_map/ppermute | solution.py:40
  40.1 1.5 %collective-permute-start.10 = (f32[32,1152]{1,0:T(8,128)S(1)}, f32[32,1152]{1,0:T(8,128)S(1)}, u32[]{:S(2)}, u32[]{:S(2)}) collective-permute-start(f32[32,1152]{1,0:T(8,128)S(1)} %get-tuple-element.90), channel_id=1, source_target_pairs={{0,32},{32,0},{64,96},{96,64},{128,160},{160,128},{192,224},{224,1... | collective-permute-start | bytes 442376 | tf_op jit(solution)/shard_map/ppermute | solution.py:39
  40.2 5.2 %collective-permute-start.11 = (f32[32,1152]{1,0:T(8,128)S(1)}, f32[32,1152]{1,0:T(8,128)S(1)}, u32[]{:S(2)}, u32[]{:S(2)}) collective-permute-start(f32[32,1152]{1,0:T(8,128)S(1)} %get-tuple-element.91), channel_id=1, source_target_pairs={{0,1},{1,0},{2,3},{3,2},{4,5},{5,4},{6,7},{7,6},{8,9},{9,8},{10,11... | collective-permute-start | bytes 442376 | tf_op jit(solution)/shard_map/ppermute | solution.py:40
  45.6 5.3 %collective-permute-start.12 = (f32[32,512]{1,0:T(8,128)S(1)}, f32[32,512]{1,0:T(8,128)S(1)}, u32[]{:S(2)}, u32[]{:S(2)}) collective-permute-start(f32[32,512]{1,0:T(8,128)S(1)} %get-tuple-element.93), channel_id=1, source_target_pairs={{0,8},{8,0},{16,24},{24,16},{1,9},{9,1},{17,25},{25,17},{2,10},{10... | collective-permute-start | bytes 196616 | tf_op jit(solution)/shard_map/ppermute | solution.py:39
  45.7 7.7 %collective-permute-start.13 = (f32[32,512]{1,0:T(8,128)S(1)}, f32[32,512]{1,0:T(8,128)S(1)}, u32[]{:S(2)}, u32[]{:S(2)}) collective-permute-start(f32[32,512]{1,0:T(8,128)S(1)} %get-tuple-element.94), channel_id=1, source_target_pairs={{0,32},{1,33},{2,34},{3,35},{4,36},{5,37},{6,38},{7,39},{8,16},{9,... | collective-permute-start | bytes 196616 | tf_op jit(solution)/shard_map/ppermute | solution.py:40

commit v6 on v5

--- a/solution.py
+++ b/solution.py
@@ -6,6 +6,7 @@
 from jax.experimental import pallas as pl
 from jax.experimental.pallas import tpu as pltpu
 from jax.sharding import PartitionSpec as P
+
 
 F32 = jnp.float32
 BF16 = jnp.bfloat16
@@ -36,8 +37,8 @@
 
 
 def exchange(even, odd, axis, spare):
+    got_odd = lax.ppermute(odd, AXES, odd_pairs(axis, spare))
     got_even = lax.ppermute(even, axis, even_pairs(lax.axis_size(axis)))
-    got_odd = lax.ppermute(odd, AXES, odd_pairs(axis, spare))
     return got_even, got_odd
 
 
@@ -83,7 +84,17 @@
     return jnp.dot(w_out, silu(pre).astype(BF16), preferred_element_type=F32)
 
 
-def rim_edges(sizes, h, e, w, w_in, w_out, bias):
+def batch(w_in, bias, w_out, groups):
+    stacked = [jnp.concatenate([p.astype(BF16) for p in pieces], axis=0) for pieces in groups]
+    out = perceptron(w_in, bias, w_out, [jnp.concatenate(stacked, axis=1)])
+    ends, results = 0, []
+    for piece in stacked:
+        results.append(out[:, ends : ends + piece.shape[1]])
+        ends += piece.shape[1]
+    return results
+
+
+def rim_groups(sizes, h, e):
     nx, ny = sizes
     lane = lanes_of()
     at, y_at = lane % 4, (lane // 4) % ny
@@ -102,24 +113,29 @@
     ahead_x = [jnp.where(lane < x_step * (nx - 1), turn(v, -x_step), 0.0) for v in h]
     ahead_y = [jnp.where(y_at < ny - 1, turn(v, -4), 0.0) for v in h]
     cur = jnp.concatenate(h, axis=1)
-    updated, weighted = [], []
-    for k, shifted in enumerate((ahead_x, ahead_y, ahead_z)):
-        edge = jnp.concatenate(e[k], axis=1)
-        msg = perceptron(w_in, bias, w_out, [cur, jnp.concatenate(shifted, axis=1), edge])
-        updated.append(edge + msg)
-        weighted.append([tile(msg, i) * w[i][k : k + 1, :] for i in range(len(h))])
-    wx, wy, wz = weighted
-    wo = wz[4] if outer else jnp.zeros_like(a)
+    return [
+        [cur, jnp.concatenate(shifted, axis=1), e[k]]
+        for k, shifted in enumerate((ahead_x, ahead_y, ahead_z))
+    ]
+
+
+def rim_sums(sizes, messages, w):
+    at = lanes_of() % 4
+    count = len(w)
+    wx, wy, wz = (
+        [tile(msg, i) * w[i][k : k + 1, :] for i in range(count)] for k, msg in enumerate(messages)
+    )
+    wo = wz[4] if count == 5 else jnp.zeros_like(wz[0])
     behind = [
         jnp.where(at == 0, wz[3], turn(wz[0], 1)),
         jnp.where(at == 0, 0.0, turn(wz[1], 1)),
         jnp.where(at == 3, wz[1], jnp.where(at == 0, 0.0, turn(wz[2], 1))),
         jnp.where(at == 0, wo, jnp.where(at == 1, turn(wo, -2), turn(wz[3], 1))),
     ]
-    sums = [
-        wx[i] + wy[i] + wz[i] + turn(wx[i], x_step) + turn(wy[i], 4) + behind[i] for i in range(4)
+    return [
+        wx[i] + wy[i] + wz[i] + turn(wx[i], 4 * sizes[1]) + turn(wy[i], 4) + behind[i]
+        for i in range(4)
     ]
-    return updated, sums
 
 
 def quarters(lane, parts):
@@ -148,18 +164,21 @@
 
 def rim_y_faces(sums):
     group = (lanes_of() // 4) % 8
-    packed = jnp.zeros_like(sums[0])
-    for i, v in enumerate(sums):
-        packed = jnp.where(group == i, turn(v, 4 * i), packed)
-        packed = jnp.where(group == 4 + i, turn(v, 4 * i - 12), packed)
-    return packed
+    faces = []
+    for first in (0, 28):
+        face = jnp.zeros_like(sums[0])
+        for i, v in enumerate(sums):
+            face = jnp.where(group == i, turn(v, 4 * i - first), face)
+        faces.append(jnp.where(group[:16] < 4, face[:16], turn(face[16:], 16)))
+    return faces
 
 
 def rim_add_y(sums, low, high):
     group = (lanes_of() // 4) % 8
+    low, high = (jnp.concatenate([v, turn(v, -16)], axis=0) for v in (low, high))
     return [
         v
-        + jnp.where(group == 0, turn(low, -16 - 4 * i), 0.0)
+        + jnp.where(group == 0, turn(low, -4 * i), 0.0)
         + jnp.where(group == 7, turn(high, 28 - 4 * i), 0.0)
         for i, v in enumerate(sums)
     ]
@@ -194,23 +213,28 @@
 def edge_rows(sizes, first, count, last, h_ref, e_in, e_out, w_ref, w_in, w_out, bias, p_ref):
     nx, ny = sizes
     whole = first + count == ny
-    prev_x = None
+    groups = []
     for x in range(nx):
         k0 = x * ny + first
-        rows = span_of(k0, count)
-        cur = h_ref[:, rows]
+        cur = h_ref[:, span_of(k0, count)]
         ahead_x = h_ref[:, span_of(k0 + ny, count)] if x + 1 < nx else jnp.zeros_like(cur)
         ahead_y = cur[:, LANES:]
         if whole:
             ahead_y = jnp.concatenate([ahead_y, jnp.zeros((32, LANES), BF16)], axis=1)
-        weighted = []
         for d, shifted in enumerate((ahead_x, ahead_y, ahead_along_z(cur))):
             n = shifted.shape[1]
-            part = slice(k0 * LANES, k0 * LANES + n)
-            edge = e_in[d, :, part]
-            msg = perceptron(w_in, bias, w_out, [cur[:, :n], shifted, edge])
+            groups.append([cur[:, :n], shifted, e_in[d, :, k0 * LANES : k0 * LANES + n]])
+    messages = batch(w_in, bias, w_out, groups)
+    prev_x = None
+    for x in range(nx):
+        k0 = x * ny + first
+        mine = messages[3 * x : 3 * x + 3]
+        weighted = []
+        for d, msg in enumerate(mine):
+            n = msg.shape[1]
             if not last:
-                e_out[d, :, part] = (edge.astype(F32) + msg).astype(BF16)
+                part = slice(k0 * LANES, k0 * LANES + n)
+                e_out[d, :, part] = (groups[3 * x + d][2].astype(F32) + msg).astype(BF16)
             weighted.append(
                 [tile(msg, i) * w_ref[k0 + i, d : d + 1, :] for i in range(n // LANES)]
             )
@@ -248,8 +272,23 @@
         sxo[:, :span] = p_ref[:, high]
 
 
+ENDS = ((-1, 4), (0, 0))
+NEXT = ((1, -4), (-2, 8))
+
+
+def collect(dest, first, size, parts, rows, row_of):
+    group = lanes_of(size) // 4
+    found = [jnp.zeros((size, LANES), F32)] * len(parts)
+    for k in range(rows):
+        turned = turn(row_of(k), 4 * k)
+        for i, (step, _) in enumerate(parts):
+            found[i] = jnp.where(group == (k + step) % 32, turned, found[i])
+    for i, (_, back) in enumerate(parts):
+        dest[i, first : first + size, :] = turn(found[i], back)
+
+
 def unpack_kernel(
-    sizes, f_in, es_in, m_in, h_ref, e_ref, w_ref, own_ref, sze, szo, buf, f_ref, es_ref, m_ref, sems
+    sizes, f_in, es_in, m_in, buf, w_ref, own_ref, sze, szo, f_ref, es_ref, m_ref, sems
 ):
     nx, ny = sizes
     rows = nx * ny
@@ -282,48 +321,46 @@
                 w_ref[x * ny + y, d : d + 1, :] = shares[d][y : y + 1, :]
             w_ref[x * ny + y, 3:8, :] = jnp.zeros((5, LANES), F32)
 
-    def collect(first, size, row_of):
-        group = lanes_of(size) // 4
-        found = [jnp.zeros((size, LANES), F32)] * 4
-        for k in range(rows):
-            turned = turn(row_of(k), 4 * k)
-            for i, shift in enumerate((-1, 0, 1, -2)):
-                found[i] = jnp.where(group == (k + shift) % 32, turned, found[i])
-        for i, shift in enumerate((4, 0, -4, 8)):
-            own_ref[i, first : first + size, :] = turn(found[i], shift)
-
     for field in range(4):
         fetches[1 + field].wait()
         source = f_ref[...] if field == 0 else es_ref[field - 1]
         buf[field] = source.astype(F32).reshape(buf.shape[1:])
+        collect(
+            own_ref, 32 * field, 32, ENDS, rows,
+            lambda k, field=field: buf[field, pl.ds(k, 32, stride=rows), :],
+        )
+    collect(own_ref, 128, 8, ENDS, rows, lambda k: w_ref[k])
+    is_even = lax.axis_index("gz") % 2 == 0
+    sze[...] = jnp.where(is_even, own_ref[0], own_ref[1])
+    szo[...] = jnp.where(is_even, own_ref[1], own_ref[0])
+
+
+def first_edges(sizes, buf, w_ref, win, wout, bias, h_ref, e_out, p_ref, next_ref, e_ref):
+    nx, ny = sizes
+    rows = nx * ny
+    for field in range(4):
 
         def row_of(k, field=field):
             t = buf[field, pl.ds(k, 32, stride=rows), :]
             if field == 0:
-                h_ref[:, k * LANES : (k + 1) * LANES] = t.astype(BF16)
+                h_ref[:, span_of(k, 1)] = t.astype(BF16)
             else:
-                e_ref[field - 1, :, k * LANES : (k + 1) * LANES] = t.astype(BF16)
+                e_ref[field - 1, :, span_of(k, 1)] = t.astype(BF16)
             return t
 
-        collect(32 * field, 32, row_of)
-    collect(128, 8, lambda k: w_ref[k])
-    is_even = lax.axis_index("gz") % 2 == 0
-    sze[...] = jnp.where(is_even, own_ref[0], own_ref[1])
-    szo[...] = jnp.where(is_even, own_ref[1], own_ref[0])
-
-
-def first_edges(sizes, h_ref, e_ref, w_ref, win, wout, bias, e_out, p_ref):
+        collect(next_ref, 32 * field, 32, NEXT, rows, row_of)
+    collect(next_ref, 128, 8, NEXT, rows, lambda k: w_ref[k])
     edge_rows(
-        sizes, 0, sizes[1], False, h_ref, e_ref, e_out, w_ref, win[0], wout[0], column(bias[0:1, :]),
-        p_ref,
+        sizes, 0, ny, False, h_ref, e_ref, e_out, w_ref, win[0], wout[0], column(bias[0:1, :]), p_ref
     )
 
 
 def first_rim(
-    sizes, p_ref, own_ref, rze, rzo, win, wout, bias, hr_out, er_out, wr_out, pr_out, sxe, sxo
+    sizes, p_ref, own_ref, next_ref, rze, rzo, win, wout, bias, hr_out, er_out, wr_out, pr_out, sxe, sxo
 ):
     at = lanes_of(own_ref.shape[1]) % 4
-    own_a, own_b, upper, lower = (own_ref[i] for i in range(4))
+    own_a, own_b = own_ref[0], own_ref[1]
+    upper, lower = next_ref[0], next_ref[1]
     prev, nxt = place("gz", rze[...], rzo[...])
     tiles = [
         own_a,
@@ -337,14 +374,15 @@
         ),
     ]
     h = [t[0:32] for t in tiles]
-    e = [[t[32 * (d + 1) : 32 * (d + 2)] for t in tiles] for d in range(3)]
+    e = [jnp.concatenate([t[32 * (d + 1) : 32 * (d + 2)] for t in tiles], axis=1) for d in range(3)]
     w = [t[128:136] for t in tiles]
-    updated, sums = rim_edges(sizes, h, e, w, win[0], wout[0], column(bias[0:1, :]))
+    messages = batch(win[0], column(bias[0:1, :]), wout[0], rim_groups(sizes, h, e))
+    sums = rim_sums(sizes, messages, w)
     for i in range(4):
         hr_out[:, i * LANES : (i + 1) * LANES] = h[i].astype(BF16)
         wr_out[:, i * LANES : (i + 1) * LANES] = w[i]
     for d in range(3):
-        er_out[d] = updated[d][:, : 4 * LANES].astype(BF16)
+        er_out[d] = (e[d] + messages[d])[:, : 4 * LANES].astype(BF16)
     write_x_faces(sizes, p_ref, sums, sxe, sxo)
     for i in range(4):
         pr_out[:, i * LANES : (i + 1) * LANES] = sums[i]
@@ -353,8 +391,11 @@
 def y_faces(sizes, p_ref, pr_ref, rxe, rxo, sye, syo, pr_out):
     nx, ny = sizes
     low_x, high_x = place("gx", rxe[...], rxo[...])
+    sums = rim_add_x([tile(pr_ref, i) for i in range(4)], tile(low_x, ny), tile(high_x, ny))
+    for i in range(4):
+        pr_out[:, i * LANES : (i + 1) * LANES] = sums[i]
     faces = []
-    for y in (0, ny - 1):
+    for y, rim in zip((0, ny - 1), rim_y_faces(sums)):
         pieces = []
         for x in range(nx):
             t = p_ref[:, (x * ny + y) * LANES : (x * ny + y + 1) * LANES]
@@ -363,17 +404,11 @@
             if x == nx - 1:
                 t = t + tile(high_x, y)
             pieces.append(t)
-        faces.append(jnp.concatenate(pieces, axis=1))
+        faces.append(jnp.concatenate(pieces + [rim], axis=0))
     low, high = faces
-    sums = rim_add_x([tile(pr_ref, i) for i in range(4)], tile(low_x, ny), tile(high_x, ny))
-    packed = rim_y_faces(sums)
-    for i in range(4):
-        pr_out[:, i * LANES : (i + 1) * LANES] = sums[i]
     is_even = lax.axis_index("gy") % 2 == 0
-    sye[:, : nx * LANES] = jnp.where(is_even, high, low)
-    syo[:, : nx * LANES] = jnp.where(is_even, low, high)
-    sye[:, nx * LANES :] = packed
-    syo[:, nx * LANES :] = packed
+    sye[...] = jnp.where(is_even, high, low)
+    syo[...] = jnp.where(is_even, low, high)
 
 
 def incoming(sizes, p_ref, faces_x, faces_y, x, y):
@@ -384,9 +419,9 @@
     if x == nx - 1:
         t = t + tile(faces_x[1], y)
     if y == 0:
-        t = t + tile(faces_y[0], x)
+        t = t + faces_y[0][32 * x : 32 * x + 32]
     if y == ny - 1:
-        t = t + tile(faces_y[1], x)
+        t = t + faces_y[1][32 * x : 32 * x + 32]
     return t.astype(BF16)
 
 
@@ -395,12 +430,13 @@
     faces_x = place("gx", rxe[...], rxo[...])
     w_in, w_out = nin[layer], nout[layer]
     b = column(nbias[layer : layer + 1, :])
+    spans = [span_of(x * ny + 1, ny - 2) for x in range(nx)]
+    groups = []
     for x in range(nx):
         pieces = [incoming(sizes, p_in, faces_x, None, x, y) for y in range(1, ny - 1)]
-        rows = span_of(x * ny + 1, ny - 2)
-        cur = h_in[:, rows]
-        res = perceptron(w_in, b, w_out, [cur, jnp.concatenate(pieces, axis=1)])
-        write(rows, cur.astype(F32) + res)
+        groups.append([h_in[:, spans[x]], jnp.concatenate(pieces, axis=1)])
+    for rows, group, res in zip(spans, groups, batch(w_in, b, w_out, groups)):
+        write(rows, group[0].astype(F32) + res)
 
 
 def outer_nodes(sizes, layer, h_in, p_in, hr_in, pr_in, rxe, rxo, rye, ryo, nin, nout, nbias):
@@ -410,7 +446,7 @@
     w_in, w_out = nin[layer], nout[layer]
     b = column(nbias[layer : layer + 1, :])
     sums = [tile(pr_in, i) for i in range(4)]
-    rim = rim_join_z(rim_add_y(sums, tile(faces_y[0], nx), tile(faces_y[1], nx)))
+    rim = rim_join_z(rim_add_y(sums, faces_y[0][32 * nx :], faces_y[1][32 * nx :]))
     outer = [(x, y) for x in range(nx) for y in (0, ny - 1)]
     cur = jnp.concatenate(
         [hr_in[...]] + [h_in[:, span_of(x * ny + y, 1)] for x, y in outer], axis=1
@@ -467,18 +503,6 @@
     layer += 1
     b = column(bias[layer : layer + 1, :])
     w_in, w_out = win[layer], wout[layer]
-    updated, sums = rim_edges(
-        sizes,
-        [tile(rim_h, i).astype(F32) for i in range(4)],
-        [[tile(er_in[d], i).astype(F32) for i in range(4)] for d in range(3)],
-        [tile(wr_in, i) for i in range(4)],
-        w_in, w_out, b,
-    )
-    for i in range(4):
-        pr_out[:, i * LANES : (i + 1) * LANES] = sums[i]
-    if not last:
-        for d in range(3):
-            er_out[d] = updated[d].astype(BF16)
     zero = jnp.zeros((32, LANES), BF16)
     mine = {place_of: tile(edge_h, i) for i, place_of in enumerate(outer)}
     cross = [(x, y) for x in range(nx) for y in (0, ny - 2, ny - 1)]
@@ -489,16 +513,29 @@
             h_new[:, span_of(x * ny + 1, 1)] if y == 0 else mine[x, ny - 1] if y == ny - 2 else zero
         )
     ahead_x = jnp.concatenate([edge_h[:, 2 * LANES :], zero, zero], axis=1)
-    weighted = []
-    for d, (at, cur, ahead) in enumerate((
+    kinds = (
         (outer, edge_h, ahead_x),
         (cross, jnp.concatenate(from_y, axis=1), jnp.concatenate(to_y, axis=1)),
         (outer, edge_h, ahead_along_z(edge_h)),
-    )):
+    )
+    groups = rim_groups(
+        sizes, [tile(rim_h, i).astype(F32) for i in range(4)], [er_in[d] for d in range(3)]
+    )
+    for d, (at, cur, ahead) in enumerate(kinds):
         edge = jnp.concatenate([e_new[d, :, span_of(x * ny + y, 1)] for x, y in at], axis=1)
-        msg = perceptron(w_in, b, w_out, [cur, ahead, edge])
+        groups.append([cur, ahead, edge])
+    messages = batch(w_in, b, w_out, groups)
+    sums = rim_sums(sizes, messages[:3], [tile(wr_in, i) for i in range(4)])
+    for i in range(4):
+        pr_out[:, i * LANES : (i + 1) * LANES] = sums[i]
+    if not last:
+        for d in range(3):
+            er_out[d] = (er_in[d].astype(F32) + messages[d]).astype(BF16)
+    weighted = []
+    for d, (at, _, _) in enumerate(kinds):
+        msg = messages[3 + d]
         if not last:
-            value = (edge.astype(F32) + msg).astype(BF16)
+            value = (groups[3 + d][2].astype(F32) + msg).astype(BF16)
             for i, (x, y) in enumerate(at):
                 e_out[d, :, span_of(x * ny + y, 1)] = tile(value, i)
         weighted.append(
@@ -585,7 +622,7 @@
     e_t = (e_shape, BF16, "fast")
     w_t = ((rows, 8, nz), F32, "fast")
     sx_t = ((ch, (ny + 1) * nz), F32, "fast")
-    sy_t = ((ch, (nx + 1) * nz), F32, "fast")
+    sy_t = ((ch * nx + ch // 2, nz), F32, "fast")
     hr_t = ((ch, 4 * LANES), BF16, "fast")
     er_t = ((3, ch, 4 * LANES), BF16, "fast")
     wr_t = ((8, 4 * LANES), F32, "fast")
@@ -594,13 +631,13 @@
     sz_t = ((z_rows, LANES), F32, "fast")
     work = 4 * 2 * 5 * 3 * ch * ch * nodes
 
-    h, e0, w, own, sze, szo = call(
+    ends_t = ((2, z_rows, LANES), F32, "fast")
+    buf, w, own, sze, szo = call(
         functools.partial(unpack_kernel, sizes),
         (),
         (features, edge_state, multiplicity),
-        (h_t, e_t, w_t, ((4, z_rows, LANES), F32, "fast"), sz_t, sz_t),
+        (((4, ch * rows, nz), F32, "fast"), w_t, ends_t, sz_t, sz_t),
         (
-            pltpu.VMEM((4, ch * rows, nz), F32),
             pltpu.VMEM(features.shape, BF16),
             pltpu.VMEM(edge_state.shape, BF16),
             pltpu.VMEM(multiplicity.shape, jnp.int32),
@@ -610,12 +647,17 @@
     rze, rzo = exchange(sze, szo, "gz", "gx")
     edge = (edge_in, edge_out, edge_bias)
     node = (node_in, node_out, node_bias)
-    e, p = call(
-        functools.partial(first_edges, sizes), (h, e0, w, *edge), (), (e_t, p_t), flops=work
+    h, e, p, nearby = call(
+        functools.partial(first_edges, sizes),
+        (buf, w, *edge),
+        (),
+        (h_t, e_t, p_t, ends_t),
+        (pltpu.VMEM(e_shape, BF16),),
+        flops=work,
     )
     hr, er, wr, pr, sxe, sxo = call(
         functools.partial(first_rim, sizes),
-        (p, own, rze, rzo, *edge),
+        (p, own, nearby, rze, rzo, *edge),
         (),
         (hr_t, er_t, wr_t, pr_t, sx_t, sx_t),
     )

time: 55.2 us -> 53 us (0.960)
  Pallas kernels: 15.8 us -> 11.1 us
  local copies, waits for them, and re-layouts: 0.69 us -> 2.17 us
    pallas_call x12, Pallas kernels: 15.8 us -> 11.1 us  [call(): pl.pallas_call(body, out_shape=[pltpu.VMEM(s, d) if where == 'fast' else...]
    unnamed x12 -> x16, local copies, waits for them, and re-layouts: 0.69 us -> 2.17 us
    ppermute x7, waiting for transfers between devices: 15.5 us -> 16.4 us  [exchange(): got_odd = lax.ppermute(odd, AXES, odd_pairs(axis, spare))]
    ppermute x7, waiting for transfers between devices: 2.35 us -> 1.56 us  [exchange(): got_even = lax.ppermute(even, axis, even_pairs(lax.axis_size(axis)))]
  transfers between devices with their start and end apart: 14 -> 14, of which waited for: 10 -> 10; matrix products, arithmetic and copies ran while one was open for 0% -> 0% of each run, Pallas kernels for 14% -> 8%
where the time goes in v6:
time: 53 us; the launch traced here: 52.1 us
  starting transfers between devices  20.7 us (39%)
  waiting for transfers between devices  17.9 us (34%)
  Pallas kernels  11.1 us (21%)
  local copies, waits for them, and re-layouts  2.17 us (4%)
    ppermute x7, starting transfers between devices, exchange(): got_odd = lax.ppermute(odd, AXES, odd_pairs(axis, spare))  19 us
    ppermute x7, waiting for transfers between devices, exchange(): got_odd = lax.ppermute(odd, AXES, odd_pairs(axis, spare))  16.4 us
    pallas_call x12, Pallas kernels, call(): pl.pallas_call(body, out_shape=[pltpu.VMEM(s, d) if where == 'fast' else...  11.1 us
    unnamed x16, local copies, waits for them, and re-layouts  2.17 us
    ppermute x7, starting transfers between devices, exchange(): got_even = lax.ppermute(even, axis, even_pairs(lax.axis_size(axis)))  1.71 us
    ppermute x7, waiting for transfers between devices, exchange(): got_even = lax.ppermute(even, axis, even_pairs(lax.axis_size(axis)))  1.56 us
  transfers between devices with their start and end apart: 14, of which 10 were waited for; matrix products, arithmetic and copies ran while one was open for 0% of the time, Pallas kernels for 8%

profile of v6, /device:TPU:68, one launch (start us, length us, event | category | flops | bytes accessed | tf_op | source)
XLA Modules:
  0.0 52.1 jit_solution(1108706875602444896)
XLA Ops:
  0.0 2.0 %shard_map.91 = (f32[4,768,128]{2,1,0:T(8,128)S(1)}, f32[24,8,128]{2,1,0:T(8,128)S(1)}, f32[2,136,128]{2,1,0:T(8,128)S(1)}, f32[136,128]{1,0:T(8,128)S(1)}, f32[136,128]{1,0:T(8,128)S(1)}) custom-call(bf16[32,3,8,128]{3,2,1,0:T(8,128)(2,1)} %f_in.1, bf16[3,32,3,8,128]{4,3,2,1,0:T(8,128)(2,1)} %es_in.1, s32[3,8,128]{2,1,0:T(8,128)} %m_in.1), custom_call_target="tpu_custom_call" | custom-call | tf_op jit(solution)/shard_map/pallas_call | solution.py:596
  2.0 1.3 %collective-permute-start = (f32[136,128]{1,0:T(8,128)S(1)}, f32[136,128]{1,0:T(8,128)S(1)}, u32[]{:S(2)}, u32[]{:S(2)}) collective-permute-start(f32[136,128]{1,0:T(8,128)S(1)} %get-tuple-element.57), channel_id=1, source_target_pairs={{0,1},{1,0},{2,3},{3,2},{4,5},{5,4},{6,7},{7,6},{8,9},{9,8},{10,11... | collective-permute-start | bytes 208904 | tf_op jit(solution)/shard_map/ppermute | solution.py:41
  3.3 0.0 collective-permute-start.1
  3.3 0.7 %copy-done = bf16[3,32,96]{2,1,0:T(8,128)(2,1)S(1)} copy-done((bf16[3,32,96]{2,1,0:T(8,128)(2,1)S(1)}, bf16[3,32,96]{2,1,0:T(8,128)(2,1)}, u32[]{:S(2)}) %copy-start) | copy-done | bytes 18456
  4.1 0.7 %copy-done.2 = bf16[3,32,32]{2,1,0:T(8,128)(2,1)S(1)} copy-done((bf16[3,32,32]{2,1,0:T(8,128)(2,1)S(1)}, bf16[3,32,32]{2,1,0:T(8,128)(2,1)}, u32[]{:S(2)}) %copy-start.2) | copy-done | bytes 6168
  4.8 0.7 %copy-done.5 = f32[3,32]{1,0:T(4,128)S(1)} copy-done((f32[3,32]{1,0:T(4,128)S(1)}, f32[3,32]{1,0:T(4,128)}, u32[]{:S(2)}) %copy-start.5) | copy-done | bytes 408
  5.5 1.4 %shard_map.92 = (bf16[32,3072]{1,0:T(8,128)(2,1)S(1)}, bf16[3,32,3072]{2,1,0:T(8,128)(2,1)S(1)}, f32[32,3072]{1,0:T(8,128)S(1)}, f32[2,136,128]{2,1,0:T(8,128)S(1)}) custom-call(f32[4,768,128]{2,1,0:T(8,128)S(1)} %get-tuple-element.51.buf, f32[24,8,128]{2,1,0:T(8,128)S(1)} %get-tuple-element.52.w_ref.w_in, bf16[3,32,96]{2,1,0:T(8,128)(2,1)S(1)} %copy-done, ...), custom_call_target="tpu_custom_call" | custom-call | flops 377487360 | tf_op jit(solution)/shard_map/pallas_call | solution.py:596
  6.9 0.0 collective-permute-done.rze
  6.9 0.7 %collective-permute-done.1.rzo = f32[136,128]{1,0:T(8,128)S(1)} collective-permute-done((f32[136,128]{1,0:T(8,128)S(1)}, f32[136,128]{1,0:T(8,128)S(1)}, u32[]{:S(2)}, u32[]{:S(2)}) %collective-permute-start.1) | collective-permute-done | bytes 69664 | tf_op jit(solution)/shard_map/ppermute | solution.py:40
  7.6 0.6 %shard_map.93 = (bf16[32,512]{1,0:T(8,128)(2,1)S(1)}, bf16[3,32,512]{2,1,0:T(8,128)(2,1)S(1)}, f32[8,512]{1,0:T(8,128)S(1)}, f32[32,512]{1,0:T(8,128)S(1)}, f32[...) custom-call(f32[32,3072]{1,0:T(8,128)S(1)} %get-tuple-element.54.p_ref.p_in, f32[2,136,128]{2,1,0:T(8,128)S(1)} %get-tuple-element.55.own_ref, ...), custom_call_target="tpu_custom_call" | custom-call | tf_op jit(solution)/shard_map/pallas_call | solution.py:596
  8.3 0.1 collective-permute-start.2
  8.4 3.0 %collective-permute-start.3 = (f32[32,1152]{1,0:T(8,128)S(1)}, f32[32,1152]{1,0:T(8,128)S(1)}, u32[]{:S(2)}, u32[]{:S(2)}) collective-permute-start(f32[32,1152]{1,0:T(8,128)S(1)} %get-tuple-element.64), channel_id=1, source_target_pairs={{0,1},{1,0},{2,3},{3,2},{4,5},{5,4},{6,7},{7,6},{8,9},{9,8},{10,11... | collective-permute-start | bytes 442376 | tf_op jit(solution)/shard_map/ppermute | solution.py:40
  11.4 0.0 collective-permute-done.2.rxe
  11.4 3.1 %collective-permute-done.3.rxo = f32[32,1152]{1,0:T(8,128)S(1)} collective-permute-done((f32[32,1152]{1,0:T(8,128)S(1)}, f32[32,1152]{1,0:T(8,128)S(1)}, u32[]{:S(2)}, u32[]{:S(2)}) %collective-permute-start.3) | collective-permute-done | bytes 147488 | tf_op jit(solution)/shard_map/ppermute | solution.py:40
  14.5 0.2 shard_map.94
  14.7 0.0 collective-permute-start.4
  14.8 5.9 %collective-permute-start.5 = (f32[112,128]{1,0:T(8,128)S(1)}, f32[112,128]{1,0:T(8,128)S(1)}, u32[]{:S(2)}, u32[]{:S(2)}) collective-permute-start(f32[112,128]{1,0:T(8,128)S(1)} %get-tuple-element.67), channel_id=1, source_target_pairs={{0,32},{1,33},{2,34},{3,35},{4,36},{5,37},{6,38},{7,39},{8,16},{9,... | collective-permute-start | bytes 172040 | tf_op jit(solution)/shard_map/ppermute | solution.py:40
  20.7 0.0 copy-done.3
  20.7 0.0 copy-done.4
  20.7 0.0 copy-done.7
  20.7 1.2 %shard_map.95 = (bf16[32,3072]{1,0:T(8,128)(2,1)S(1)}, f32[32,3072]{1,0:T(8,128)S(1)}, bf16[3,32,3072]{2,1,0:T(8,128)(2,1)S(1)}, f32[24,8,128]{2,1,0:T(8,128)S(1)}) custom-call(bf16[32,3072]{1,0:T(8,128)(2,1)S(1)} %get-tuple-element.53.h_in, f32[32,3072]{1,0:T(8,128)S(1)} %get-tuple-element.54.p_ref.p_in, f32[32,1152]{1,0:T(8,128)S(1)} %collective-permute-done.2.rxe, ...), custom_call_target="tpu_custom_call" | custom-call | flops 377487360 | tf_op jit(solution)/shard_map/pallas_call | solution.py:596
  21.9 0.0 collective-permute-done.4.rye
  22.0 1.4 %collective-permute-done.5.ryo = f32[112,128]{1,0:T(8,128)S(1)} collective-permute-done((f32[112,128]{1,0:T(8,128)S(1)}, f32[112,128]{1,0:T(8,128)S(1)}, u32[]{:S(2)}, u32[]{:S(2)}) %collective-permute-start.5) | collective-permute-done | bytes 57376 | tf_op jit(solution)/shard_map/ppermute | solution.py:40
  23.3 0.0 copy-done.1
  23.3 0.0 copy-done.6
  23.3 1.1 %shard_map.96 = (bf16[32,3072]{1,0:T(8,128)(2,1)S(1)}, f32[32,3072]{1,0:T(8,128)S(1)}, bf16[3,32,3072]{2,1,0:T(8,128)(2,1)S(1)}, bf16[32,512]{1,0:T(8,128)(2,1)S...) custom-call(bf16[32,3072]{1,0:T(8,128)(2,1)S(1)} %get-tuple-element., ...), custom_call_target="tpu_custom_call", output_to_operand_aliasing={{0}: (17, {}), {1}: (18, {}), {2}: (19, {})} | custom-call | tf_op jit(solution)/shard_map/pallas_call | solution.py:596
  24.5 0.1 collective-permute-start.6
  24.6 1.7 %collective-permute-start.7 = (f32[32,1152]{1,0:T(8,128)S(1)}, f32[32,1152]{1,0:T(8,128)S(1)}, u32[]{:S(2)}, u32[]{:S(2)}) collective-permute-start(f32[32,1152]{1,0:T(8,128)S(1)} %get-tuple-element.79), channel_id=1, source_target_pairs={{0,1},{1,0},{2,3},{3,2},{4,5},{5,4},{6,7},{7,6},{8,9},{9,8},{10,11... | collective-permute-start | bytes 442376 | tf_op jit(solution)/shard_map/ppermute | solution.py:40
  26.2 0.0 collective-permute-done.6.rxe
  26.2 3.6 %collective-permute-done.7.rxo = f32[32,1152]{1,0:T(8,128)S(1)} collective-permute-done((f32[32,1152]{1,0:T(8,128)S(1)}, f32[32,1152]{1,0:T(8,128)S(1)}, u32[]{:S(2)}, u32[]{:S(2)}) %collective-permute-start.7) | collective-permute-done | bytes 147488 | tf_op jit(solution)/shard_map/ppermute | solution.py:40
  29.8 0.2 shard_map.97
  30.0 0.0 collective-permute-start.8
  30.1 3.8 %collective-permute-start.9 = (f32[112,128]{1,0:T(8,128)S(1)}, f32[112,128]{1,0:T(8,128)S(1)}, u32[]{:S(2)}, u32[]{:S(2)}) collective-permute-start(f32[112,128]{1,0:T(8,128)S(1)} %get-tuple-element.82), channel_id=1, source_target_pairs={{0,32},{1,33},{2,34},{3,35},{4,36},{5,37},{6,38},{7,39},{8,16},{9,... | collective-permute-start | bytes 172040 | tf_op jit(solution)/shard_map/ppermute | solution.py:40
  33.9 1.2 %shard_map.98 = (bf16[32,3072]{1,0:T(8,128)(2,1)S(1)}, f32[32,3072]{1,0:T(8,128)S(1)}, bf16[3,32,3072]{2,1,0:T(8,128)(2,1)S(1)}, f32[24,8,128]{2,1,0:T(8,128)S(1)}) custom-call(bf16[32,3072]{1,0:T(8,128)(2,1)S(1)} %get-tuple-element.73.h_in, f32[32,3072]{1,0:T(8,128)S(1)} %get-tuple-element.74.p_ref.p_in, f32[32,1152]{1,0:T(8,128)S(1)} %collective-permute-done.6.rxe, ...), custom_call_target="tpu_custom_call" | custom-call | flops 377487360 | tf_op jit(solution)/shard_map/pallas_call | solution.py:596
  35.1 0.1 collective-permute-done.8.rye
  35.2 1.8 %collective-permute-done.9.ryo = f32[112,128]{1,0:T(8,128)S(1)} collective-permute-done((f32[112,128]{1,0:T(8,128)S(1)}, f32[112,128]{1,0:T(8,128)S(1)}, u32[]{:S(2)}, u32[]{:S(2)}) %collective-permute-start.9) | collective-permute-done | bytes 57376 | tf_op jit(solution)/shard_map/ppermute | solution.py:40
  36.9 1.1 %shard_map.99 = (bf16[32,3072]{1,0:T(8,128)(2,1)S(1)}, f32[32,3072]{1,0:T(8,128)S(1)}, bf16[32,512]{1,0:T(8,128)(2,1)S(1)}, f32[32,512]{1,0:T(8,128)S(1)}, f32[3...) custom-call(bf16[32,3072]{1,0:T(8,128)(2,1)S(1)} %get-tuple-element.73.h_in, ...), custom_call_target="tpu_custom_call", output_to_operand_aliasing={{0}: (17, {}), {1}: (18, {})} | custom-call | tf_op jit(solution)/shard_map/pallas_call | solution.py:596
  38.0 0.1 collective-permute-start.10
  38.1 1.3 %collective-permute-start.11 = (f32[32,1152]{1,0:T(8,128)S(1)}, f32[32,1152]{1,0:T(8,128)S(1)}, u32[]{:S(2)}, u32[]{:S(2)}) collective-permute-start(f32[32,1152]{1,0:T(8,128)S(1)} %get-tuple-element.93), channel_id=1, source_target_pairs={{0,1},{1,0},{2,3},{3,2},{4,5},{5,4},{6,7},{7,6},{8,9},{9,8},{10,11... | collective-permute-start | bytes 442376 | tf_op jit(solution)/shard_map/ppermute | solution.py:40
  39.4 0.1 collective-permute-done.10.rxe
  39.5 3.9 %collective-permute-done.11.rxo = f32[32,1152]{1,0:T(8,128)S(1)} collective-permute-done((f32[32,1152]{1,0:T(8,128)S(1)}, f32[32,1152]{1,0:T(8,128)S(1)}, u32[]{:S(2)}, u32[]{:S(2)}) %collective-permute-start.11) | collective-permute-done | bytes 147488 | tf_op jit(solution)/shard_map/ppermute | solution.py:40
  43.3 0.2 shard_map.100
  43.6 0.0 collective-permute-start.12
  43.6 3.3 %collective-permute-start.13 = (f32[112,128]{1,0:T(8,128)S(1)}, f32[112,128]{1,0:T(8,128)S(1)}, u32[]{:S(2)}, u32[]{:S(2)}) collective-permute-start(f32[112,128]{1,0:T(8,128)S(1)} %get-tuple-element.96), channel_id=1, source_target_pairs={{0,32},{1,33},{2,34},{3,35},{4,36},{5,37},{6,38},{7,39},{8,16},{9,... | collective-permute-start | bytes 172040 | tf_op jit(solution)/shard_map/ppermute | solution.py:40
  47.0 0.4 shard_map.101.res
  47.3 1.4 %collective-permute-done.12.rye = f32[112,128]{1,0:T(8,128)S(1)} collective-permute-done((f32[112,128]{1,0:T(8,128)S(1)}, f32[112,128]{1,0:T(8,128)S(1)}, u32[]{:S(2)}, u32[]{:S(2)}) %collective-permute-start.12) | collective-permute-done | bytes 57376 | tf_op jit(solution)/shard_map/ppermute | solution.py:41
  48.7 1.9 %collective-permute-done.13.ryo = f32[112,128]{1,0:T(8,128)S(1)} collective-permute-done((f32[112,128]{1,0:T(8,128)S(1)}, f32[112,128]{1,0:T(8,128)S(1)}, u32[]{:S(2)}, u32[]{:S(2)}) %collective-permute-start.13) | collective-permute-done | bytes 57376 | tf_op jit(solution)/shard_map/ppermute | solution.py:40
  50.6 1.5 %shard_map.102 = bf16[32,3,8,128]{3,2,1,0:T(8,128)(2,1)} custom-call(bf16[32,3072]{1,0:T(8,128)(2,1)S(1)} %get-tuple-element.88.h_in, f32[32,3072]{1,0:T(8,128)S(1)} %get-tuple-element.89.p_ref.p_in, bf16[32,512]{1,0:T(8,128)(2,1)S(1)} %get-tuple-element.90.hr_in, f32[32,512]{1,0:T(8,128)S(1)} %get-tuple-element.94.pr_in, ...), custom_call_target="tpu_custom_call" | custom-call | tf_op jit(solution)/shard_map/pallas_call | solution.py:596
  (8 shorter events, 0.0 us)
Async XLA Ops:
  2.0 4.8 %collective-permute-start = (f32[136,128]{1,0:T(8,128)S(1)}, f32[136,128]{1,0:T(8,128)S(1)}, u32[]{:S(2)}, u32[]{:S(2)}) collective-permute-start(f32[136,128]{1,0:T(8,128)S(1)} %get-tuple-element.57), channel_id=1, source_target_pairs={{0,1},{1,0},{2,3},{3,2},{4,5},{5,4},{6,7},{7,6},{8,9},{9,8},{10,11... | collective-permute-start | bytes 208904 | tf_op jit(solution)/shard_map/ppermute | solution.py:41
  3.3 4.3 %collective-permute-start.1 = (f32[136,128]{1,0:T(8,128)S(1)}, f32[136,128]{1,0:T(8,128)S(1)}, u32[]{:S(2)}, u32[]{:S(2)}) collective-permute-start(f32[136,128]{1,0:T(8,128)S(1)} %get-tuple-element.58), channel_id=1, source_target_pairs={{0,32},{1,2},{2,1},{3,4},{4,3},{5,6},{6,5},{7,39},{8,40},{9,10},{1... | collective-permute-start | bytes 208904 | tf_op jit(solution)/shard_map/ppermute | solution.py:40
  3.3 0.7 %copy-start = (bf16[3,32,96]{2,1,0:T(8,128)(2,1)S(1)}, bf16[3,32,96]{2,1,0:T(8,128)(2,1)}, u32[]{:S(2)}) copy-start(bf16[3,32,96]{2,1,0:T(8,128)(2,1)} %win.11) | copy-start | bytes 55300
  4.0 0.7 %copy-start.2 = (bf16[3,32,32]{2,1,0:T(8,128)(2,1)S(1)}, bf16[3,32,32]{2,1,0:T(8,128)(2,1)}, u32[]{:S(2)}) copy-start(bf16[3,32,32]{2,1,0:T(8,128)(2,1)} %wout.11) | copy-start | bytes 18436
  4.8 0.7 %copy-start.5 = (f32[3,32]{1,0:T(4,128)S(1)}, f32[3,32]{1,0:T(4,128)}, u32[]{:S(2)}) copy-start(f32[3,32]{1,0:T(4,128)} %bias.11) | copy-start | bytes 1156
  5.5 15.3 %copy-start.3 = (bf16[3,32,64]{2,1,0:T(8,128)(2,1)S(1)}, bf16[3,32,64]{2,1,0:T(8,128)(2,1)}, u32[]{:S(2)}) copy-start(bf16[3,32,64]{2,1,0:T(8,128)(2,1)} %nin.11) | copy-start | bytes 36868
  5.5 15.3 %copy-start.4 = (bf16[3,32,32]{2,1,0:T(8,128)(2,1)S(1)}, bf16[3,32,32]{2,1,0:T(8,128)(2,1)}, u32[]{:S(2)}) copy-start(bf16[3,32,32]{2,1,0:T(8,128)(2,1)} %nout.11) | copy-start | bytes 18436
  5.5 15.3 %copy-start.7 = (f32[3,32]{1,0:T(4,128)S(1)}, f32[3,32]{1,0:T(4,128)}, u32[]{:S(2)}) copy-start(f32[3,32]{1,0:T(4,128)} %nbias.11) | copy-start | bytes 1156
  7.6 15.7 %copy-start.1 = (bf16[3,32,96]{2,1,0:T(8,128)(2,1)S(1)}, bf16[3,32,96]{2,1,0:T(8,128)(2,1)}, u32[]{:S(2)}) copy-start(bf16[3,32,96]{2,1,0:T(8,128)(2,1)} %win.11) | copy-start | bytes 55300
  7.6 15.7 %copy-start.6 = (f32[3,32]{1,0:T(4,128)S(1)}, f32[3,32]{1,0:T(4,128)}, u32[]{:S(2)}) copy-start(f32[3,32]{1,0:T(4,128)} %bias.11) | copy-start | bytes 1156
  8.3 3.1 %collective-permute-start.2 = (f32[32,1152]{1,0:T(8,128)S(1)}, f32[32,1152]{1,0:T(8,128)S(1)}, u32[]{:S(2)}, u32[]{:S(2)}) collective-permute-start(f32[32,1152]{1,0:T(8,128)S(1)} %get-tuple-element.63), channel_id=1, source_target_pairs={{0,32},{32,0},{64,96},{96,64},{128,160},{160,128},{192,224},{224,1... | collective-permute-start | bytes 442376 | tf_op jit(solution)/shard_map/ppermute | solution.py:41
  8.4 6.1 %collective-permute-start.3 = (f32[32,1152]{1,0:T(8,128)S(1)}, f32[32,1152]{1,0:T(8,128)S(1)}, u32[]{:S(2)}, u32[]{:S(2)}) collective-permute-start(f32[32,1152]{1,0:T(8,128)S(1)} %get-tuple-element.64), channel_id=1, source_target_pairs={{0,1},{1,0},{2,3},{3,2},{4,5},{5,4},{6,7},{7,6},{8,9},{9,8},{10,11... | collective-permute-start | bytes 442376 | tf_op jit(solution)/shard_map/ppermute | solution.py:40
  14.7 7.2 %collective-permute-start.4 = (f32[112,128]{1,0:T(8,128)S(1)}, f32[112,128]{1,0:T(8,128)S(1)}, u32[]{:S(2)}, u32[]{:S(2)}) collective-permute-start(f32[112,128]{1,0:T(8,128)S(1)} %get-tuple-element.66), channel_id=1, source_target_pairs={{0,8},{8,0},{16,24},{24,16},{1,9},{9,1},{17,25},{25,17},{2,10},{10... | collective-permute-start | bytes 172040 | tf_op jit(solution)/shard_map/ppermute | solution.py:41
  14.8 8.5 %collective-permute-start.5 = (f32[112,128]{1,0:T(8,128)S(1)}, f32[112,128]{1,0:T(8,128)S(1)}, u32[]{:S(2)}, u32[]{:S(2)}) collective-permute-start(f32[112,128]{1,0:T(8,128)S(1)} %get-tuple-element.67), channel_id=1, source_target_pairs={{0,32},{1,33},{2,34},{3,35},{4,36},{5,37},{6,38},{7,39},{8,16},{9,... | collective-permute-start | bytes 172040 | tf_op jit(solution)/shard_map/ppermute | solution.py:40
  24.5 1.8 %collective-permute-start.6 = (f32[32,1152]{1,0:T(8,128)S(1)}, f32[32,1152]{1,0:T(8,128)S(1)}, u32[]{:S(2)}, u32[]{:S(2)}) collective-permute-start(f32[32,1152]{1,0:T(8,128)S(1)} %get-tuple-element.78), channel_id=1, source_target_pairs={{0,32},{32,0},{64,96},{96,64},{128,160},{160,128},{192,224},{224,1... | collective-permute-start | bytes 442376 | tf_op jit(solution)/shard_map/ppermute | solution.py:41
  24.6 5.2 %collective-permute-start.7 = (f32[32,1152]{1,0:T(8,128)S(1)}, f32[32,1152]{1,0:T(8,128)S(1)}, u32[]{:S(2)}, u32[]{:S(2)}) collective-permute-start(f32[32,1152]{1,0:T(8,128)S(1)} %get-tuple-element.79), channel_id=1, source_target_pairs={{0,1},{1,0},{2,3},{3,2},{4,5},{5,4},{6,7},{7,6},{8,9},{9,8},{10,11... | collective-permute-start | bytes 442376 | tf_op jit(solution)/shard_map/ppermute | solution.py:40
  30.0 5.1 %collective-permute-start.8 = (f32[112,128]{1,0:T(8,128)S(1)}, f32[112,128]{1,0:T(8,128)S(1)}, u32[]{:S(2)}, u32[]{:S(2)}) collective-permute-start(f32[112,128]{1,0:T(8,128)S(1)} %get-tuple-element.81), channel_id=1, source_target_pairs={{0,8},{8,0},{16,24},{24,16},{1,9},{9,1},{17,25},{25,17},{2,10},{10... | collective-permute-start | bytes 172040 | tf_op jit(solution)/shard_map/ppermute | solution.py:41
  30.1 6.8 %collective-permute-start.9 = (f32[112,128]{1,0:T(8,128)S(1)}, f32[112,128]{1,0:T(8,128)S(1)}, u32[]{:S(2)}, u32[]{:S(2)}) collective-permute-start(f32[112,128]{1,0:T(8,128)S(1)} %get-tuple-element.82), channel_id=1, source_target_pairs={{0,32},{1,33},{2,34},{3,35},{4,36},{5,37},{6,38},{7,39},{8,16},{9,... | collective-permute-start | bytes 172040 | tf_op jit(solution)/shard_map/ppermute | solution.py:40
  38.0 1.5 %collective-permute-start.10 = (f32[32,1152]{1,0:T(8,128)S(1)}, f32[32,1152]{1,0:T(8,128)S(1)}, u32[]{:S(2)}, u32[]{:S(2)}) collective-permute-start(f32[32,1152]{1,0:T(8,128)S(1)} %get-tuple-element.92), channel_id=1, source_target_pairs={{0,32},{32,0},{64,96},{96,64},{128,160},{160,128},{192,224},{224,1... | collective-permute-start | bytes 442376 | tf_op jit(solution)/shard_map/ppermute | solution.py:41
  38.1 5.2 %collective-permute-start.11 = (f32[32,1152]{1,0:T(8,128)S(1)}, f32[32,1152]{1,0:T(8,128)S(1)}, u32[]{:S(2)}, u32[]{:S(2)}) collective-permute-start(f32[32,1152]{1,0:T(8,128)S(1)} %get-tuple-element.93), channel_id=1, source_target_pairs={{0,1},{1,0},{2,3},{3,2},{4,5},{5,4},{6,7},{7,6},{8,9},{9,8},{10,11... | collective-permute-start | bytes 442376 | tf_op jit(solution)/shard_map/ppermute | solution.py:40
  43.6 5.1 %collective-permute-start.12 = (f32[112,128]{1,0:T(8,128)S(1)}, f32[112,128]{1,0:T(8,128)S(1)}, u32[]{:S(2)}, u32[]{:S(2)}) collective-permute-start(f32[112,128]{1,0:T(8,128)S(1)} %get-tuple-element.95), channel_id=1, source_target_pairs={{0,8},{8,0},{16,24},{24,16},{1,9},{9,1},{17,25},{25,17},{2,10},{10... | collective-permute-start | bytes 172040 | tf_op jit(solution)/shard_map/ppermute | solution.py:41
  43.6 7.0 %collective-permute-start.13 = (f32[112,128]{1,0:T(8,128)S(1)}, f32[112,128]{1,0:T(8,128)S(1)}, u32[]{:S(2)}, u32[]{:S(2)}) collective-permute-start(f32[112,128]{1,0:T(8,128)S(1)} %get-tuple-element.96), channel_id=1, source_target_pairs={{0,32},{1,33},{2,34},{3,35},{4,36},{5,37},{6,38},{7,39},{8,16},{9,... | collective-permute-start | bytes 172040 | tf_op jit(solution)/shard_map/ppermute | solution.py:40

commit v7 on v6

--- a/solution.py
+++ b/solution.py
@@ -36,10 +36,16 @@
     return pairs
 
 
+def send_even(values, axis):
+    return lax.ppermute(values, axis, even_pairs(lax.axis_size(axis)))
+
+
+def send_odd(values, axis, spare):
+    return lax.ppermute(values, AXES, odd_pairs(axis, spare))
+
+
 def exchange(even, odd, axis, spare):
-    got_odd = lax.ppermute(odd, AXES, odd_pairs(axis, spare))
-    got_even = lax.ppermute(even, axis, even_pairs(lax.axis_size(axis)))
-    return got_even, got_odd
+    return send_even(even, axis), send_odd(odd, axis, spare)
 
 
 def silu(v):
@@ -251,25 +257,33 @@
         prev_x = wx
 
 
-def write_x_faces(sizes, p_ref, sums, sxe, sxo):
+def write_x_faces(sizes, p_ref, sums, sxe, sxa, sxb):
     nx, ny = sizes
     span = ny * LANES
     low_rim, high_rim = rim_x_faces(sums)
     is_even = lax.axis_index("gx") % 2 == 0
     sxe[:, span:] = jnp.where(is_even, high_rim, low_rim)
-    sxo[:, span:] = jnp.where(is_even, low_rim, high_rim)
-    low = slice(0, span)
-    high = slice((nx - 1) * span, nx * span)
+    sxa[:, 2 * LANES :] = jnp.where(is_even, low_rim, high_rim)
+    low, high = 0, (nx - 1) * ny
+
+    def odd(first):
+        sxa[:, :LANES] = p_ref[:, span_of(first, 1)]
+        sxa[:, LANES : 2 * LANES] = p_ref[:, span_of(first + ny - 1, 1)]
+        sxb[...] = p_ref[:, span_of(first + 1, ny - 2)]
 
     @pl.when(is_even)
     def _():
-        sxe[:, :span] = p_ref[:, high]
-        sxo[:, :span] = p_ref[:, low]
+        sxe[:, :span] = p_ref[:, span_of(high, ny)]
+        odd(low)
 
     @pl.when(jnp.logical_not(is_even))
     def _():
-        sxe[:, :span] = p_ref[:, low]
-        sxo[:, :span] = p_ref[:, high]
+        sxe[:, :span] = p_ref[:, span_of(low, ny)]
+        odd(high)
+
+
+def outer_x(ny, rxe, rxa, y):
+    return place("gx", tile(rxe, y), tile(rxa, {0: 0, ny - 1: 1, ny: 2}[y]))
 
 
 ENDS = ((-1, 4), (0, 0))
@@ -356,7 +370,7 @@
 
 
 def first_rim(
-    sizes, p_ref, own_ref, next_ref, rze, rzo, win, wout, bias, hr_out, er_out, wr_out, pr_out, sxe, sxo
+    sizes, p_ref, own_ref, next_ref, rze, rzo, win, wout, bias, hr_out, er_out, wr_out, pr_out, sxe, sxa, sxb
 ):
     at = lanes_of(own_ref.shape[1]) % 4
     own_a, own_b = own_ref[0], own_ref[1]
@@ -383,26 +397,26 @@
         wr_out[:, i * LANES : (i + 1) * LANES] = w[i]
     for d in range(3):
         er_out[d] = (e[d] + messages[d])[:, : 4 * LANES].astype(BF16)
-    write_x_faces(sizes, p_ref, sums, sxe, sxo)
+    write_x_faces(sizes, p_ref, sums, sxe, sxa, sxb)
     for i in range(4):
         pr_out[:, i * LANES : (i + 1) * LANES] = sums[i]
 
 
-def y_faces(sizes, p_ref, pr_ref, rxe, rxo, sye, syo, pr_out):
-    nx, ny = sizes
-    low_x, high_x = place("gx", rxe[...], rxo[...])
-    sums = rim_add_x([tile(pr_ref, i) for i in range(4)], tile(low_x, ny), tile(high_x, ny))
+def y_faces(sizes, p_ref, pr_ref, rxe, rxa, sye, syo, pr_out):
+    nx, ny = sizes
+    sums = rim_add_x([tile(pr_ref, i) for i in range(4)], *outer_x(ny, rxe, rxa, ny))
     for i in range(4):
         pr_out[:, i * LANES : (i + 1) * LANES] = sums[i]
     faces = []
     for y, rim in zip((0, ny - 1), rim_y_faces(sums)):
+        low_x, high_x = outer_x(ny, rxe, rxa, y)
         pieces = []
         for x in range(nx):
-            t = p_ref[:, (x * ny + y) * LANES : (x * ny + y + 1) * LANES]
+            t = p_ref[:, span_of(x * ny + y, 1)]
             if x == 0:
-                t = t + tile(low_x, y)
+                t = t + low_x
             if x == nx - 1:
-                t = t + tile(high_x, y)
+                t = t + high_x
             pieces.append(t)
         faces.append(jnp.concatenate(pieces + [rim], axis=0))
     low, high = faces
@@ -415,9 +429,9 @@
     nx, ny = sizes
     t = p_ref[:, span_of(x * ny + y, 1)]
     if x == 0:
-        t = t + tile(faces_x[0], y)
+        t = t + faces_x[y][0]
     if x == nx - 1:
-        t = t + tile(faces_x[1], y)
+        t = t + faces_x[y][1]
     if y == 0:
         t = t + faces_y[0][32 * x : 32 * x + 32]
     if y == ny - 1:
@@ -425,9 +439,9 @@
     return t.astype(BF16)
 
 
-def inner_nodes(sizes, layer, h_in, p_in, rxe, rxo, nin, nout, nbias, write):
-    nx, ny = sizes
-    faces_x = place("gx", rxe[...], rxo[...])
+def inner_nodes(sizes, layer, h_in, p_in, rxe, rxb, nin, nout, nbias, write):
+    nx, ny = sizes
+    faces_x = {y: place("gx", tile(rxe, y), tile(rxb, y - 1)) for y in range(1, ny - 1)}
     w_in, w_out = nin[layer], nout[layer]
     b = column(nbias[layer : layer + 1, :])
     spans = [span_of(x * ny + 1, ny - 2) for x in range(nx)]
@@ -439,9 +453,9 @@
         write(rows, group[0].astype(F32) + res)
 
 
-def outer_nodes(sizes, layer, h_in, p_in, hr_in, pr_in, rxe, rxo, rye, ryo, nin, nout, nbias):
-    nx, ny = sizes
-    faces_x = place("gx", rxe[...], rxo[...])
+def outer_nodes(sizes, layer, h_in, p_in, hr_in, pr_in, rxe, rxa, rye, ryo, nin, nout, nbias):
+    nx, ny = sizes
+    faces_x = {y: outer_x(ny, rxe, rxa, y) for y in (0, ny - 1)}
     faces_y = place("gy", rye[...], ryo[...])
     w_in, w_out = nin[layer], nout[layer]
     b = column(nbias[layer : layer + 1, :])
@@ -461,7 +475,7 @@
 
 
 def inner_kernel(
-    sizes, layer, last, h_in, p_in, rxe, rxo, nin, nout, nbias, win, wout, bias, e_in, w_in,
+    sizes, layer, last, h_in, p_in, rxe, rxb, nin, nout, nbias, win, wout, bias, e_in, w_in,
     h_out, p_out, e_out, w_out, sems,
 ):
     ny = sizes[1]
@@ -473,7 +487,7 @@
     def write(rows, value):
         h_out[:, rows] = value.astype(BF16)
 
-    inner_nodes(sizes, layer, h_in, p_in, rxe, rxo, nin, nout, nbias, write)
+    inner_nodes(sizes, layer, h_in, p_in, rxe, rxb, nin, nout, nbias, write)
     layer += 1
     fetch_e.wait()
     fetch_w.wait()
@@ -484,16 +498,16 @@
 
 
 def outer_kernel(
-    sizes, layer, last, h_in, p_in, hr_in, er_in, wr_in, pr_in, rxe, rxo, rye, ryo, nin, nout, nbias,
+    sizes, layer, last, h_in, p_in, hr_in, er_in, wr_in, pr_in, rxe, rxa, rye, ryo, nin, nout, nbias,
     win, wout, bias, w_ref, h_new, p_new, e_new, *outs,
 ):
     nx, ny = sizes
     if last:
-        h_out, p_out, hr_out, pr_out, sxe, sxo = outs
+        h_out, p_out, hr_out, pr_out, sxe, sxa, sxb = outs
     else:
-        h_out, p_out, e_out, hr_out, er_out, pr_out, sxe, sxo = outs
+        h_out, p_out, e_out, hr_out, er_out, pr_out, sxe, sxa, sxb = outs
     rim_h, edge_h = outer_nodes(
-        sizes, layer, h_in, p_in, hr_in, pr_in, rxe, rxo, rye, ryo, nin, nout, nbias
+        sizes, layer, h_in, p_in, hr_in, pr_in, rxe, rxa, rye, ryo, nin, nout, nbias
     )
     rim_h, edge_h = rim_h.astype(BF16), edge_h.astype(BF16)
     hr_out[...] = rim_h
@@ -555,23 +569,23 @@
             p_out[:, span_of(x * ny + y, 1)] = acc
         for y, add in ((1, wy[x, 0]), (ny - 2, wy[x, ny - 2])):
             p_out[:, span_of(x * ny + y, 1)] = p_new[:, span_of(x * ny + y, 1)] + add
-    write_x_faces(sizes, p_out, sums, sxe, sxo)
-
-
-def last_inner(sizes, layer, h_in, p_in, rxe, rxo, nin, nout, nbias, res):
+    write_x_faces(sizes, p_out, sums, sxe, sxa, sxb)
+
+
+def last_inner(sizes, layer, h_in, p_in, rxe, rxb, nin, nout, nbias, res):
     def write(rows, value):
         res[:, rows] = value
 
-    inner_nodes(sizes, layer, h_in, p_in, rxe, rxo, nin, nout, nbias, write)
+    inner_nodes(sizes, layer, h_in, p_in, rxe, rxb, nin, nout, nbias, write)
 
 
 def last_kernel(
-    sizes, layer, h_in, p_in, hr_in, pr_in, rxe, rxo, rye, ryo, nin, nout, nbias, res, out, buf
+    sizes, layer, h_in, p_in, hr_in, pr_in, rxe, rxa, rye, ryo, nin, nout, nbias, res, out, buf
 ):
     nx, ny = sizes
     rows = nx * ny
     rim_h, edge_h = outer_nodes(
-        sizes, layer, h_in, p_in, hr_in, pr_in, rxe, rxo, rye, ryo, nin, nout, nbias
+        sizes, layer, h_in, p_in, hr_in, pr_in, rxe, rxa, rye, ryo, nin, nout, nbias
     )
     lane = lanes_of()
     upper = turn(tile(rim_h, 0), -4)
@@ -621,7 +635,7 @@
     e_shape = (3, ch, nodes)
     e_t = (e_shape, BF16, "fast")
     w_t = ((rows, 8, nz), F32, "fast")
-    sx_t = ((ch, (ny + 1) * nz), F32, "fast")
+    sx_t = tuple(((ch, n * nz), F32, "fast") for n in (ny + 1, 3, ny - 2))
     sy_t = ((ch * nx + ch // 2, nz), F32, "fast")
     hr_t = ((ch, 4 * LANES), BF16, "fast")
     er_t = ((3, ch, 4 * LANES), BF16, "fast")
@@ -655,23 +669,25 @@
         (pltpu.VMEM(e_shape, BF16),),
         flops=work,
     )
-    hr, er, wr, pr, sxe, sxo = call(
+    hr, er, wr, pr, sxe, sxa, sxb = call(
         functools.partial(first_rim, sizes),
         (p, own, nearby, rze, rzo, *edge),
         (),
-        (hr_t, er_t, wr_t, pr_t, sx_t, sx_t),
+        (hr_t, er_t, wr_t, pr_t, *sx_t),
     )
     for layer in range(layers):
-        got_x = exchange(sxe, sxo, "gx", "gz")
+        rxe = send_even(sxe, "gx")
+        rxa = send_odd(sxa, "gx", "gz")
+        rxb = send_odd(sxb, "gx", "gz")
         sye, syo, pr = call(
-            functools.partial(y_faces, sizes), (p, pr, *got_x), (), (sy_t, sy_t, pr_t)
+            functools.partial(y_faces, sizes), (p, pr, rxe, rxa), (), (sy_t, sy_t, pr_t)
         )
-        got = (*got_x, *exchange(sye, syo, "gy", "gx"))
+        got = (rxe, rxa, *exchange(sye, syo, "gy", "gx"))
         if layer + 1 < layers:
             last = layer + 2 == layers
             h_new, p_new, e_new, w_new = call(
                 functools.partial(inner_kernel, sizes, layer, last),
-                (h, p, *got_x, *node, *edge),
+                (h, p, rxe, rxb, *node, *edge),
                 (e, w),
                 (h_t, p_t, e_t, w_t),
                 (pltpu.SemaphoreType.DMA((2,)),),
@@ -680,13 +696,13 @@
         else:
             (res,) = call(
                 functools.partial(last_inner, sizes, layer),
-                (h, p, *got_x, *node),
+                (h, p, rxe, rxb, *node),
                 (),
                 (((ch, nodes), F32, "fast"),),
                 flops=work,
             )
         if layer + 1 < layers:
-            outs = (hr_t, pr_t, sx_t, sx_t) if last else (e_t, hr_t, er_t, pr_t, sx_t, sx_t)
+            outs = (hr_t, pr_t, *sx_t) if last else (e_t, hr_t, er_t, pr_t, *sx_t)
             args = (h, p, hr, er, wr, pr, *got, *node, *edge, w_new, h_new, p_new, e_new)
             n = len(args)
             moved = call(
@@ -697,9 +713,9 @@
                 aliases=((n - 3, 0), (n - 2, 1)) + (() if last else ((n - 1, 2),)),
             )
             if last:
-                h, p, hr, pr, sxe, sxo = moved
+                h, p, hr, pr, sxe, sxa, sxb = moved
             else:
-                h, p, e, hr, er, pr, sxe, sxo = moved
+                h, p, e, hr, er, pr, sxe, sxa, sxb = moved
         else:
             (out,) = call(
                 functools.partial(last_kernel, sizes, layer),

time: 53 us -> 54.1 us (1.021)
  the two profiles are of different devices: /device:TPU:68 before, /device:TPU:161 now
where the time goes in v7:
time: 54.1 us; the launch traced here: 53.9 us
  waiting for transfers between devices  26.4 us (49%)
  starting transfers between devices  13.9 us (26%)
  Pallas kernels  11.2 us (21%)
  local copies, waits for them, and re-layouts  2.18 us (4%)
    ppermute x10, waiting for transfers between devices, send_odd(): return lax.ppermute(values, AXES, odd_pairs(axis, spare))  19.2 us
    pallas_call x12, Pallas kernels, call(): pl.pallas_call(body, out_shape=[pltpu.VMEM(s, d) if where == 'fast' else...  11.2 us
    ppermute x10, starting transfers between devices, send_odd(): return lax.ppermute(values, AXES, odd_pairs(axis, spare))  7.93 us
    ppermute x7, waiting for transfers between devices, send_even(): return lax.ppermute(values, axis, even_pairs(lax.axis_size(axis)))  7.26 us
    ppermute x7, starting transfers between devices, send_even(): return lax.ppermute(values, axis, even_pairs(lax.axis_size(axis)))  5.96 us
    unnamed x16, local copies, waits for them, and re-layouts  2.18 us
  transfers between devices with their start and end apart: 17, of which 9 were waited for; matrix products, arithmetic and copies ran while one was open for 0% of the time, Pallas kernels for 9%

profile of v7, /device:TPU:161, one launch (start us, length us, event | category | flops | bytes accessed | tf_op | source)
XLA Modules:
  0.0 53.9 jit_solution(1539264828573383427)
XLA Ops:
  0.0 2.0 %shard_map.91 = (f32[4,768,128]{2,1,0:T(8,128)S(1)}, f32[24,8,128]{2,1,0:T(8,128)S(1)}, f32[2,136,128]{2,1,0:T(8,128)S(1)}, f32[136,128]{1,0:T(8,128)S(1)}, f32[136,128]{1,0:T(8,128)S(1)}) custom-call(bf16[32,3,8,128]{3,2,1,0:T(8,128)(2,1)} %f_in.1, bf16[3,32,3,8,128]{4,3,2,1,0:T(8,128)(2,1)} %es_in.1, s32[3,8,128]{2,1,0:T(8,128)} %m_in.1), custom_call_target="tpu_custom_call" | custom-call | tf_op jit(solution)/shard_map/pallas_call | solution.py:610
  2.0 1.3 %collective-permute-start = (f32[136,128]{1,0:T(8,128)S(1)}, f32[136,128]{1,0:T(8,128)S(1)}, u32[]{:S(2)}, u32[]{:S(2)}) collective-permute-start(f32[136,128]{1,0:T(8,128)S(1)} %get-tuple-element.60), channel_id=1, source_target_pairs={{0,1},{1,0},{2,3},{3,2},{4,5},{5,4},{6,7},{7,6},{8,9},{9,8},{10,11... | collective-permute-start | bytes 208904 | tf_op jit(solution)/shard_map/ppermute | solution.py:40
  3.3 2.3 %collective-permute-start.1 = (f32[136,128]{1,0:T(8,128)S(1)}, f32[136,128]{1,0:T(8,128)S(1)}, u32[]{:S(2)}, u32[]{:S(2)}) collective-permute-start(f32[136,128]{1,0:T(8,128)S(1)} %get-tuple-element.61), channel_id=1, source_target_pairs={{0,32},{1,2},{2,1},{3,4},{4,3},{5,6},{6,5},{7,39},{8,40},{9,10},{1... | collective-permute-start | bytes 208904 | tf_op jit(solution)/shard_map/ppermute | solution.py:44
  5.6 0.7 %copy-done = bf16[3,32,96]{2,1,0:T(8,128)(2,1)S(1)} copy-done((bf16[3,32,96]{2,1,0:T(8,128)(2,1)S(1)}, bf16[3,32,96]{2,1,0:T(8,128)(2,1)}, u32[]{:S(2)}) %copy-start) | copy-done | bytes 18456
  6.3 0.7 %copy-done.2 = bf16[3,32,32]{2,1,0:T(8,128)(2,1)S(1)} copy-done((bf16[3,32,32]{2,1,0:T(8,128)(2,1)S(1)}, bf16[3,32,32]{2,1,0:T(8,128)(2,1)}, u32[]{:S(2)}) %copy-start.2) | copy-done | bytes 6168
  7.1 0.7 %copy-done.6 = f32[3,32]{1,0:T(4,128)S(1)} copy-done((f32[3,32]{1,0:T(4,128)S(1)}, f32[3,32]{1,0:T(4,128)}, u32[]{:S(2)}) %copy-start.6) | copy-done | bytes 408
  7.8 0.0 copy-start.7
  7.8 1.4 %shard_map.92 = (bf16[32,3072]{1,0:T(8,128)(2,1)S(1)}, bf16[3,32,3072]{2,1,0:T(8,128)(2,1)S(1)}, f32[32,3072]{1,0:T(8,128)S(1)}, f32[2,136,128]{2,1,0:T(8,128)S(1)}) custom-call(f32[4,768,128]{2,1,0:T(8,128)S(1)} %get-tuple-element.54.buf, f32[24,8,128]{2,1,0:T(8,128)S(1)} %get-tuple-element.55.w_ref.w_in, bf16[3,32,96]{2,1,0:T(8,128)(2,1)S(1)} %copy-done, ...), custom_call_target="tpu_custom_call" | custom-call | flops 377487360 | tf_op jit(solution)/shard_map/pallas_call | solution.py:610
  9.1 0.0 collective-permute-done.rze
  9.2 0.0 collective-permute-done.1.rzo
  9.2 0.6 %shard_map.93 = (bf16[32,512]{1,0:T(8,128)(2,1)S(1)}, bf16[3,32,512]{2,1,0:T(8,128)(2,1)S(1)}, f32[8,512]{1,0:T(8,128)S(1)}, f32[32,512]{1,0:T(8,128)S(1)}, f32[...) custom-call(f32[32,3072]{1,0:T(8,128)S(1)} %get-tuple-element.57.p_ref.p_in, ...), custom_call_target="tpu_custom_call" | custom-call | tf_op jit(solution)/shard_map/pallas_call | solution.py:610
  9.8 1.6 %collective-permute-start.2 = (f32[32,1152]{1,0:T(8,128)S(1)}, f32[32,1152]{1,0:T(8,128)S(1)}, u32[]{:S(2)}, u32[]{:S(2)}) collective-permute-start(f32[32,1152]{1,0:T(8,128)S(1)} %get-tuple-element.66), channel_id=1, source_target_pairs={{0,32},{32,0},{64,96},{96,64},{128,160},{160,128},{192,224},{224,1... | collective-permute-start | bytes 442376 | tf_op jit(solution)/shard_map/ppermute | solution.py:40
  11.4 1.3 %collective-permute-start.6 = (f32[32,768]{1,0:T(8,128)S(1)}, f32[32,768]{1,0:T(8,128)S(1)}, u32[]{:S(2)}, u32[]{:S(2)}) collective-permute-start(f32[32,768]{1,0:T(8,128)S(1)} %get-tuple-element.71), channel_id=1, source_target_pairs={{0,1},{1,0},{2,3},{3,2},{4,5},{5,4},{6,7},{7,6},{8,9},{9,8},{10,11... | collective-permute-start | bytes 294920 | tf_op jit(solution)/shard_map/ppermute | solution.py:44
  12.7 0.5 collective-permute-start.3
  13.2 3.1 %collective-permute-done.3.rxa = f32[32,384]{1,0:T(8,128)S(1)} collective-permute-done((f32[32,384]{1,0:T(8,128)S(1)}, f32[32,384]{1,0:T(8,128)S(1)}, u32[]{:S(2)}, u32[]{:S(2)}) %collective-permute-start.3) | collective-permute-done | bytes 49184 | tf_op jit(solution)/shard_map/ppermute | solution.py:44
  16.3 0.0 collective-permute-done.2.rxe
  16.3 0.2 shard_map.94
  16.5 1.2 %collective-permute-start.4 = (f32[112,128]{1,0:T(8,128)S(1)}, f32[112,128]{1,0:T(8,128)S(1)}, u32[]{:S(2)}, u32[]{:S(2)}) collective-permute-start(f32[112,128]{1,0:T(8,128)S(1)} %get-tuple-element.69), channel_id=1, source_target_pairs={{0,8},{8,0},{16,24},{24,16},{1,9},{9,1},{17,25},{25,17},{2,10},{10... | collective-permute-start | bytes 172040 | tf_op jit(solution)/shard_map/ppermute | solution.py:40
  17.7 0.0 collective-permute-start.5
  17.7 0.0 collective-permute-done.6.rxb
  17.8 1.2 %shard_map.95 = (bf16[32,3072]{1,0:T(8,128)(2,1)S(1)}, f32[32,3072]{1,0:T(8,128)S(1)}, bf16[3,32,3072]{2,1,0:T(8,128)(2,1)S(1)}, f32[24,8,128]{2,1,0:T(8,128)S(1)}) custom-call(bf16[32,3072]{1,0:T(8,128)(2,1)S(1)} %get-tuple-element.56.h_in, f32[32,3072]{1,0:T(8,128)S(1)} %get-tuple-element.57.p_ref.p_in, f32[32,1152]{1,0:T(8,128)S(1)} %collective-permute-done.2.rxe, ...), custom_call_target="tpu_custom_call" | custom-call | flops 377487360 | tf_op jit(solution)/shard_map/pallas_call | solution.py:610
  19.0 1.5 %collective-permute-done.4.rye = f32[112,128]{1,0:T(8,128)S(1)} collective-permute-done((f32[112,128]{1,0:T(8,128)S(1)}, f32[112,128]{1,0:T(8,128)S(1)}, u32[]{:S(2)}, u32[]{:S(2)}) %collective-permute-start.4) | collective-permute-done | bytes 57376 | tf_op jit(solution)/shard_map/ppermute | solution.py:40
  20.5 3.4 %collective-permute-done.5.ryo = f32[112,128]{1,0:T(8,128)S(1)} collective-permute-done((f32[112,128]{1,0:T(8,128)S(1)}, f32[112,128]{1,0:T(8,128)S(1)}, u32[]{:S(2)}, u32[]{:S(2)}) %collective-permute-start.5) | collective-permute-done | bytes 57376 | tf_op jit(solution)/shard_map/ppermute | solution.py:44
  23.9 1.1 %shard_map.96 = (bf16[32,3072]{1,0:T(8,128)(2,1)S(1)}, f32[32,3072]{1,0:T(8,128)S(1)}, bf16[3,32,3072]{2,1,0:T(8,128)(2,1)S(1)}, bf16[32,512]{1,0:T(8,128)(2,1)S...) custom-call(bf16[32,3072]{1,0:T(8,128)(2,1)S(1)} %get-tuple-element., ...), custom_call_target="tpu_custom_call", output_to_operand_aliasing={{0}: (17, {}), {1}: (18, {}), {2}: (19, {})} | custom-call | tf_op jit(solution)/shard_map/pallas_call | solution.py:610
  25.0 1.0 %collective-permute-start.7 = (f32[32,1152]{1,0:T(8,128)S(1)}, f32[32,1152]{1,0:T(8,128)S(1)}, u32[]{:S(2)}, u32[]{:S(2)}) collective-permute-start(f32[32,1152]{1,0:T(8,128)S(1)} %get-tuple-element.82), channel_id=1, source_target_pairs={{0,32},{32,0},{64,96},{96,64},{128,160},{160,128},{192,224},{224,1... | collective-permute-start | bytes 442376 | tf_op jit(solution)/shard_map/ppermute | solution.py:40
  26.0 0.7 %collective-permute-start.11 = (f32[32,768]{1,0:T(8,128)S(1)}, f32[32,768]{1,0:T(8,128)S(1)}, u32[]{:S(2)}, u32[]{:S(2)}) collective-permute-start(f32[32,768]{1,0:T(8,128)S(1)} %get-tuple-element.87), channel_id=1, source_target_pairs={{0,1},{1,0},{2,3},{3,2},{4,5},{5,4},{6,7},{7,6},{8,9},{9,8},{10,11... | collective-permute-start | bytes 294920 | tf_op jit(solution)/shard_map/ppermute | solution.py:44
  26.7 1.1 %collective-permute-start.8 = (f32[32,384]{1,0:T(8,128)S(1)}, f32[32,384]{1,0:T(8,128)S(1)}, u32[]{:S(2)}, u32[]{:S(2)}) collective-permute-start(f32[32,384]{1,0:T(8,128)S(1)} %get-tuple-element.83), channel_id=1, source_target_pairs={{0,1},{1,0},{2,3},{3,2},{4,5},{5,4},{6,7},{7,6},{8,9},{9,8},{10,11... | collective-permute-start | bytes 147464 | tf_op jit(solution)/shard_map/ppermute | solution.py:44
  27.8 3.1 %collective-permute-done.8.rxa = f32[32,384]{1,0:T(8,128)S(1)} collective-permute-done((f32[32,384]{1,0:T(8,128)S(1)}, f32[32,384]{1,0:T(8,128)S(1)}, u32[]{:S(2)}, u32[]{:S(2)}) %collective-permute-start.8) | collective-permute-done | bytes 49184 | tf_op jit(solution)/shard_map/ppermute | solution.py:44
  30.9 0.2 shard_map.97
  31.1 0.1 collective-permute-start.9
  31.2 0.3 collective-permute-start.10
  31.4 0.0 collective-permute-done.11.rxb
  31.5 1.2 %shard_map.98 = (bf16[32,3072]{1,0:T(8,128)(2,1)S(1)}, f32[32,3072]{1,0:T(8,128)S(1)}, bf16[3,32,3072]{2,1,0:T(8,128)(2,1)S(1)}, f32[24,8,128]{2,1,0:T(8,128)S(1)}) custom-call(bf16[32,3072]{1,0:T(8,128)(2,1)S(1)} %get-tuple-element.77.h_in, f32[32,3072]{1,0:T(8,128)S(1)} %get-tuple-element.78.p_ref.p_in, f32[32,1152]{1,0:T(8,128)S(1)} %collective-permute-done.7.rxe, ...), custom_call_target="tpu_custom_call" | custom-call | flops 377487360 | tf_op jit(solution)/shard_map/pallas_call | solution.py:610
  32.7 2.4 %collective-permute-done.9.rye = f32[112,128]{1,0:T(8,128)S(1)} collective-permute-done((f32[112,128]{1,0:T(8,128)S(1)}, f32[112,128]{1,0:T(8,128)S(1)}, u32[]{:S(2)}, u32[]{:S(2)}) %collective-permute-start.9) | collective-permute-done | bytes 57376 | tf_op jit(solution)/shard_map/ppermute | solution.py:40
  35.1 3.3 %collective-permute-done.10.ryo = f32[112,128]{1,0:T(8,128)S(1)} collective-permute-done((f32[112,128]{1,0:T(8,128)S(1)}, f32[112,128]{1,0:T(8,128)S(1)}, u32[]{:S(2)}, u32[]{:S(2)}) %collective-permute-start.10) | collective-permute-done | bytes 57376 | tf_op jit(solution)/shard_map/ppermute | solution.py:44
  38.4 1.1 %shard_map.99 = (bf16[32,3072]{1,0:T(8,128)(2,1)S(1)}, f32[32,3072]{1,0:T(8,128)S(1)}, bf16[32,512]{1,0:T(8,128)(2,1)S(1)}, f32[32,512]{1,0:T(8,128)S(1)}, f32[3...) custom-call(bf16[32,3072]{1,0:T(8,128)(2,1)S(1)} %get-tuple-element., ...), custom_call_target="tpu_custom_call", output_to_operand_aliasing={{0}: (17, {}), {1}: (18, {})} | custom-call | tf_op jit(solution)/shard_map/pallas_call | solution.py:610
  39.5 0.7 %collective-permute-start.12 = (f32[32,1152]{1,0:T(8,128)S(1)}, f32[32,1152]{1,0:T(8,128)S(1)}, u32[]{:S(2)}, u32[]{:S(2)}) collective-permute-start(f32[32,1152]{1,0:T(8,128)S(1)} %get-tuple-element.97), channel_id=1, source_target_pairs={{0,32},{32,0},{64,96},{96,64},{128,160},{160,128},{192,224},{224,1... | collective-permute-start | bytes 442376 | tf_op jit(solution)/shard_map/ppermute | solution.py:40
  40.2 1.7 %collective-permute-start.13 = (f32[32,384]{1,0:T(8,128)S(1)}, f32[32,384]{1,0:T(8,128)S(1)}, u32[]{:S(2)}, u32[]{:S(2)}) collective-permute-start(f32[32,384]{1,0:T(8,128)S(1)} %get-tuple-element.98), channel_id=1, source_target_pairs={{0,1},{1,0},{2,3},{3,2},{4,5},{5,4},{6,7},{7,6},{8,9},{9,8},{10,11... | collective-permute-start | bytes 147464 | tf_op jit(solution)/shard_map/ppermute | solution.py:44
  42.0 3.1 %collective-permute-done.13.rxa = f32[32,384]{1,0:T(8,128)S(1)} collective-permute-done((f32[32,384]{1,0:T(8,128)S(1)}, f32[32,384]{1,0:T(8,128)S(1)}, u32[]{:S(2)}, u32[]{:S(2)}) %collective-permute-start.13) | collective-permute-done | bytes 49184 | tf_op jit(solution)/shard_map/ppermute | solution.py:44
  45.1 0.0 collective-permute-done.12.rxe
  45.1 0.2 shard_map.100
  45.3 0.1 collective-permute-start.14
  45.4 0.2 collective-permute-start.15
  45.5 0.0 collective-permute-done.16.rxb
  45.5 0.4 shard_map.101.res
  45.9 3.4 %collective-permute-done.14.rye = f32[112,128]{1,0:T(8,128)S(1)} collective-permute-done((f32[112,128]{1,0:T(8,128)S(1)}, f32[112,128]{1,0:T(8,128)S(1)}, u32[]{:S(2)}, u32[]{:S(2)}) %collective-permute-start.14) | collective-permute-done | bytes 57376 | tf_op jit(solution)/shard_map/ppermute | solution.py:40
  49.3 3.1 %collective-permute-done.15.ryo = f32[112,128]{1,0:T(8,128)S(1)} collective-permute-done((f32[112,128]{1,0:T(8,128)S(1)}, f32[112,128]{1,0:T(8,128)S(1)}, u32[]{:S(2)}, u32[]{:S(2)}) %collective-permute-start.15) | collective-permute-done | bytes 57376 | tf_op jit(solution)/shard_map/ppermute | solution.py:44
  52.4 1.5 %shard_map.102 = bf16[32,3,8,128]{3,2,1,0:T(8,128)(2,1)} custom-call(bf16[32,3072]{1,0:T(8,128)(2,1)S(1)} %get-tuple-element.93.h_in, f32[32,3072]{1,0:T(8,128)S(1)} %get-tuple-element.94.p_ref.p_in, bf16[32,512]{1,0:T(8,128)(2,1)S(1)} %get-tuple-element.95.hr_in, f32[32,512]{1,0:T(8,128)S(1)} %get-tuple-element.99.pr_in, ...), custom_call_target="tpu_custom_call" | custom-call | tf_op jit(solution)/shard_map/pallas_call | solution.py:610
  (14 shorter events, 0.0 us)
Async XLA Ops:
  2.0 7.1 %collective-permute-start = (f32[136,128]{1,0:T(8,128)S(1)}, f32[136,128]{1,0:T(8,128)S(1)}, u32[]{:S(2)}, u32[]{:S(2)}) collective-permute-start(f32[136,128]{1,0:T(8,128)S(1)} %get-tuple-element.60), channel_id=1, source_target_pairs={{0,1},{1,0},{2,3},{3,2},{4,5},{5,4},{6,7},{7,6},{8,9},{9,8},{10,11... | collective-permute-start | bytes 208904 | tf_op jit(solution)/shard_map/ppermute | solution.py:40
  3.3 5.8 %collective-permute-start.1 = (f32[136,128]{1,0:T(8,128)S(1)}, f32[136,128]{1,0:T(8,128)S(1)}, u32[]{:S(2)}, u32[]{:S(2)}) collective-permute-start(f32[136,128]{1,0:T(8,128)S(1)} %get-tuple-element.61), channel_id=1, source_target_pairs={{0,32},{1,2},{2,1},{3,4},{4,3},{5,6},{6,5},{7,39},{8,40},{9,10},{1... | collective-permute-start | bytes 208904 | tf_op jit(solution)/shard_map/ppermute | solution.py:44
  5.6 0.7 %copy-start = (bf16[3,32,96]{2,1,0:T(8,128)(2,1)S(1)}, bf16[3,32,96]{2,1,0:T(8,128)(2,1)}, u32[]{:S(2)}) copy-start(bf16[3,32,96]{2,1,0:T(8,128)(2,1)} %win.11) | copy-start | bytes 55300
  6.3 0.7 %copy-start.2 = (bf16[3,32,32]{2,1,0:T(8,128)(2,1)S(1)}, bf16[3,32,32]{2,1,0:T(8,128)(2,1)}, u32[]{:S(2)}) copy-start(bf16[3,32,32]{2,1,0:T(8,128)(2,1)} %wout.11) | copy-start | bytes 18436
  7.1 0.7 %copy-start.6 = (f32[3,32]{1,0:T(4,128)S(1)}, f32[3,32]{1,0:T(4,128)}, u32[]{:S(2)}) copy-start(f32[3,32]{1,0:T(4,128)} %bias.11) | copy-start | bytes 1156
  7.7 10.0 %copy-start.1 = (bf16[3,32,96]{2,1,0:T(8,128)(2,1)S(1)}, bf16[3,32,96]{2,1,0:T(8,128)(2,1)}, u32[]{:S(2)}) copy-start(bf16[3,32,96]{2,1,0:T(8,128)(2,1)} %win.11) | copy-start | bytes 55300
  7.7 10.0 %copy-start.3 = (bf16[3,32,32]{2,1,0:T(8,128)(2,1)S(1)}, bf16[3,32,32]{2,1,0:T(8,128)(2,1)}, u32[]{:S(2)}) copy-start(bf16[3,32,32]{2,1,0:T(8,128)(2,1)} %wout.11) | copy-start | bytes 18436
  7.7 10.0 %copy-start.4 = (bf16[3,32,64]{2,1,0:T(8,128)(2,1)S(1)}, bf16[3,32,64]{2,1,0:T(8,128)(2,1)}, u32[]{:S(2)}) copy-start(bf16[3,32,64]{2,1,0:T(8,128)(2,1)} %nin.11) | copy-start | bytes 36868
  7.7 10.0 %copy-start.5 = (bf16[3,32,32]{2,1,0:T(8,128)(2,1)S(1)}, bf16[3,32,32]{2,1,0:T(8,128)(2,1)}, u32[]{:S(2)}) copy-start(bf16[3,32,32]{2,1,0:T(8,128)(2,1)} %nout.11) | copy-start | bytes 18436
  7.8 10.0 %copy-start.7 = (f32[3,32]{1,0:T(4,128)S(1)}, f32[3,32]{1,0:T(4,128)}, u32[]{:S(2)}) copy-start(f32[3,32]{1,0:T(4,128)} %nbias.11) | copy-start | bytes 1156
  9.8 6.5 %collective-permute-start.2 = (f32[32,1152]{1,0:T(8,128)S(1)}, f32[32,1152]{1,0:T(8,128)S(1)}, u32[]{:S(2)}, u32[]{:S(2)}) collective-permute-start(f32[32,1152]{1,0:T(8,128)S(1)} %get-tuple-element.66), channel_id=1, source_target_pairs={{0,32},{32,0},{64,96},{96,64},{128,160},{160,128},{192,224},{224,1... | collective-permute-start | bytes 442376 | tf_op jit(solution)/shard_map/ppermute | solution.py:40
  11.4 6.3 %collective-permute-start.6 = (f32[32,768]{1,0:T(8,128)S(1)}, f32[32,768]{1,0:T(8,128)S(1)}, u32[]{:S(2)}, u32[]{:S(2)}) collective-permute-start(f32[32,768]{1,0:T(8,128)S(1)} %get-tuple-element.71), channel_id=1, source_target_pairs={{0,1},{1,0},{2,3},{3,2},{4,5},{5,4},{6,7},{7,6},{8,9},{9,8},{10,11... | collective-permute-start | bytes 294920 | tf_op jit(solution)/shard_map/ppermute | solution.py:44
  12.7 3.6 %collective-permute-start.3 = (f32[32,384]{1,0:T(8,128)S(1)}, f32[32,384]{1,0:T(8,128)S(1)}, u32[]{:S(2)}, u32[]{:S(2)}) collective-permute-start(f32[32,384]{1,0:T(8,128)S(1)} %get-tuple-element.67), channel_id=1, source_target_pairs={{0,1},{1,0},{2,3},{3,2},{4,5},{5,4},{6,7},{7,6},{8,9},{9,8},{10,11... | collective-permute-start | bytes 147464 | tf_op jit(solution)/shard_map/ppermute | solution.py:44
  16.5 4.0 %collective-permute-start.4 = (f32[112,128]{1,0:T(8,128)S(1)}, f32[112,128]{1,0:T(8,128)S(1)}, u32[]{:S(2)}, u32[]{:S(2)}) collective-permute-start(f32[112,128]{1,0:T(8,128)S(1)} %get-tuple-element.69), channel_id=1, source_target_pairs={{0,8},{8,0},{16,24},{24,16},{1,9},{9,1},{17,25},{25,17},{2,10},{10... | collective-permute-start | bytes 172040 | tf_op jit(solution)/shard_map/ppermute | solution.py:40
  17.7 6.1 %collective-permute-start.5 = (f32[112,128]{1,0:T(8,128)S(1)}, f32[112,128]{1,0:T(8,128)S(1)}, u32[]{:S(2)}, u32[]{:S(2)}) collective-permute-start(f32[112,128]{1,0:T(8,128)S(1)} %get-tuple-element.70), channel_id=1, source_target_pairs={{0,32},{1,33},{2,34},{3,35},{4,36},{5,37},{6,38},{7,39},{8,16},{9,... | collective-permute-start | bytes 172040 | tf_op jit(solution)/shard_map/ppermute | solution.py:44
  25.0 5.9 %collective-permute-start.7 = (f32[32,1152]{1,0:T(8,128)S(1)}, f32[32,1152]{1,0:T(8,128)S(1)}, u32[]{:S(2)}, u32[]{:S(2)}) collective-permute-start(f32[32,1152]{1,0:T(8,128)S(1)} %get-tuple-element.82), channel_id=1, source_target_pairs={{0,32},{32,0},{64,96},{96,64},{128,160},{160,128},{192,224},{224,1... | collective-permute-start | bytes 442376 | tf_op jit(solution)/shard_map/ppermute | solution.py:40
  26.0 5.4 %collective-permute-start.11 = (f32[32,768]{1,0:T(8,128)S(1)}, f32[32,768]{1,0:T(8,128)S(1)}, u32[]{:S(2)}, u32[]{:S(2)}) collective-permute-start(f32[32,768]{1,0:T(8,128)S(1)} %get-tuple-element.87), channel_id=1, source_target_pairs={{0,1},{1,0},{2,3},{3,2},{4,5},{5,4},{6,7},{7,6},{8,9},{9,8},{10,11... | collective-permute-start | bytes 294920 | tf_op jit(solution)/shard_map/ppermute | solution.py:44
  26.7 4.2 %collective-permute-start.8 = (f32[32,384]{1,0:T(8,128)S(1)}, f32[32,384]{1,0:T(8,128)S(1)}, u32[]{:S(2)}, u32[]{:S(2)}) collective-permute-start(f32[32,384]{1,0:T(8,128)S(1)} %get-tuple-element.83), channel_id=1, source_target_pairs={{0,1},{1,0},{2,3},{3,2},{4,5},{5,4},{6,7},{7,6},{8,9},{9,8},{10,11... | collective-permute-start | bytes 147464 | tf_op jit(solution)/shard_map/ppermute | solution.py:44
  31.1 4.0 %collective-permute-start.9 = (f32[112,128]{1,0:T(8,128)S(1)}, f32[112,128]{1,0:T(8,128)S(1)}, u32[]{:S(2)}, u32[]{:S(2)}) collective-permute-start(f32[112,128]{1,0:T(8,128)S(1)} %get-tuple-element.85), channel_id=1, source_target_pairs={{0,8},{8,0},{16,24},{24,16},{1,9},{9,1},{17,25},{25,17},{2,10},{10... | collective-permute-start | bytes 172040 | tf_op jit(solution)/shard_map/ppermute | solution.py:40
  31.2 7.2 %collective-permute-start.10 = (f32[112,128]{1,0:T(8,128)S(1)}, f32[112,128]{1,0:T(8,128)S(1)}, u32[]{:S(2)}, u32[]{:S(2)}) collective-permute-start(f32[112,128]{1,0:T(8,128)S(1)} %get-tuple-element.86), channel_id=1, source_target_pairs={{0,32},{1,33},{2,34},{3,35},{4,36},{5,37},{6,38},{7,39},{8,16},{9,... | collective-permute-start | bytes 172040 | tf_op jit(solution)/shard_map/ppermute | solution.py:44
  39.5 5.6 %collective-permute-start.12 = (f32[32,1152]{1,0:T(8,128)S(1)}, f32[32,1152]{1,0:T(8,128)S(1)}, u32[]{:S(2)}, u32[]{:S(2)}) collective-permute-start(f32[32,1152]{1,0:T(8,128)S(1)} %get-tuple-element.97), channel_id=1, source_target_pairs={{0,32},{32,0},{64,96},{96,64},{128,160},{160,128},{192,224},{224,1... | collective-permute-start | bytes 442376 | tf_op jit(solution)/shard_map/ppermute | solution.py:40
  40.2 5.3 %collective-permute-start.16 = (f32[32,768]{1,0:T(8,128)S(1)}, f32[32,768]{1,0:T(8,128)S(1)}, u32[]{:S(2)}, u32[]{:S(2)}) collective-permute-start(f32[32,768]{1,0:T(8,128)S(1)} %get-tuple-element.102), channel_id=1, source_target_pairs={{0,1},{1,0},{2,3},{3,2},{4,5},{5,4},{6,7},{7,6},{8,9},{9,8},{10,11... | collective-permute-start | bytes 294920 | tf_op jit(solution)/shard_map/ppermute | solution.py:44
  40.2 4.8 %collective-permute-start.13 = (f32[32,384]{1,0:T(8,128)S(1)}, f32[32,384]{1,0:T(8,128)S(1)}, u32[]{:S(2)}, u32[]{:S(2)}) collective-permute-start(f32[32,384]{1,0:T(8,128)S(1)} %get-tuple-element.98), channel_id=1, source_target_pairs={{0,1},{1,0},{2,3},{3,2},{4,5},{5,4},{6,7},{7,6},{8,9},{9,8},{10,11... | collective-permute-start | bytes 147464 | tf_op jit(solution)/shard_map/ppermute | solution.py:44
  45.3 4.0 %collective-permute-start.14 = (f32[112,128]{1,0:T(8,128)S(1)}, f32[112,128]{1,0:T(8,128)S(1)}, u32[]{:S(2)}, u32[]{:S(2)}) collective-permute-start(f32[112,128]{1,0:T(8,128)S(1)} %get-tuple-element.100), channel_id=1, source_target_pairs={{0,8},{8,0},{16,24},{24,16},{1,9},{9,1},{17,25},{25,17},{2,10},{10... | collective-permute-start | bytes 172040 | tf_op jit(solution)/shard_map/ppermute | solution.py:40
  45.4 7.1 %collective-permute-start.15 = (f32[112,128]{1,0:T(8,128)S(1)}, f32[112,128]{1,0:T(8,128)S(1)}, u32[]{:S(2)}, u32[]{:S(2)}) collective-permute-start(f32[112,128]{1,0:T(8,128)S(1)} %get-tuple-element.101), channel_id=1, source_target_pairs={{0,32},{1,33},{2,34},{3,35},{4,36},{5,37},{6,38},{7,39},{8,16},{9,... | collective-permute-start | bytes 172040 | tf_op jit(solution)/shard_map/ppermute | solution.py:44

commit v8 on v7

--- a/solution.py
+++ b/solution.py
@@ -301,16 +301,39 @@
         dest[i, first : first + size, :] = turn(found[i], back)
 
 
+def pack_ends(v):
+    free = lanes_of() >= 96
+    e_z = v[96:128]
+    pieces = [
+        jnp.where(free, turn(e_z, 96 - 32 * i), v[32 * i : 32 * i + 32]) for i in range(3)
+    ]
+    return jnp.concatenate(pieces + [v[128:136]], axis=0)
+
+
+def unpack_ends(v):
+    lane = lanes_of()
+    pieces = [v[32 * i : 32 * i + 32] for i in range(3)]
+    e_z = jnp.zeros_like(pieces[0])
+    for i, piece in enumerate(pieces):
+        e_z = jnp.where(lane // 32 == i, turn(piece, 32 + 32 * i), e_z)
+    pieces = [jnp.where(lane < 96, piece, 0.0) for piece in pieces]
+    return jnp.concatenate(pieces + [e_z, v[96:104]], axis=0)
+
+
 def unpack_kernel(
-    sizes, f_in, es_in, m_in, buf, w_ref, own_ref, sze, szo, f_ref, es_ref, m_ref, sems
+    sizes, f_in, es_in, m_in, *rest
 ):
     nx, ny = sizes
     rows = nx * ny
+    weights, (buf, w_ref, own_ref, sze, szo), rest = rest[:6], rest[6:11], rest[11:]
+    weights_out, (f_ref, es_ref, m_ref, sems) = rest[:6], rest[6:]
     fetches = [pltpu.make_async_copy(m_in, m_ref, sems.at[0])]
     fetches.append(pltpu.make_async_copy(f_in, f_ref, sems.at[1]))
     for d in range(3):
         fetches.append(pltpu.make_async_copy(es_in.at[d], es_ref.at[d], sems.at[2 + d]))
-    for fetch in fetches:
+    for i, (source, dest) in enumerate(zip(weights, weights_out)):
+        fetches.append(pltpu.make_async_copy(source, dest, sems.at[5 + i]))
+    for fetch in fetches[:1] + fetches[5:] + fetches[1:5]:
         fetch.start()
     fetches[0].wait()
     counts = m_ref[...]
@@ -345,8 +368,11 @@
         )
     collect(own_ref, 128, 8, ENDS, rows, lambda k: w_ref[k])
     is_even = lax.axis_index("gz") % 2 == 0
-    sze[...] = jnp.where(is_even, own_ref[0], own_ref[1])
-    szo[...] = jnp.where(is_even, own_ref[1], own_ref[0])
+    lower, upper = pack_ends(own_ref[0]), pack_ends(own_ref[1])
+    sze[...] = jnp.where(is_even, lower, upper)
+    szo[...] = jnp.where(is_even, upper, lower)
+    for fetch in fetches[5:]:
+        fetch.wait()
 
 
 def first_edges(sizes, buf, w_ref, win, wout, bias, h_ref, e_out, p_ref, next_ref, e_ref):
@@ -375,7 +401,7 @@
     at = lanes_of(own_ref.shape[1]) % 4
     own_a, own_b = own_ref[0], own_ref[1]
     upper, lower = next_ref[0], next_ref[1]
-    prev, nxt = place("gz", rze[...], rzo[...])
+    prev, nxt = (unpack_ends(v) for v in place("gz", rze[...], rzo[...]))
     tiles = [
         own_a,
         own_b,
@@ -580,7 +606,7 @@
 
 
 def last_kernel(
-    sizes, layer, h_in, p_in, hr_in, pr_in, rxe, rxa, rye, ryo, nin, nout, nbias, res, out, buf
+    sizes, layer, h_in, p_in, hr_in, pr_in, rxe, rxa, rye, ryo, nin, nout, nbias, res, out, buf, done, sems
 ):
     nx, ny = sizes
     rows = nx * ny
@@ -590,14 +616,20 @@
     lane = lanes_of()
     upper = turn(tile(rim_h, 0), -4)
     lower = tile(rim_h, 1)
+    sends = []
     for k in range(rows):
         x, y = divmod(k, ny)
         inside = 0 < y < ny - 1
         t = res[:, span_of(k, 1)] if inside else tile(edge_h, 2 * x + (y > 0))
         t = jnp.where(lane < 3, turn(lower, -4 * k), t)
         t = jnp.where(lane >= LANES - 3, turn(upper, -4 * k), t)
-        buf[pl.ds(k, 32, stride=rows), :] = t
-    out[...] = buf[...].reshape(out.shape).astype(BF16)
+        buf[x, pl.ds(y, 32, stride=ny), :] = t
+        if y == ny - 1:
+            done[x] = buf[x].reshape(done.shape[1:]).astype(BF16)
+            sends.append(pltpu.make_async_copy(done.at[x], out.at[:, x], sems.at[x]))
+            sends[-1].start()
+    for send in sends:
+        send.wait()
 
 
 def call(body, fast, slow, outs, scratch=(), flops=0, aliases=()):
@@ -614,7 +646,9 @@
             for s, d, where in outs
         ],
         in_specs=[vmem] * len(fast) + [anywhere] * len(slow),
-        out_specs=[vmem] * len(outs),
+        out_specs=[
+            pl.BlockSpec(memory_space=pltpu.HBM) if where == "out" else vmem for _, _, where in outs
+        ],
         scratch_shapes=list(scratch),
         input_output_aliases=dict(aliases),
         compiler_params=pltpu.CompilerParams(vmem_limit_bytes=12 * 2**20),
@@ -642,25 +676,28 @@
     wr_t = ((8, 4 * LANES), F32, "fast")
     pr_t = ((ch, 4 * LANES), F32, "fast")
     z_rows = 4 * ch + 8
-    sz_t = ((z_rows, LANES), F32, "fast")
+    sz_t = ((3 * ch + 8, LANES), F32, "fast")
     work = 4 * 2 * 5 * 3 * ch * ch * nodes
 
     ends_t = ((2, z_rows, LANES), F32, "fast")
-    buf, w, own, sze, szo = call(
+    weights = (edge_in, edge_out, edge_bias, node_in, node_out, node_bias)
+    buf, w, own, sze, szo, *weights = call(
         functools.partial(unpack_kernel, sizes),
         (),
-        (features, edge_state, multiplicity),
-        (((4, ch * rows, nz), F32, "fast"), w_t, ends_t, sz_t, sz_t),
+        (features, edge_state, multiplicity, *weights),
+        (
+            ((4, ch * rows, nz), F32, "fast"), w_t, ends_t, sz_t, sz_t,
+            *((v.shape, v.dtype, "fast") for v in weights),
+        ),
         (
             pltpu.VMEM(features.shape, BF16),
             pltpu.VMEM(edge_state.shape, BF16),
             pltpu.VMEM(multiplicity.shape, jnp.int32),
-            pltpu.SemaphoreType.DMA((5,)),
+            pltpu.SemaphoreType.DMA((11,)),
         ),
     )
     rze, rzo = exchange(sze, szo, "gz", "gx")
-    edge = (edge_in, edge_out, edge_bias)
-    node = (node_in, node_out, node_bias)
+    edge, node = weights[:3], weights[3:]
     h, e, p, nearby = call(
         functools.partial(first_edges, sizes),
         (buf, w, *edge),
@@ -722,7 +759,11 @@
                 (h, p, hr, pr, *got, *node, res),
                 (),
                 ((features.shape, BF16, "out"),),
-                (pltpu.VMEM((ch * rows, nz), F32),),
+                (
+                    pltpu.VMEM((nx, ch * ny, nz), F32),
+                    pltpu.VMEM((nx, ch, ny, nz), BF16),
+                    pltpu.SemaphoreType.DMA((nx,)),
+                ),
             )
     return out
 

time: 54.1 us -> 53.2 us (0.983)
  the two profiles are of different devices: /device:TPU:161 before, /device:TPU:68 now
where the time goes in v8:
time: 53.2 us; the launch traced here: 52.5 us
  starting transfers between devices  23.2 us (44%)
  waiting for transfers between devices  17.6 us (33%)
  Pallas kernels  11.4 us (21%)
    ppermute x10, starting transfers between devices, send_odd(): return lax.ppermute(values, AXES, odd_pairs(axis, spare))  21.5 us
    ppermute x10, waiting for transfers between devices, send_odd(): return lax.ppermute(values, AXES, odd_pairs(axis, spare))  15.1 us
    pallas_call x12, Pallas kernels, call(): pl.pallas_call(body, out_shape=[pltpu.VMEM(s, d) if where == 'fast' else...  11.4 us
    ppermute x7, waiting for transfers between devices, send_even(): return lax.ppermute(values, axis, even_pairs(lax.axis_size(axis)))  2.46 us
    ppermute x7, starting transfers between devices, send_even(): return lax.ppermute(values, axis, even_pairs(lax.axis_size(axis)))  1.71 us
  transfers between devices with their start and end apart: 17, of which 9 were waited for; matrix products, arithmetic and copies ran while one was open for 0% of the time, Pallas kernels for 9%

profile of v8, /device:TPU:68, one launch (start us, length us, event | category | flops | bytes accessed | tf_op | source)
XLA Modules:
  0.0 52.5 jit_solution(4844955424977519906)
XLA Ops:
  0.0 2.3 %shard_map.91 = (f32[4,768,128]{2,1,0:T(8,128)S(1)}, f32[24,8,128]{2,1,0:T(8,128)S(1)}, f32[2,136,128]{2,1,0:T(8,128)S(1)}, f32[104,128]{1,0:T(8,128)S(1)}, f32[...) custom-call(bf16[32,3,8,128]{3,2,1,0:T(8,128)(2,1)} %f_in.1, ...), custom_call_target="tpu_custom_call" | custom-call | tf_op jit(solution)/shard_map/pallas_call | solution.py:642
  2.3 1.3 %collective-permute-start = (f32[104,128]{1,0:T(8,128)S(1)}, f32[104,128]{1,0:T(8,128)S(1)}, u32[]{:S(2)}, u32[]{:S(2)}) collective-permute-start(f32[104,128]{1,0:T(8,128)S(1)} %get-tuple-element.69), channel_id=1, source_target_pairs={{0,1},{1,0},{2,3},{3,2},{4,5},{5,4},{6,7},{7,6},{8,9},{9,8},{10,11... | collective-permute-start | bytes 159752 | tf_op jit(solution)/shard_map/ppermute | solution.py:40
  3.5 0.0 collective-permute-start.1
  3.5 1.4 %shard_map.92 = (bf16[32,3072]{1,0:T(8,128)(2,1)S(1)}, bf16[3,32,3072]{2,1,0:T(8,128)(2,1)S(1)}, f32[32,3072]{1,0:T(8,128)S(1)}, f32[2,136,128]{2,1,0:T(8,128)S(1)}) custom-call(f32[4,768,128]{2,1,0:T(8,128)S(1)} %get-tuple-element.60.buf, f32[24,8,128]{2,1,0:T(8,128)S(1)} %get-tuple-element.61.w_ref.w_in, bf16[3,32,96]{2,1,0:T(8,128)(2,1)S(1)} %get-tuple-element.62.win, ...), custom_call_target="tpu_custom_call" | custom-call | flops 377487360 | tf_op jit(solution)/shard_map/pallas_call | solution.py:642
  4.9 1.5 %collective-permute-done.rze = f32[104,128]{1,0:T(8,128)S(1)} collective-permute-done((f32[104,128]{1,0:T(8,128)S(1)}, f32[104,128]{1,0:T(8,128)S(1)}, u32[]{:S(2)}, u32[]{:S(2)}) %collective-permute-start) | collective-permute-done | bytes 53280 | tf_op jit(solution)/shard_map/ppermute | solution.py:40
  6.5 1.2 %collective-permute-done.1.rzo = f32[104,128]{1,0:T(8,128)S(1)} collective-permute-done((f32[104,128]{1,0:T(8,128)S(1)}, f32[104,128]{1,0:T(8,128)S(1)}, u32[]{:S(2)}, u32[]{:S(2)}) %collective-permute-start.1) | collective-permute-done | bytes 53280 | tf_op jit(solution)/shard_map/ppermute | solution.py:44
  7.7 0.6 %shard_map.93 = (bf16[32,512]{1,0:T(8,128)(2,1)S(1)}, bf16[3,32,512]{2,1,0:T(8,128)(2,1)S(1)}, f32[8,512]{1,0:T(8,128)S(1)}, f32[32,512]{1,0:T(8,128)S(1)}, f32[...) custom-call(f32[32,3072]{1,0:T(8,128)S(1)} %get-tuple-element.66.p_ref.p_in, ...), custom_call_target="tpu_custom_call" | custom-call | tf_op jit(solution)/shard_map/pallas_call | solution.py:642
  8.3 0.1 collective-permute-start.2
  8.4 3.0 %collective-permute-start.6 = (f32[32,768]{1,0:T(8,128)S(1)}, f32[32,768]{1,0:T(8,128)S(1)}, u32[]{:S(2)}, u32[]{:S(2)}) collective-permute-start(f32[32,768]{1,0:T(8,128)S(1)} %get-tuple-element.83), channel_id=1, source_target_pairs={{0,1},{1,0},{2,3},{3,2},{4,5},{5,4},{6,7},{7,6},{8,9},{9,8},{10,11... | collective-permute-start | bytes 294920 | tf_op jit(solution)/shard_map/ppermute | solution.py:44
  11.4 0.1 collective-permute-start.3
  11.5 4.0 %collective-permute-done.3.rxa = f32[32,384]{1,0:T(8,128)S(1)} collective-permute-done((f32[32,384]{1,0:T(8,128)S(1)}, f32[32,384]{1,0:T(8,128)S(1)}, u32[]{:S(2)}, u32[]{:S(2)}) %collective-permute-start.3) | collective-permute-done | bytes 49184 | tf_op jit(solution)/shard_map/ppermute | solution.py:44
  15.5 0.0 collective-permute-done.2.rxe
  15.5 0.2 shard_map.94
  15.8 0.0 collective-permute-start.4
  15.8 5.9 %collective-permute-start.5 = (f32[112,128]{1,0:T(8,128)S(1)}, f32[112,128]{1,0:T(8,128)S(1)}, u32[]{:S(2)}, u32[]{:S(2)}) collective-permute-start(f32[112,128]{1,0:T(8,128)S(1)} %get-tuple-element.79), channel_id=1, source_target_pairs={{0,32},{1,33},{2,34},{3,35},{4,36},{5,37},{6,38},{7,39},{8,16},{9,... | collective-permute-start | bytes 172040 | tf_op jit(solution)/shard_map/ppermute | solution.py:44
  21.8 0.0 collective-permute-done.6.rxb
  21.8 1.2 %shard_map.95 = (bf16[32,3072]{1,0:T(8,128)(2,1)S(1)}, f32[32,3072]{1,0:T(8,128)S(1)}, bf16[3,32,3072]{2,1,0:T(8,128)(2,1)S(1)}, f32[24,8,128]{2,1,0:T(8,128)S(1)}) custom-call(bf16[32,3072]{1,0:T(8,128)(2,1)S(1)} %get-tuple-element.65.h_in, f32[32,3072]{1,0:T(8,128)S(1)} %get-tuple-element.66.p_ref.p_in, f32[32,1152]{1,0:T(8,128)S(1)} %collective-permute-done.2.rxe, ...), custom_call_target="tpu_custom_call" | custom-call | flops 377487360 | tf_op jit(solution)/shard_map/pallas_call | solution.py:642
  23.0 0.0 collective-permute-done.4.rye
  23.0 0.9 %collective-permute-done.5.ryo = f32[112,128]{1,0:T(8,128)S(1)} collective-permute-done((f32[112,128]{1,0:T(8,128)S(1)}, f32[112,128]{1,0:T(8,128)S(1)}, u32[]{:S(2)}, u32[]{:S(2)}) %collective-permute-start.5) | collective-permute-done | bytes 57376 | tf_op jit(solution)/shard_map/ppermute | solution.py:44
  23.9 1.1 %shard_map.96 = (bf16[32,3072]{1,0:T(8,128)(2,1)S(1)}, f32[32,3072]{1,0:T(8,128)S(1)}, bf16[3,32,3072]{2,1,0:T(8,128)(2,1)S(1)}, bf16[32,512]{1,0:T(8,128)(2,1)S...) custom-call(bf16[32,3072]{1,0:T(8,128)(2,1)S(1)} %get-tuple-element., ...), custom_call_target="tpu_custom_call", output_to_operand_aliasing={{0}: (17, {}), {1}: (18, {}), {2}: (19, {})} | custom-call | tf_op jit(solution)/shard_map/pallas_call | solution.py:642
  25.0 0.1 collective-permute-start.7
  25.1 1.1 %collective-permute-start.11 = (f32[32,768]{1,0:T(8,128)S(1)}, f32[32,768]{1,0:T(8,128)S(1)}, u32[]{:S(2)}, u32[]{:S(2)}) collective-permute-start(f32[32,768]{1,0:T(8,128)S(1)} %get-tuple-element.99), channel_id=1, source_target_pairs={{0,1},{1,0},{2,3},{3,2},{4,5},{5,4},{6,7},{7,6},{8,9},{9,8},{10,11... | collective-permute-start | bytes 294920 | tf_op jit(solution)/shard_map/ppermute | solution.py:44
  26.3 1.0 %collective-permute-start.8 = (f32[32,384]{1,0:T(8,128)S(1)}, f32[32,384]{1,0:T(8,128)S(1)}, u32[]{:S(2)}, u32[]{:S(2)}) collective-permute-start(f32[32,384]{1,0:T(8,128)S(1)} %get-tuple-element.95), channel_id=1, source_target_pairs={{0,1},{1,0},{2,3},{3,2},{4,5},{5,4},{6,7},{7,6},{8,9},{9,8},{10,11... | collective-permute-start | bytes 147464 | tf_op jit(solution)/shard_map/ppermute | solution.py:44
  27.3 3.1 %collective-permute-done.8.rxa = f32[32,384]{1,0:T(8,128)S(1)} collective-permute-done((f32[32,384]{1,0:T(8,128)S(1)}, f32[32,384]{1,0:T(8,128)S(1)}, u32[]{:S(2)}, u32[]{:S(2)}) %collective-permute-start.8) | collective-permute-done | bytes 49184 | tf_op jit(solution)/shard_map/ppermute | solution.py:44
  30.4 0.0 collective-permute-done.7.rxe
  30.4 0.2 shard_map.97
  30.6 0.0 collective-permute-start.9
  30.7 4.4 %collective-permute-start.10 = (f32[112,128]{1,0:T(8,128)S(1)}, f32[112,128]{1,0:T(8,128)S(1)}, u32[]{:S(2)}, u32[]{:S(2)}) collective-permute-start(f32[112,128]{1,0:T(8,128)S(1)} %get-tuple-element.98), channel_id=1, source_target_pairs={{0,32},{1,33},{2,34},{3,35},{4,36},{5,37},{6,38},{7,39},{8,16},{9,... | collective-permute-start | bytes 172040 | tf_op jit(solution)/shard_map/ppermute | solution.py:44
  35.1 0.0 collective-permute-done.11.rxb
  35.1 1.2 %shard_map.98 = (bf16[32,3072]{1,0:T(8,128)(2,1)S(1)}, f32[32,3072]{1,0:T(8,128)S(1)}, bf16[3,32,3072]{2,1,0:T(8,128)(2,1)S(1)}, f32[24,8,128]{2,1,0:T(8,128)S(1)}) custom-call(bf16[32,3072]{1,0:T(8,128)(2,1)S(1)} %get-tuple-element.89.h_in, f32[32,3072]{1,0:T(8,128)S(1)} %get-tuple-element.90.p_ref.p_in, f32[32,1152]{1,0:T(8,128)S(1)} %collective-permute-done.7.rxe, ...), custom_call_target="tpu_custom_call" | custom-call | flops 377487360 | tf_op jit(solution)/shard_map/pallas_call | solution.py:642
  36.3 0.0 collective-permute-done.9.rye
  36.3 1.4 %collective-permute-done.10.ryo = f32[112,128]{1,0:T(8,128)S(1)} collective-permute-done((f32[112,128]{1,0:T(8,128)S(1)}, f32[112,128]{1,0:T(8,128)S(1)}, u32[]{:S(2)}, u32[]{:S(2)}) %collective-permute-start.10) | collective-permute-done | bytes 57376 | tf_op jit(solution)/shard_map/ppermute | solution.py:44
  37.7 1.1 %shard_map.99 = (bf16[32,3072]{1,0:T(8,128)(2,1)S(1)}, f32[32,3072]{1,0:T(8,128)S(1)}, bf16[32,512]{1,0:T(8,128)(2,1)S(1)}, f32[32,512]{1,0:T(8,128)S(1)}, f32[3...) custom-call(bf16[32,3072]{1,0:T(8,128)(2,1)S(1)} %get-tuple-element., ...), custom_call_target="tpu_custom_call", output_to_operand_aliasing={{0}: (17, {}), {1}: (18, {})} | custom-call | tf_op jit(solution)/shard_map/pallas_call | solution.py:642
  38.8 0.1 collective-permute-start.12
  38.9 0.7 %collective-permute-start.16 = (f32[32,768]{1,0:T(8,128)S(1)}, f32[32,768]{1,0:T(8,128)S(1)}, u32[]{:S(2)}, u32[]{:S(2)}) collective-permute-start(f32[32,768]{1,0:T(8,128)S(1)} %get-tuple-element.114), channel_id=1, source_target_pairs={{0,1},{1,0},{2,3},{3,2},{4,5},{5,4},{6,7},{7,6},{8,9},{9,8},{10,11... | collective-permute-start | bytes 294920 | tf_op jit(solution)/shard_map/ppermute | solution.py:44
  39.6 1.4 %collective-permute-start.13 = (f32[32,384]{1,0:T(8,128)S(1)}, f32[32,384]{1,0:T(8,128)S(1)}, u32[]{:S(2)}, u32[]{:S(2)}) collective-permute-start(f32[32,384]{1,0:T(8,128)S(1)} %get-tuple-element.110), channel_id=1, source_target_pairs={{0,1},{1,0},{2,3},{3,2},{4,5},{5,4},{6,7},{7,6},{8,9},{9,8},{10,11... | collective-permute-start | bytes 147464 | tf_op jit(solution)/shard_map/ppermute | solution.py:44
  41.0 3.1 %collective-permute-done.13.rxa = f32[32,384]{1,0:T(8,128)S(1)} collective-permute-done((f32[32,384]{1,0:T(8,128)S(1)}, f32[32,384]{1,0:T(8,128)S(1)}, u32[]{:S(2)}, u32[]{:S(2)}) %collective-permute-start.13) | collective-permute-done | bytes 49184 | tf_op jit(solution)/shard_map/ppermute | solution.py:44
  44.1 0.0 collective-permute-done.12.rxe
  44.1 0.2 shard_map.100
  44.3 0.0 collective-permute-start.14
  44.4 3.8 %collective-permute-start.15 = (f32[112,128]{1,0:T(8,128)S(1)}, f32[112,128]{1,0:T(8,128)S(1)}, u32[]{:S(2)}, u32[]{:S(2)}) collective-permute-start(f32[112,128]{1,0:T(8,128)S(1)} %get-tuple-element.113), channel_id=1, source_target_pairs={{0,32},{1,33},{2,34},{3,35},{4,36},{5,37},{6,38},{7,39},{8,16},{9,... | collective-permute-start | bytes 172040 | tf_op jit(solution)/shard_map/ppermute | solution.py:44
  48.2 0.0 collective-permute-done.16.rxb
  48.2 0.4 shard_map.101.res
  48.6 0.9 %collective-permute-done.14.rye = f32[112,128]{1,0:T(8,128)S(1)} collective-permute-done((f32[112,128]{1,0:T(8,128)S(1)}, f32[112,128]{1,0:T(8,128)S(1)}, u32[]{:S(2)}, u32[]{:S(2)}) %collective-permute-start.14) | collective-permute-done | bytes 57376 | tf_op jit(solution)/shard_map/ppermute | solution.py:40
  49.5 1.4 %collective-permute-done.15.ryo = f32[112,128]{1,0:T(8,128)S(1)} collective-permute-done((f32[112,128]{1,0:T(8,128)S(1)}, f32[112,128]{1,0:T(8,128)S(1)}, u32[]{:S(2)}, u32[]{:S(2)}) %collective-permute-start.15) | collective-permute-done | bytes 57376 | tf_op jit(solution)/shard_map/ppermute | solution.py:44
  50.9 1.4 %shard_map.102 = bf16[32,3,8,128]{3,2,1,0:T(8,128)(2,1)} custom-call(bf16[32,3072]{1,0:T(8,128)(2,1)S(1)} %get-tuple-element.105.h_in, f32[32,3072]{1,0:T(8,128)S(1)} %get-tuple-element.106.p_ref.p_in, bf16[32,512]{1,0:T(8,128)(2,1)S(1)} %get-tuple-element.107.hr_in, f32[32,512]{1,0:T(8,128)S(1)} %get-tuple-element.111.pr_in, ...), custom_call_target="tpu_custom_call" | custom-call | tf_op jit(solution)/shard_map/pallas_call | solution.py:642
Async XLA Ops:
  2.3 4.2 %collective-permute-start = (f32[104,128]{1,0:T(8,128)S(1)}, f32[104,128]{1,0:T(8,128)S(1)}, u32[]{:S(2)}, u32[]{:S(2)}) collective-permute-start(f32[104,128]{1,0:T(8,128)S(1)} %get-tuple-element.69), channel_id=1, source_target_pairs={{0,1},{1,0},{2,3},{3,2},{4,5},{5,4},{6,7},{7,6},{8,9},{9,8},{10,11... | collective-permute-start | bytes 159752 | tf_op jit(solution)/shard_map/ppermute | solution.py:40
  3.5 4.1 %collective-permute-start.1 = (f32[104,128]{1,0:T(8,128)S(1)}, f32[104,128]{1,0:T(8,128)S(1)}, u32[]{:S(2)}, u32[]{:S(2)}) collective-permute-start(f32[104,128]{1,0:T(8,128)S(1)} %get-tuple-element.70), channel_id=1, source_target_pairs={{0,32},{1,2},{2,1},{3,4},{4,3},{5,6},{6,5},{7,39},{8,40},{9,10},{1... | collective-permute-start | bytes 159752 | tf_op jit(solution)/shard_map/ppermute | solution.py:44
  8.3 7.2 %collective-permute-start.2 = (f32[32,1152]{1,0:T(8,128)S(1)}, f32[32,1152]{1,0:T(8,128)S(1)}, u32[]{:S(2)}, u32[]{:S(2)}) collective-permute-start(f32[32,1152]{1,0:T(8,128)S(1)} %get-tuple-element.75), channel_id=1, source_target_pairs={{0,32},{32,0},{64,96},{96,64},{128,160},{160,128},{192,224},{224,1... | collective-permute-start | bytes 442376 | tf_op jit(solution)/shard_map/ppermute | solution.py:40
  8.4 13.4 %collective-permute-start.6 = (f32[32,768]{1,0:T(8,128)S(1)}, f32[32,768]{1,0:T(8,128)S(1)}, u32[]{:S(2)}, u32[]{:S(2)}) collective-permute-start(f32[32,768]{1,0:T(8,128)S(1)} %get-tuple-element.83), channel_id=1, source_target_pairs={{0,1},{1,0},{2,3},{3,2},{4,5},{5,4},{6,7},{7,6},{8,9},{9,8},{10,11... | collective-permute-start | bytes 294920 | tf_op jit(solution)/shard_map/ppermute | solution.py:44
  11.4 4.1 %collective-permute-start.3 = (f32[32,384]{1,0:T(8,128)S(1)}, f32[32,384]{1,0:T(8,128)S(1)}, u32[]{:S(2)}, u32[]{:S(2)}) collective-permute-start(f32[32,384]{1,0:T(8,128)S(1)} %get-tuple-element.76), channel_id=1, source_target_pairs={{0,1},{1,0},{2,3},{3,2},{4,5},{5,4},{6,7},{7,6},{8,9},{9,8},{10,11... | collective-permute-start | bytes 147464 | tf_op jit(solution)/shard_map/ppermute | solution.py:44
  15.8 7.2 %collective-permute-start.4 = (f32[112,128]{1,0:T(8,128)S(1)}, f32[112,128]{1,0:T(8,128)S(1)}, u32[]{:S(2)}, u32[]{:S(2)}) collective-permute-start(f32[112,128]{1,0:T(8,128)S(1)} %get-tuple-element.78), channel_id=1, source_target_pairs={{0,8},{8,0},{16,24},{24,16},{1,9},{9,1},{17,25},{25,17},{2,10},{10... | collective-permute-start | bytes 172040 | tf_op jit(solution)/shard_map/ppermute | solution.py:40
  15.8 8.1 %collective-permute-start.5 = (f32[112,128]{1,0:T(8,128)S(1)}, f32[112,128]{1,0:T(8,128)S(1)}, u32[]{:S(2)}, u32[]{:S(2)}) collective-permute-start(f32[112,128]{1,0:T(8,128)S(1)} %get-tuple-element.79), channel_id=1, source_target_pairs={{0,32},{1,33},{2,34},{3,35},{4,36},{5,37},{6,38},{7,39},{8,16},{9,... | collective-permute-start | bytes 172040 | tf_op jit(solution)/shard_map/ppermute | solution.py:44
  25.0 5.3 %collective-permute-start.7 = (f32[32,1152]{1,0:T(8,128)S(1)}, f32[32,1152]{1,0:T(8,128)S(1)}, u32[]{:S(2)}, u32[]{:S(2)}) collective-permute-start(f32[32,1152]{1,0:T(8,128)S(1)} %get-tuple-element.94), channel_id=1, source_target_pairs={{0,32},{32,0},{64,96},{96,64},{128,160},{160,128},{192,224},{224,1... | collective-permute-start | bytes 442376 | tf_op jit(solution)/shard_map/ppermute | solution.py:40
  25.1 9.9 %collective-permute-start.11 = (f32[32,768]{1,0:T(8,128)S(1)}, f32[32,768]{1,0:T(8,128)S(1)}, u32[]{:S(2)}, u32[]{:S(2)}) collective-permute-start(f32[32,768]{1,0:T(8,128)S(1)} %get-tuple-element.99), channel_id=1, source_target_pairs={{0,1},{1,0},{2,3},{3,2},{4,5},{5,4},{6,7},{7,6},{8,9},{9,8},{10,11... | collective-permute-start | bytes 294920 | tf_op jit(solution)/shard_map/ppermute | solution.py:44
  26.3 4.1 %collective-permute-start.8 = (f32[32,384]{1,0:T(8,128)S(1)}, f32[32,384]{1,0:T(8,128)S(1)}, u32[]{:S(2)}, u32[]{:S(2)}) collective-permute-start(f32[32,384]{1,0:T(8,128)S(1)} %get-tuple-element.95), channel_id=1, source_target_pairs={{0,1},{1,0},{2,3},{3,2},{4,5},{5,4},{6,7},{7,6},{8,9},{9,8},{10,11... | collective-permute-start | bytes 147464 | tf_op jit(solution)/shard_map/ppermute | solution.py:44
  30.6 5.7 %collective-permute-start.9 = (f32[112,128]{1,0:T(8,128)S(1)}, f32[112,128]{1,0:T(8,128)S(1)}, u32[]{:S(2)}, u32[]{:S(2)}) collective-permute-start(f32[112,128]{1,0:T(8,128)S(1)} %get-tuple-element.97), channel_id=1, source_target_pairs={{0,8},{8,0},{16,24},{24,16},{1,9},{9,1},{17,25},{25,17},{2,10},{10... | collective-permute-start | bytes 172040 | tf_op jit(solution)/shard_map/ppermute | solution.py:40
  30.7 7.0 %collective-permute-start.10 = (f32[112,128]{1,0:T(8,128)S(1)}, f32[112,128]{1,0:T(8,128)S(1)}, u32[]{:S(2)}, u32[]{:S(2)}) collective-permute-start(f32[112,128]{1,0:T(8,128)S(1)} %get-tuple-element.98), channel_id=1, source_target_pairs={{0,32},{1,33},{2,34},{3,35},{4,36},{5,37},{6,38},{7,39},{8,16},{9,... | collective-permute-start | bytes 172040 | tf_op jit(solution)/shard_map/ppermute | solution.py:44
  38.8 5.3 %collective-permute-start.12 = (f32[32,1152]{1,0:T(8,128)S(1)}, f32[32,1152]{1,0:T(8,128)S(1)}, u32[]{:S(2)}, u32[]{:S(2)}) collective-permute-start(f32[32,1152]{1,0:T(8,128)S(1)} %get-tuple-element.109), channel_id=1, source_target_pairs={{0,32},{32,0},{64,96},{96,64},{128,160},{160,128},{192,224},{224,1... | collective-permute-start | bytes 442376 | tf_op jit(solution)/shard_map/ppermute | solution.py:40
  38.9 9.3 %collective-permute-start.16 = (f32[32,768]{1,0:T(8,128)S(1)}, f32[32,768]{1,0:T(8,128)S(1)}, u32[]{:S(2)}, u32[]{:S(2)}) collective-permute-start(f32[32,768]{1,0:T(8,128)S(1)} %get-tuple-element.114), channel_id=1, source_target_pairs={{0,1},{1,0},{2,3},{3,2},{4,5},{5,4},{6,7},{7,6},{8,9},{9,8},{10,11... | collective-permute-start | bytes 294920 | tf_op jit(solution)/shard_map/ppermute | solution.py:44
  39.6 4.5 %collective-permute-start.13 = (f32[32,384]{1,0:T(8,128)S(1)}, f32[32,384]{1,0:T(8,128)S(1)}, u32[]{:S(2)}, u32[]{:S(2)}) collective-permute-start(f32[32,384]{1,0:T(8,128)S(1)} %get-tuple-element.110), channel_id=1, source_target_pairs={{0,1},{1,0},{2,3},{3,2},{4,5},{5,4},{6,7},{7,6},{8,9},{9,8},{10,11... | collective-permute-start | bytes 147464 | tf_op jit(solution)/shard_map/ppermute | solution.py:44
  44.3 5.1 %collective-permute-start.14 = (f32[112,128]{1,0:T(8,128)S(1)}, f32[112,128]{1,0:T(8,128)S(1)}, u32[]{:S(2)}, u32[]{:S(2)}) collective-permute-start(f32[112,128]{1,0:T(8,128)S(1)} %get-tuple-element.112), channel_id=1, source_target_pairs={{0,8},{8,0},{16,24},{24,16},{1,9},{9,1},{17,25},{25,17},{2,10},{10... | collective-permute-start | bytes 172040 | tf_op jit(solution)/shard_map/ppermute | solution.py:40
  44.4 6.5 %collective-permute-start.15 = (f32[112,128]{1,0:T(8,128)S(1)}, f32[112,128]{1,0:T(8,128)S(1)}, u32[]{:S(2)}, u32[]{:S(2)}) collective-permute-start(f32[112,128]{1,0:T(8,128)S(1)} %get-tuple-element.113), channel_id=1, source_target_pairs={{0,32},{1,33},{2,34},{3,35},{4,36},{5,37},{6,38},{7,39},{8,16},{9,... | collective-permute-start | bytes 172040 | tf_op jit(solution)/shard_map/ppermute | solution.py:44
